TPU v7x, 8 devices: a whole 2x2x1 slice. The times are simulated.
8 devices in a mesh: tp: 2 (over z, y), cp: 4 (over x, core).
Axes of the slice: x: 2, y: 2, z: 1, core: 2. Of those that a mesh axis runs over, the one named last changes fastest.
Arguments:
- x: bfloat16 [8, 2048, 4096], P(None, 'cp')
- grad_out: bfloat16 [8, 2048, 4096], P(None, 'cp')
- norm_gain: bfloat16 [4096], replicated
- w_qkv: bfloat16 [4096, 4608], P(None, 'tp')
- b_qkv: bfloat16 [4608], P('tp')
- w_out: bfloat16 [4096, 4096], P('tp')
- doc_id: int32 [8, 2048], P(None, 'cp')
- pos_in_doc: int32 [8, 2048], P(None, 'cp')
Outputs:
- output 1: bfloat16 [8, 2048, 4096], P(None, 'cp')
- output 2: bfloat16 [8, 2048, 4096], P(None, 'cp')
- output 3: float32 [4096], replicated
- output 4: float32 [4096, 4608], P(None, 'tp')
- output 5: float32 [4608], P('tp')
- output 6: float32 [4096, 4096], P('tp')
All inputs are finite; a program needn't handle non-finite values.
Results may differ from a plain program's by a relative error of at most 0.00824973.
Values are sent between devices in bfloat16 or wider.
A program may use at most 1 GiB of HBM per device.

v0:
```python
import jax
import jax.numpy as jnp
from jax import lax
from jax.sharding import PartitionSpec as P

HEAD_DIM = 128
EPS = 1.5625e-07
ROPE_BASE = 5000000.0
NEG_BIG = -1e30


def rope_tables(pos_blk):
    rot_dims = HEAD_DIM // 2
    inv_freq = 1.0 / ROPE_BASE ** (jnp.arange(0, rot_dims, 2, dtype=jnp.float32) / rot_dims)
    angles = pos_blk.astype(jnp.float32)[..., None] * inv_freq
    return jnp.cos(angles), jnp.sin(angles)


def rotate_pairs(vals, cos_t, sin_t):
    half_rot = cos_t.shape[-1]
    turned_part = vals[..., : 2 * half_rot]
    pairs = turned_part.reshape(turned_part.shape[:-1] + (half_rot, 2))
    even = pairs[..., 0]
    odd = pairs[..., 1]
    turned = jnp.stack([even * cos_t - odd * sin_t, odd * cos_t + even * sin_t], axis=-1)
    return jnp.concatenate([turned.reshape(turned_part.shape), vals[..., 2 * half_rot:]], axis=-1)


def norm_forward(x_blk, norm_gain):
    x_wide = x_blk.astype(jnp.float32)
    inv_rms = lax.rsqrt(jnp.mean(x_wide * x_wide, axis=-1, keepdims=True) + EPS)
    normed = x_wide * inv_rms
    return x_wide, inv_rms, normed, (normed * norm_gain.astype(jnp.float32)).astype(jnp.bfloat16)


def norm_backward(d_hidden, grad_blk, norm_gain, normed, inv_rms):
    grad_gain = jnp.sum(d_hidden * normed, axis=(0, 1))
    d_normed = d_hidden * norm_gain.astype(jnp.float32)
    grad_x = (grad_blk.astype(jnp.float32) + inv_rms * (d_normed - normed * jnp.mean(d_normed * normed, axis=-1, keepdims=True))).astype(jnp.bfloat16)
    return grad_gain, grad_x


def project(h_in, w_qkv, b_qkv, pos_blk, groups, per_group):
    batch, rows = h_in.shape[:2]
    qkv_proj = (jnp.dot(h_in, w_qkv, preferred_element_type=jnp.float32) + b_qkv.astype(jnp.float32)).astype(jnp.bfloat16)
    qkv_proj = qkv_proj.reshape(batch, rows, groups, per_group + 2, HEAD_DIM)
    cos_t, sin_t = rope_tables(pos_blk)
    q_rot = rotate_pairs(qkv_proj[:, :, :, :per_group].astype(jnp.float32), cos_t[:, :, None, None], sin_t[:, :, None, None]).astype(jnp.bfloat16)
    k_rot = rotate_pairs(qkv_proj[:, :, :, per_group].astype(jnp.float32), cos_t[:, :, None], sin_t[:, :, None]).astype(jnp.bfloat16)
    kv_own = jnp.stack([k_rot, qkv_proj[:, :, :, per_group + 1]], axis=3)
    return q_rot, kv_own, cos_t, sin_t


def assemble_grad(dq_acc, dkv_own, cos_t, sin_t):
    dq_pre = rotate_pairs(dq_acc, cos_t[:, :, None, None], -sin_t[:, :, None, None])
    dk_pre = rotate_pairs(dkv_own[:, :, :, 0], cos_t[:, :, None], -sin_t[:, :, None])
    d_proj = jnp.concatenate([dq_pre, dk_pre[:, :, :, None], dkv_own[:, :, :, 1:]], axis=3).astype(jnp.bfloat16)
    return d_proj.reshape(d_proj.shape[0], d_proj.shape[1], -1)


def make_keep(q_doc, k_doc, q_start, k_start):
    q_pos = q_start + jnp.arange(q_doc.shape[1])
    k_pos = k_start + jnp.arange(k_doc.shape[1])
    keep = (q_doc[:, :, None] == k_doc[:, None, :]) & (k_pos[None, None, :] <= q_pos[None, :, None])
    return keep[:, :, None, None, :]


def fwd_update(state, q_rot, kv_blk, keep, scale):
    o_acc, m_acc, l_acc = state
    scores = jnp.einsum('btghe,bsge->btghs', q_rot, kv_blk[:, :, :, 0], preferred_element_type=jnp.float32) * scale
    scores = jnp.where(keep, scores, NEG_BIG)
    m_new = jnp.maximum(m_acc, jnp.max(scores, axis=-1))
    alpha = jnp.exp(m_acc - m_new)
    probs = jnp.where(keep, jnp.exp(scores - m_new[..., None]), 0.0)
    l_new = alpha * l_acc + jnp.sum(probs, axis=-1)
    o_new = alpha[..., None] * o_acc + jnp.einsum('btghs,bsge->btghe', probs.astype(jnp.bfloat16), kv_blk[:, :, :, 1], preferred_element_type=jnp.float32)
    return o_new, m_new, l_new


def attn_backward(q_rot, d_heads, lse, delta, kv_blk, keep, scale):
    k_rot = kv_blk[:, :, :, 0]
    values = kv_blk[:, :, :, 1]
    scores = jnp.einsum('btghe,bsge->btghs', q_rot, k_rot, preferred_element_type=jnp.float32) * scale
    probs = jnp.where(keep, jnp.exp(scores - lse[..., None]), 0.0)
    d_probs = jnp.einsum('btghe,bsge->btghs', d_heads, values, preferred_element_type=jnp.float32)
    d_scores = (probs * (d_probs - delta[..., None])).astype(jnp.bfloat16)
    dq_part = scale * jnp.einsum('btghs,bsge->btghe', d_scores, k_rot, preferred_element_type=jnp.float32)
    dk_part = scale * jnp.einsum('btghs,btghe->bsge', d_scores, q_rot, preferred_element_type=jnp.float32)
    dv_part = jnp.einsum('btghs,btghe->bsge', probs.astype(jnp.bfloat16), d_heads, preferred_element_type=jnp.float32)
    return dq_part, jnp.stack([dk_part, dv_part], axis=3)


def solution(mesh):
    cp_size = mesh.shape['cp']
    shift = [(i, (i + 1) % cp_size) for i in range(cp_size)]

    def body(x_blk, grad_blk, norm_gain, w_qkv, b_qkv, w_out, doc_blk, pos_blk):
        batch, rows = x_blk.shape[:2]
        groups = (w_qkv.shape[1] - w_out.shape[0]) // (2 * HEAD_DIM)
        per_group = w_out.shape[0] // (groups * HEAD_DIM)
        scale = HEAD_DIM ** -0.5
        cp_index = lax.axis_index('cp')
        q_start = cp_index * rows
        x_wide, inv_rms, normed, h_in = norm_forward(x_blk, norm_gain)
        q_rot, kv_own, cos_t, sin_t = project(h_in, w_qkv, b_qkv, pos_blk, groups, per_group)

        def attend(step, state, kv_blk, key_doc):
            origin = (cp_index - step) % cp_size
            keep = make_keep(doc_blk, key_doc, q_start, origin * rows)
            return lax.cond(step <= cp_index, lambda held: fwd_update(held, q_rot, kv_blk, keep, scale), lambda held: held, state)

        def fwd_loop(step, carry):
            state, kv_blk, key_doc = carry
            state = attend(step, state, kv_blk, key_doc)
            kv_blk = lax.ppermute(kv_blk, 'cp', shift)
            key_doc = lax.ppermute(key_doc, 'cp', shift)
            return state, kv_blk, key_doc

        start_state = (jnp.zeros(q_rot.shape, jnp.float32), jnp.full(q_rot.shape[:-1], NEG_BIG, jnp.float32), jnp.zeros(q_rot.shape[:-1], jnp.float32))
        state, kv_last, doc_last = lax.fori_loop(0, cp_size - 1, fwd_loop, (start_state, kv_own, doc_blk))
        o_acc, m_acc, l_acc = attend(cp_size - 1, state, kv_last, doc_last)
        lse = m_acc + jnp.log(l_acc)
        context = (o_acc / l_acc[..., None]).astype(jnp.bfloat16)
        context_flat = context.reshape(batch, rows, -1)
        attn = lax.psum(jnp.dot(context_flat, w_out, preferred_element_type=jnp.float32), 'tp')
        out = (x_wide + attn).astype(jnp.bfloat16)

        grad_w_out = lax.psum(jnp.einsum('btk,btd->kd', context_flat, grad_blk, preferred_element_type=jnp.float32), 'cp')
        d_heads = jnp.einsum('btd,kd->btk', grad_blk, w_out, preferred_element_type=jnp.float32).astype(jnp.bfloat16).reshape(context.shape)
        delta = jnp.sum(d_heads.astype(jnp.float32) * context.astype(jnp.float32), axis=-1)

        def grad_step(step, dq_acc, dkv_acc, kv_blk, key_doc):
            origin = (cp_index - step) % cp_size
            keep = make_keep(doc_blk, key_doc, q_start, origin * rows)

            def run(accums):
                dq_part, dkv_part = attn_backward(q_rot, d_heads, lse, delta, kv_blk, keep, scale)
                return accums[0] + dq_part, accums[1] + dkv_part

            return lax.cond(step <= cp_index, run, lambda accums: accums, (dq_acc, dkv_acc))

        def bwd_loop(step, carry):
            dq_acc, dkv_acc, kv_blk, key_doc = carry
            dq_acc, dkv_acc = grad_step(step, dq_acc, dkv_acc, kv_blk, key_doc)
            dkv_acc = lax.ppermute(dkv_acc, 'cp', shift)
            kv_blk = lax.ppermute(kv_blk, 'cp', shift)
            key_doc = lax.ppermute(key_doc, 'cp', shift)
            return dq_acc, dkv_acc, kv_blk, key_doc

        start_grads = (jnp.zeros(q_rot.shape, jnp.float32), jnp.zeros(kv_own.shape, jnp.float32), kv_own, doc_blk)
        dq_acc, dkv_acc, kv_last, doc_last = lax.fori_loop(0, cp_size - 1, bwd_loop, start_grads)
        dq_acc, dkv_acc = grad_step(cp_size - 1, dq_acc, dkv_acc, kv_last, doc_last)
        dkv_own = lax.ppermute(dkv_acc, 'cp', shift)

        d_proj = assemble_grad(dq_acc, dkv_own, cos_t, sin_t)
        grad_b_qkv = lax.psum(jnp.sum(d_proj.astype(jnp.float32), axis=(0, 1)), 'cp')
        grad_w_qkv = lax.psum(jnp.einsum('btd,btk->dk', h_in, d_proj, preferred_element_type=jnp.float32), 'cp')
        d_hidden = lax.psum(jnp.einsum('btk,dk->btd', d_proj, w_qkv, preferred_element_type=jnp.float32), 'tp')
        grad_gain, grad_x = norm_backward(d_hidden, grad_blk, norm_gain, normed, inv_rms)
        grad_gain = lax.psum(grad_gain, 'cp')
        return out, grad_x, grad_gain, grad_w_qkv, grad_b_qkv, grad_w_out

    specs_in = (P(None, 'cp', None), P(None, 'cp', None), P(), P(None, 'tp'), P('tp'), P('tp', None), P(None, 'cp'), P(None, 'cp'))
    specs_out = (P(None, 'cp', None), P(None, 'cp', None), P(), P(None, 'tp'), P('tp'), P('tp', None))
    return jax.shard_map(body, mesh=mesh, in_specs=specs_in, out_specs=specs_out, check_vma=False)
```

profile of v0, /device:TPU:0, one launch (start us, length us, event | category | flops | bytes accessed | tf_op | source)
XLA Modules:
  0.0 6865.1 jit_solution(1341027202787591053)
XLA Ops:
  19.8 88.8 %add_convert_fusion = bf16[8,512,2304]{2,1,0:T(8,128)(2,1)} fusion(bf16[8,512,4096]{2,1,0:T(8,128)(2,1)} %param.20, f32[4096]{0:T(1024)S(1)} %convert_element_type.163, f32[8,512]{1,0:T(8,128)S(1)} %add_rsqrt_fusion, bf16[4096,2304]{1,0:T(8,128)(2,1)} %param.23, f32[2304]{0:T(1024)S(1)} %convert_element_type.165), kind=kOutput, calls=%fused_computation.141 | convolution fusion | flops 77395394560 | bytes 71345152 | tf_op jit(solution)/shard_map/dot_general | solution.py:45
  152.1 78.1 %fusion.135 = bf16[8,512,2048]{2,1,0:T(8,128)(2,1)} fusion(bf16[8,512,4096]{2,1,0:T(8,128)(2,1)} %param.21, bf16[2048,4096]{1,0:T(8,128)(2,1)} %param.25), kind=kOutput, calls=%fused_computation.155 | convolution fusion | flops 68727865344 | bytes 67108864 | tf_op jit(solution)/shard_map/btd,kd->btk/dot_general | solution.py:129
  427.2 374.1 %while.44 = (s32[]{:T(128)}, f32[8,512,1,16,128]{4,1,3,0,2:T(8,128)}, f32[8,512,1,16]{1,3,0,2:T(8,128)S(1)}, f32[8,512,1,16]{1,3,0,2:T(8,128)S(1)}, bf16[8,512,1...) while((s32[]{:T(128)}, ...), condition=%wide.region_6.7_spmd, body=%wide.region_1.6_spmd.sunk | while | flops 17637507072 | bytes 514474464 | solution.py:120
  435.5 166.2 %conditional.8 = ((f32[8,512,1,16,128]{4,1,3,0,2:T(8,128)}, f32[8,512,1,16]{1,3,0,2:T(8,128)S(1)}, f32[8,512,1,16]{1,3,0,2:T(8,128)S(1)})) conditional(s32[]{:T(128)} %convert_element_type.271, (f32[8,512,1,16,128]{4,1,3,0,2:T(8,128)}, f32[8,512,1,16]{1,3,0,2:T(8,128)S(1)}, f32[8,512,1,16]{1,3,0,2:T(8,128)S(1)}) %tuple.212, (s32[8,512]{1,0:T(8,128)}, ...), branch_computations={%region_2.2_spmd, %region_3.5_spmd} | conditional | flops 17637507072 | bytes 501788832 | solution.py:110
  438.4 50.0 fusion
  530.0 71.8 %bitcast_add_fusion = f32[8,512,1,16,128]{4,1,3,0,2:T(8,128)} fusion(f32[8,512,1,16,128]{4,1,3,0,2:T(8,128)} %get-tuple-element.947, f32[8,512,16]{1,2,0:T(8,128)S(1)} %get-tuple-element.1232, f32[8,512,512,16]{2,1,3,0:T(8,128)} %get-tuple-element.1241, f32[8,512,16]{1,2,0:T(8,128)S(1)} %bitcast.506, pred[8,512,512]{1,2,0:T(8,128)(4,1)S(1)} %compare_and_fusion, ...), kind=kOutput, calls=%fused_computation.8 | convolution fusion | flops 8774483968 | bytes 204996608 | tf_op jit(solution)/shard_map/while/body/eval_jaxpr/cond/branch_1_fun/btghs,bsge->btghe/dot_general | solution.py:76
  633.7 142.0 %collective-permute-start = (bf16[8,512,1,2,128]{4,1,0,3,2:T(8,128)(2,1)}, bf16[8,512,1,2,128]{4,1,0,3,2:T(8,128)(2,1)}, u32[]{:S(2)}, u32[]{:S(2)}) collective-permute-start(bf16[8,512,1,2,128]{4,1,0,3,2:T(8,128)(2,1)} %copy.131), channel_id=1, source_target_pairs={{0,1},{1,2},{2,3},{3,0},{4,5},{5,6},{6,7},{7,4}} | collective-permute-start | bytes 6291464 | tf_op jit(solution)/shard_map/while/body/eval_jaxpr/ppermute | solution.py:115
  804.1 45.3 conditional.4
  885.9 1336.8 %while.45 = (s32[]{:T(128)}, f32[8,512,1,16,128]{4,1,3,0,2:T(8,128)}, f32[8,512,1,2,128]{4,1,0,3,2:T(8,128)}, bf16[8,512,1,2,128]{4,1,0,3,2:T(8,128)(2,1)}, s32[...) while((s32[]{:T(128)}, ...), condition=%wide.region_16.17_spmd, body=%wide.region_13.16_spmd.sunk | while | flops 43309072384 | bytes 812007936 | solution.py:151
  887.5 272.3 %conditional.9 = ((f32[8,512,1,16,128]{4,1,3,0,2:T(8,128)}, f32[8,512,1,2,128]{4,1,0,3,2:T(8,128)})) conditional(s32[]{:T(128)} %convert_element_type.272, (f32[8,512,1,16,128]{4,1,3,0,2:T(8,128)}, f32[8,512,1,2,128]{4,1,0,3,2:T(8,128)}) %tuple.215, (s32[8,512]{1,0:T(8,128)}, s32[8,512]{1,0:T(8,128)S(1)}, s32[]{:T(128)}, s32[]{:T(128)}, ...), branch_computations={%region_14.14_spmd, %region_15.15_spmd} | conditional | flops 43309072384 | bytes 774156480 | solution.py:140
  890.3 51.7 fusion.33
  942.0 81.2 %fusion.19 = bf16[8,512,1,16,512]{1,4,3,0,2:T(8,128)(2,1)} fusion(f32[8,512,512,16]{2,1,3,0:T(8,128)} %fusion.33, f32[8,512,16]{1,2,0:T(8,128)S(1)} %bitcast.524, f32[8,512,16]{1,2,0:T(8,128)S(1)} %bitcast.526, pred[8,512,512]{1,2,0:T(8,128)(4,1)S(1)} %compare_and_fusion.1, bf16[8,512,1,16,128]{4,1,3,0,2:T(8,128)(2,1)} %get-tuple-element.982, ...), kind=kOutput, calls=%fused_computation.27 | convolution fusion | flops 8791261184 | bytes 221773824 | tf_op jit(solution)/shard_map/while/body/eval_jaxpr/cond/branch_1_fun/btghe,bsge->btghs/dot_general | solution.py:85
  1054.9 52.0 fusion.38
  1112.9 47.0 bitcast_add_fusion.2
  1159.8 144.2 %collective-permute-start.3 = (bf16[8,512,1,2,128]{4,1,0,3,2:T(8,128)(2,1)S(1)}, bf16[8,512,1,2,128]{4,1,0,3,2:T(8,128)(2,1)}, u32[]{:S(2)}, u32[]{:S(2)}) collective-permute-start(bf16[8,512,1,2,128]{4,1,0,3,2:T(8,128)(2,1)S(1)} %copy.153), channel_id=1, source_target_pairs={{0,1},{1,2},{2,3},{3,0},{4,5},{5,6},{6,7},{7,4}} | collective-permute-start | bytes 6291464 | tf_op jit(solution)/shard_map/while/body/eval_jaxpr/ppermute | solution.py:146
  1304.1 154.7 %collective-permute-start.4 = (s32[8,512]{1,0:T(8,128)S(1)}, s32[8,512]{1,0:T(8,128)S(1)}, u32[]{:S(2)}, u32[]{:S(2)}) collective-permute-start(s32[8,512]{1,0:T(8,128)S(1)} %copy.154), channel_id=1, source_target_pairs={{0,1},{1,2},{2,3},{3,0},{4,5},{5,6},{6,7},{7,4}} | collective-permute-start | bytes 49160 | tf_op jit(solution)/shard_map/while/body/eval_jaxpr/ppermute | solution.py:147
  1458.8 45.7 collective-permute-done.2
  1528.7 227.1 %collective-permute-start.2 = (f32[8,512,1,2,128]{4,1,0,3,2:T(8,128)}, f32[8,512,1,2,128]{4,1,0,3,2:T(8,128)}, u32[]{:S(2)}, u32[]{:S(2)}) collective-permute-start(f32[8,512,1,2,128]{4,1,0,3,2:T(8,128)} %get-tuple-element.1409), channel_id=1, source_target_pairs={{0,1},{1,2},{2,3},{3,0},{4,5},{5,6},{6,7},{7,4}} | collective-permute-start | bytes 12582920 | tf_op jit(solution)/shard_map/while/body/eval_jaxpr/ppermute | solution.py:145
  1758.3 42.4 collective-permute-start.4
  1800.7 45.7 collective-permute-done.2
  1870.7 232.0 %collective-permute-start.3 = (bf16[8,512,1,2,128]{4,1,0,3,2:T(8,128)(2,1)S(1)}, bf16[8,512,1,2,128]{4,1,0,3,2:T(8,128)(2,1)}, u32[]{:S(2)}, u32[]{:S(2)}) collective-permute-start(bf16[8,512,1,2,128]{4,1,0,3,2:T(8,128)(2,1)S(1)} %copy.153), channel_id=1, source_target_pairs={{0,1},{1,2},{2,3},{3,0},{4,5},{5,6},{6,7},{7,4}} | collective-permute-start | bytes 6291464 | tf_op jit(solution)/shard_map/while/body/eval_jaxpr/ppermute | solution.py:146
  2142.7 45.7 collective-permute-done.2
  2223.4 64.1 conditional.5
  2358.8 244.8 %collective-permute-done.5 = f32[8,512,1,2,128]{1,4,3,0,2:T(8,128)} collective-permute-done((f32[8,512,1,2,128]{1,4,3,0,2:T(8,128)}, f32[8,512,1,2,128]{1,4,3,0,2:T(8,128)}, u32[]{:S(2)}, u32[]{:S(2)}) %collective-permute-start.5) | collective-permute-done | bytes 4194336 | tf_op jit(solution)/shard_map/ppermute | solution.py:153
  2628.8 89.3 %fusion.128 = f32[8,512,4096]{2,1,0:T(8,128)} fusion(bf16[8,512,2304]{1,2,0:T(8,128)(2,1)} %bitcast.514, bf16[4096,2304]{1,0:T(8,128)(2,1)} %param.23), kind=kOutput, calls=%fused_computation.145 | convolution fusion | flops 77309411328 | bytes 104857600 | tf_op jit(solution)/shard_map/btk,dk->btd/dot_general | solution.py:158
  2718.2 79.8 %fusion.133 = f32[8,512,4096]{2,1,0:T(8,128)} fusion(bf16[8,512,2048]{1,2,0:T(8,128)(2,1)} %bitcast.517, bf16[2048,4096]{1,0:T(8,128)(2,1)} %param.25), kind=kOutput, calls=%fused_computation.153 | convolution fusion | flops 68719476736 | bytes 100663296 | tf_op jit(solution)/shard_map/dot_general | solution.py:125
  2798.1 78.4 %convolution_bitcast_fusion.1 = f32[2048,4096]{1,0:T(8,128)} fusion(bf16[8,512,2048]{1,2,0:T(8,128)(2,1)} %bitcast.518, bf16[8,512,4096]{2,1,0:T(8,128)(2,1)} %param.21), kind=kOutput, calls=%fused_computation.148 | convolution fusion | flops 68719476736 | bytes 83886080 | tf_op jit(solution)/shard_map/btk,btd->kd/dot_general | solution.py:128
  2876.5 98.4 %convolution_bitcast_fusion = f32[4096,2304]{1,0:T(8,128)} fusion(bf16[8,512,2304]{1,2,0:T(8,128)(2,1)} %bitcast.515, bf16[8,512,4096]{2,1,0:T(8,128)(2,1)} %param.20, f32[4096]{0:T(1024)S(1)} %copy-done.19, f32[8,512]{1,0:T(8,128)S(1)} %copy-done.17), kind=kOutput, calls=%fused_computation.144 | convolution fusion | flops 77376520192 | bytes 90210304 | tf_op jit(solution)/shard_map/btd,btk->dk/dot_general | solution.py:157
  2975.0 1215.0 %all-reduce.8.cloned.1.call-done = f32[8,512,4096]{2,1,0:T(8,128)} async-done(((f32[8,512,4096]{2,1,0:T(8,128)}), f32[8,512,4096]{2,1,0:T(8,128)}) %all-reduce.8.cloned.1.call-update) | async-done | bytes 67108880 | tf_op jit(solution)/shard_map/psum | solution.py:158
  4233.7 1412.5 %all-reduce.6.cloned.1.call-done = f32[8,512,4096]{2,1,0:T(8,128)} async-done(((f32[8,512,4096]{2,1,0:T(8,128)}), f32[8,512,4096]{2,1,0:T(8,128)}) %all-reduce.6.cloned.1.call-update) | async-done | bytes 67108880 | tf_op jit(solution)/shard_map/psum | solution.py:125
  5646.2 85.0 %fusion.122 = (bf16[8,512,4096]{2,1,0:T(8,128)(2,1)}, bf16[8,512,4096]{2,1,0:T(8,128)(2,1)}) fusion(bf16[8,512,4096]{2,1,0:T(8,128)(2,1)} %param.20, bf16[8,512,4096]{2,1,0:T(8,128)(2,1)} %param.21, f32[8,512,4096]{2,1,0:T(8,128)} %all-reduce.8.cloned.1.call-done, f32[8,512]{1,0:T(8,128)S(1)} %broadcast_multiply_fusion, f32[4096]{0:T(1024)S(1)} %copy-done.19, ...), kind=kLoop, calls=%fused_computation.135 | loop fusion | flops 184549376 | bytes 268484608 | tf_op jit(solution)/shard_map/convert_element_type | solution.py:39
  5731.1 1080.8 %all-reduce.10.cloned.1.call-done = (f32[4096,2304]{1,0:T(8,128)}, f32[2048,4096]{1,0:T(8,128)}) async-done(((f32[4096,2304]{1,0:T(8,128)}, f32[2048,4096]{1,0:T(8,128)}), (f32[4096,2304]{1,0:T(8,128)}, f32[2048,4096]{1,0:T(8,128)})) %all-reduce.10.cloned.1.call-update) | async-done | bytes 71303184 | tf_op jit(solution)/shard_map/psum | solution.py:157
  (200 shorter events, 840.3 us)
Async XLA Ops:
  7.2 4182.8 %all-reduce.8.cloned.1.call-start = ((), (), s32[]{:S(2)}) async-start(), calls=%async_computation.1 | async-start | bytes 134217728 | tf_op jit(solution)/shard_map/psum | solution.py:158
  308.4 98.2 %copy-start.11 = (f32[8,512]{1,0:T(8,128)}, f32[8,512]{1,0:T(8,128)S(1)}, u32[]{:S(2)}) copy-start(f32[8,512]{1,0:T(8,128)S(1)} %convert_element_type.168) | copy-start | bytes 49156
  311.1 46.2 copy-start.2
  430.8 171.0 %collective-permute-start = (bf16[8,512,1,2,128]{4,1,0,3,2:T(8,128)(2,1)}, bf16[8,512,1,2,128]{4,1,0,3,2:T(8,128)(2,1)}, u32[]{:S(2)}, u32[]{:S(2)}) collective-permute-start(bf16[8,512,1,2,128]{4,1,0,3,2:T(8,128)(2,1)} %copy.131), channel_id=1, source_target_pairs={{0,1},{1,2},{2,3},{3,0},{4,5},{5,6},{6,7},{7,4}} | collective-permute-start | bytes 6291464 | tf_op jit(solution)/shard_map/while/body/eval_jaxpr/ppermute | solution.py:115
  432.9 168.8 %collective-permute-start.1 = (s32[8,512]{1,0:T(8,128)}, s32[8,512]{1,0:T(8,128)}, u32[]{:S(2)}, u32[]{:S(2)}) collective-permute-start(s32[8,512]{1,0:T(8,128)} %copy.132), channel_id=1, source_target_pairs={{0,1},{1,2},{2,3},{3,0},{4,5},{5,6},{6,7},{7,4}} | collective-permute-start | bytes 49160 | tf_op jit(solution)/shard_map/while/body/eval_jaxpr/ppermute | solution.py:116
  604.9 25.6 collective-permute-start
  606.3 24.3 collective-permute-start.1
  633.7 167.6 %collective-permute-start = (bf16[8,512,1,2,128]{4,1,0,3,2:T(8,128)(2,1)}, bf16[8,512,1,2,128]{4,1,0,3,2:T(8,128)(2,1)}, u32[]{:S(2)}, u32[]{:S(2)}) collective-permute-start(bf16[8,512,1,2,128]{4,1,0,3,2:T(8,128)(2,1)} %copy.131), channel_id=1, source_target_pairs={{0,1},{1,2},{2,3},{3,0},{4,5},{5,6},{6,7},{7,4}} | collective-permute-start | bytes 6291464 | tf_op jit(solution)/shard_map/while/body/eval_jaxpr/ppermute | solution.py:115
  777.0 24.3 collective-permute-start.1
  890.3 51.7 copy-start
  1159.8 344.6 %collective-permute-start.2 = (f32[8,512,1,2,128]{4,1,0,3,2:T(8,128)}, f32[8,512,1,2,128]{4,1,0,3,2:T(8,128)}, u32[]{:S(2)}, u32[]{:S(2)}) collective-permute-start(f32[8,512,1,2,128]{4,1,0,3,2:T(8,128)} %get-tuple-element.1409), channel_id=1, source_target_pairs={{0,1},{1,2},{2,3},{3,0},{4,5},{5,6},{6,7},{7,4}} | collective-permute-start | bytes 12582920 | tf_op jit(solution)/shard_map/while/body/eval_jaxpr/ppermute | solution.py:145
  1159.8 367.3 %collective-permute-start.3 = (bf16[8,512,1,2,128]{4,1,0,3,2:T(8,128)(2,1)S(1)}, bf16[8,512,1,2,128]{4,1,0,3,2:T(8,128)(2,1)}, u32[]{:S(2)}, u32[]{:S(2)}) collective-permute-start(bf16[8,512,1,2,128]{4,1,0,3,2:T(8,128)(2,1)S(1)} %copy.153), channel_id=1, source_target_pairs={{0,1},{1,2},{2,3},{3,0},{4,5},{5,6},{6,7},{7,4}} | collective-permute-start | bytes 6291464 | tf_op jit(solution)/shard_map/while/body/eval_jaxpr/ppermute | solution.py:146
  1304.1 223.0 %collective-permute-start.4 = (s32[8,512]{1,0:T(8,128)S(1)}, s32[8,512]{1,0:T(8,128)S(1)}, u32[]{:S(2)}, u32[]{:S(2)}) collective-permute-start(s32[8,512]{1,0:T(8,128)S(1)} %copy.154), channel_id=1, source_target_pairs={{0,1},{1,2},{2,3},{3,0},{4,5},{5,6},{6,7},{7,4}} | collective-permute-start | bytes 49160 | tf_op jit(solution)/shard_map/while/body/eval_jaxpr/ppermute | solution.py:147
  1528.7 317.7 %collective-permute-start.2 = (f32[8,512,1,2,128]{4,1,0,3,2:T(8,128)}, f32[8,512,1,2,128]{4,1,0,3,2:T(8,128)}, u32[]{:S(2)}, u32[]{:S(2)}) collective-permute-start(f32[8,512,1,2,128]{4,1,0,3,2:T(8,128)} %get-tuple-element.1409), channel_id=1, source_target_pairs={{0,1},{1,2},{2,3},{3,0},{4,5},{5,6},{6,7},{7,4}} | collective-permute-start | bytes 12582920 | tf_op jit(solution)/shard_map/while/body/eval_jaxpr/ppermute | solution.py:145
  1755.8 113.3 %collective-permute-start.3 = (bf16[8,512,1,2,128]{4,1,0,3,2:T(8,128)(2,1)S(1)}, bf16[8,512,1,2,128]{4,1,0,3,2:T(8,128)(2,1)}, u32[]{:S(2)}, u32[]{:S(2)}) collective-permute-start(bf16[8,512,1,2,128]{4,1,0,3,2:T(8,128)(2,1)S(1)} %copy.153), channel_id=1, source_target_pairs={{0,1},{1,2},{2,3},{3,0},{4,5},{5,6},{6,7},{7,4}} | collective-permute-start | bytes 6291464 | tf_op jit(solution)/shard_map/while/body/eval_jaxpr/ppermute | solution.py:146
  1758.3 110.8 %collective-permute-start.4 = (s32[8,512]{1,0:T(8,128)S(1)}, s32[8,512]{1,0:T(8,128)S(1)}, u32[]{:S(2)}, u32[]{:S(2)}) collective-permute-start(s32[8,512]{1,0:T(8,128)S(1)} %copy.154), channel_id=1, source_target_pairs={{0,1},{1,2},{2,3},{3,0},{4,5},{5,6},{6,7},{7,4}} | collective-permute-start | bytes 49160 | tf_op jit(solution)/shard_map/while/body/eval_jaxpr/ppermute | solution.py:147
  1870.7 317.7 %collective-permute-start.2 = (f32[8,512,1,2,128]{4,1,0,3,2:T(8,128)}, f32[8,512,1,2,128]{4,1,0,3,2:T(8,128)}, u32[]{:S(2)}, u32[]{:S(2)}) collective-permute-start(f32[8,512,1,2,128]{4,1,0,3,2:T(8,128)} %get-tuple-element.1409), channel_id=1, source_target_pairs={{0,1},{1,2},{2,3},{3,0},{4,5},{5,6},{6,7},{7,4}} | collective-permute-start | bytes 12582920 | tf_op jit(solution)/shard_map/while/body/eval_jaxpr/ppermute | solution.py:145
  1870.7 340.3 %collective-permute-start.3 = (bf16[8,512,1,2,128]{4,1,0,3,2:T(8,128)(2,1)S(1)}, bf16[8,512,1,2,128]{4,1,0,3,2:T(8,128)(2,1)}, u32[]{:S(2)}, u32[]{:S(2)}) collective-permute-start(bf16[8,512,1,2,128]{4,1,0,3,2:T(8,128)(2,1)S(1)} %copy.153), channel_id=1, source_target_pairs={{0,1},{1,2},{2,3},{3,0},{4,5},{5,6},{6,7},{7,4}} | collective-permute-start | bytes 6291464 | tf_op jit(solution)/shard_map/while/body/eval_jaxpr/ppermute | solution.py:146
  2102.8 108.3 %collective-permute-start.4 = (s32[8,512]{1,0:T(8,128)S(1)}, s32[8,512]{1,0:T(8,128)S(1)}, u32[]{:S(2)}, u32[]{:S(2)}) collective-permute-start(s32[8,512]{1,0:T(8,128)S(1)} %copy.154), channel_id=1, source_target_pairs={{0,1},{1,2},{2,3},{3,0},{4,5},{5,6},{6,7},{7,4}} | collective-permute-start | bytes 49160 | tf_op jit(solution)/shard_map/while/body/eval_jaxpr/ppermute | solution.py:147
  2223.4 69.6 %copy-start.3 = (f32[8,512,32]{1,2,0:T(8,128)S(1)}, f32[8,512,32]{1,2,0:T(8,128)}, u32[]{:S(2)}) copy-start(f32[8,512,32]{1,2,0:T(8,128)} %copy-done.2) | copy-start | bytes 1572868
  2223.4 69.6 %copy-start.6 = (f32[8,512,32]{1,2,0:T(8,128)S(1)}, f32[8,512,32]{1,2,0:T(8,128)}, u32[]{:S(2)}) copy-start(f32[8,512,32]{1,2,0:T(8,128)} %get-tuple-element.1261) | copy-start | bytes 1572868
  2293.0 310.6 %collective-permute-start.5 = (f32[8,512,1,2,128]{1,4,3,0,2:T(8,128)}, f32[8,512,1,2,128]{1,4,3,0,2:T(8,128)}, u32[]{:S(2)}, u32[]{:S(2)}) collective-permute-start(f32[8,512,1,2,128]{1,4,3,0,2:T(8,128)} %copy.59), channel_id=1, source_target_pairs={{0,1},{1,2},{2,3},{3,0},{4,5},{5,6},{6,7},{7,4}} | collective-permute-start | bytes 12582920 | tf_op jit(solution)/shard_map/ppermute | solution.py:153
  2339.0 267.3 %copy-start.12 = (f32[8,512]{1,0:T(8,128)S(1)}, f32[8,512]{1,0:T(8,128)}, u32[]{:S(2)}) copy-start(f32[8,512]{1,0:T(8,128)} %copy-done.11) | copy-start | bytes 49156
  2339.0 267.3 %copy-start.25 = (f32[32]{0:T(128)S(1)}, f32[32]{0:T(128)}, u32[]{:S(2)}) copy-start(f32[32]{0:T(128)} %negate_power_fusion) | copy-start | bytes 388
  2352.0 258.6 %slice-start.8 = ((s8[8388608]{0:T(1024)(128)(4,1)}), s8[4194304]{0:T(1024)(128)(4,1)S(1)}, s32[]{:S(2)}) async-start(s8[8388608]{0:T(1024)(128)(4,1)} %bitcast.511), calls=%async_computation.11 | async-start | bytes 8388608
  2358.8 251.8 %slice-start.9 = ((s8[8388608]{0:T(1024)(128)(4,1)}), s8[4194304]{0:T(1024)(128)(4,1)S(1)}, s32[]{:S(2)}) async-start(s8[8388608]{0:T(1024)(128)(4,1)} %bitcast.511), calls=%async_computation.12 | async-start | bytes 8388608
  2718.2 2928.0 %all-reduce.6.cloned.1.call-start = ((), (), s32[]{:S(2)}) async-start(), calls=%async_computation | async-start | bytes 134217728 | tf_op jit(solution)/shard_map/psum | solution.py:125
  2798.1 4013.9 %all-reduce.10.cloned.1.call-start = ((), (), s32[]{:S(2)}) async-start(), calls=%async_computation.2 | async-start | bytes 142606336 | tf_op jit(solution)/shard_map/psum | solution.py:157
  2798.1 78.4 %copy-start.17 = (f32[8,512]{1,0:T(8,128)S(1)}, f32[8,512]{1,0:T(8,128)}, u32[]{:S(2)}) copy-start(f32[8,512]{1,0:T(8,128)} %copy-done.16) | copy-start | bytes 49156
  2798.1 78.4 %copy-start.19 = (f32[4096]{0:T(1024)S(1)}, f32[4096]{0:T(1024)}, u32[]{:S(2)}) copy-start(f32[4096]{0:T(1024)} %copy-done.18) | copy-start | bytes 49156
  2975.0 1246.3 %copy-start.20 = (f32[18,128]{1,0:T(8,128)S(1)}, f32[18,128]{1,0:T(8,128)}, u32[]{:S(2)}) copy-start(f32[18,128]{1,0:T(8,128)} %get-tuple-element.1236) | copy-start | bytes 27652
  6812.0 34.7 slice-start.7
  (18 other events, 351.9 us)
Sparse Core Ops, SparseCore 0:
  2718.3 1471.6 all-reduce.7
  4192.4 1453.6 all-reduce.5
  5649.4 1162.4 all-reduce.9
where the time goes:
time: 6880 us; the launch traced here: 6870 us
  waiting for transfers between devices  4190 us (61%)
  starting transfers between devices  991 us (14%)
  matrix products  898 us (13%)
  local copies, waits for them, and re-layouts  380 us (6%)
  other arithmetic  353 us (5%)
    psum x1, waiting for transfers between devices, body(): lax.psum(jnp.dot(context_flat, w_out, preferred_element_type=jnp.float32)...  1410 us
    psum x1, waiting for transfers between devices, body(): lax.psum(jnp.einsum('btk,dk->btd', d_proj, w_qkv, preferred_element_type=...  1220 us
    psum x1, waiting for transfers between devices, body(): lax.psum(jnp.einsum('btd,btk->dk', h_in, d_proj, preferred_element_type=j...  1080 us
    ppermute x3, starting transfers between devices, bwd_loop(): kv_blk = lax.ppermute(kv_blk, 'cp', shift)  379 us
    ppermute x1, waiting for transfers between devices, body(): dkv_own = lax.ppermute(dkv_acc, 'cp', shift)  245 us
    ppermute x3, starting transfers between devices, bwd_loop(): key_doc = lax.ppermute(key_doc, 'cp', shift)  237 us
    ppermute x3, starting transfers between devices, bwd_loop(): dkv_acc = lax.ppermute(dkv_acc, 'cp', shift)  227 us
    ppermute x3, starting transfers between devices, fwd_loop(): kv_blk = lax.ppermute(kv_blk, 'cp', shift)  143 us
  transfers between devices with their start and end apart: 19, of which 12 were waited for; matrix products, arithmetic and copies ran while one was open for 9% of the time, Pallas kernels for 0%

commit v1 on v0

v1 whole, which is shorter than its diff:
```python
import functools
import math

import jax
import jax.numpy as jnp
from jax import lax
from jax.experimental import pallas as pl
from jax.experimental.pallas import tpu as pltpu
from jax.sharding import PartitionSpec as P


HEAD = 128
ROT = 64
EPS = 1.5625e-07
ROPE_BASE = 5000000.0
TQ = 256
TK = 256
COLS = 512
NEG = -3e38
SCALE = HEAD ** -0.5
SCALE2 = SCALE * math.log2(math.e)
BF = jnp.bfloat16
F32 = jnp.float32
VMEM_ALL = 67043328


def mxu(a, b, contract=((1,), (0,))):
    return lax.dot_general(a, b, (contract, ((), ())), preferred_element_type=F32)


def swap_pairs(v):
    n = v.shape[0]
    even = lax.broadcasted_iota(jnp.int32, v.shape, 0) % 2 == 0
    return jnp.where(even, pltpu.roll(v, n - 1, 0), pltpu.roll(v, 1, 0))


def kernel_call(body, us, grid, in_specs, out_specs, out_shape, args, scratch=(), prefetch=0, alias=None):
    return pl.pallas_call(
        body,
        grid_spec=pltpu.PrefetchScalarGridSpec(
            num_scalar_prefetch=prefetch, grid=grid, in_specs=in_specs, out_specs=out_specs, scratch_shapes=scratch),
        out_shape=out_shape,
        input_output_aliases=alias or {},
        compiler_params=pltpu.CompilerParams(dimension_semantics=("arbitrary",) * len(grid), vmem_limit_bytes=VMEM_ALL),
        cost_estimate=pl.CostEstimate(flops=int(us * 9.96e8), bytes_accessed=int(us * 1e6), transcendentals=0),
    )(*args)


def shape(dims, dtype):
    return jax.ShapeDtypeStruct(dims, dtype)


ANYWHERE = pl.BlockSpec(memory_space=pl.ANY)


def once(dims, column=0):
    return pl.BlockSpec(dims, lambda *_: (0, column), pipeline_mode=pl.Buffered(1))


def rows_of(tm, width, first=0):
    return pl.BlockSpec((tm, width), lambda i, *_: (i + first, 0))


def cols_of(height, tn, first=0):
    return pl.BlockSpec((height, tn), lambda i, *_: (0, i + first))


def tiles_of(dims, nq, b0=0):
    return pl.BlockSpec(dims, lambda b, i, *_: ((b + b0) * nq + i,) + (0,) * (len(dims) - 1))


def tile_cols(height, nq, b0=0):
    return pl.BlockSpec((height, TQ), lambda b, i, *_: (0, (b + b0) * nq + i))


def with_whole(body, n_in, args, in_specs, whole):
    if whole is None:
        return body, {}
    first, extra = len(args), len(whole)
    in_specs += [ANYWHERE] * extra
    args += whole
    return (lambda *refs: body(*refs[:n_in], *refs[n_in + extra:])), {first + u: u for u in range(extra)}


def ride(steps, step_of, quarter, arrays):
    n = steps // 2
    rows, width = arrays[0].shape[0] // n, arrays[0].shape[1]

    def held(slot):
        return pl.BlockSpec((rows, width), lambda *g: (jnp.clip(step_of(*g) - slot * n, 0, n - 1), 0))

    def put(*g):
        return quarter(g[-1][0] % 2 ^ (step_of(*g) // n)) * n + step_of(*g) % n

    return [held(0), held(0), held(1), held(1)], (rows, width), put


def put_sums(step, steps, refs, o_ref):
    for slot in range(2):
        @pl.when(step // (steps // 2) == slot)
        def _():
            o_ref[...] = refs[2 * slot][...] + refs[2 * slot + 1][...]


def head_slice(h):
    return slice(h * HEAD, (h + 1) * HEAD)


def tok_slice(h):
    return slice(h * TQ, (h + 1) * TQ)


def prep_kernel(x_ref, gain_ref, w_ref, b_ref, cos_ref, sin_ref, h_ref, r_ref, kv_ref):
    rows, d = x_ref.shape
    total = jnp.zeros((rows, HEAD), F32)
    for c in range(0, d, HEAD):
        x = x_ref[:, c:c + HEAD].astype(F32)
        total += x * x
    r = lax.rsqrt(jnp.sum(total, axis=1, keepdims=True) * (1.0 / d) + EPS)
    r_ref[...] = r
    for c in range(0, d, HEAD):
        h_ref[:, c:c + HEAD] = (x_ref[:, c:c + HEAD].astype(F32) * r * gain_ref[:, c:c + HEAD]).astype(BF)
    kv = (mxu(h_ref[...], w_ref[...]) + b_ref[...]).astype(BF)
    k = kv[:, :HEAD].T
    top = k[:ROT].astype(F32)
    turned = (top * cos_ref[...] + swap_pairs(top) * sin_ref[...]).astype(BF)
    kv_ref[:, :HEAD] = jnp.concatenate([turned, k[ROT:]], axis=0).T
    kv_ref[:, HEAD:] = kv[:, HEAD:]


def prep(x, gain, w, bias, cos_t, sin_t, qw):
    tokens, d = x.shape
    tm, kv = 256, 2 * HEAD
    row, tab = rows_of(tm, d), cols_of(ROT, tm)
    return kernel_call(
        prep_kernel, 28, (tokens // tm,),
        [row, once((1, d)), once((d, kv), qw // kv), once((1, kv), qw // kv), tab, tab],
        [row, rows_of(tm, 1), rows_of(tm, kv)],
        [shape((tokens, d), BF), shape((tokens, 1), F32), shape((tokens, kv), BF)],
        (x, gain, w, bias, cos_t, sin_t))


def q_kernel(h_ref, w_ref, b_ref, cos_ref, sin_ref, q_ref, qt_ref):
    nq = qt_ref.shape[0]
    for n in range(q_ref.shape[1] // COLS):
        c0 = n * COLS
        p = (mxu(h_ref[...], w_ref[:, c0:c0 + COLS]) + b_ref[:, c0:c0 + COLS]).astype(BF)
        for u in range(4):
            hs = slice(u * HEAD, (u + 1) * HEAD)
            for t in range(nq):
                ts = slice(t * TQ, (t + 1) * TQ)
                tile = p[ts, hs].T
                top = tile[:ROT].astype(F32)
                turned = (top * cos_ref[:, ts] + swap_pairs(top) * sin_ref[:, ts]).astype(BF)
                tile = jnp.concatenate([turned, tile[ROT:]], axis=0)
                qt_ref[t, :, (c0 // HEAD + u) * TQ:(c0 // HEAD + u + 1) * TQ] = tile
                q_ref[ts, c0 + u * HEAD:c0 + (u + 1) * HEAD] = tile.T


def q_turn_kernel(s_ref, h_ref, w_ref, b_ref, cos_ref, sin_ref, rows_ref, q_ref, qt_ref, t_ref, half_ref):
    t = rows_ref[...].T
    t_ref[...] = t

    @pl.when(pl.program_id(0) // (pl.num_programs(0) // 2) == s_ref[0] % 2)
    def _():
        half_ref[...] = t

    q_kernel(h_ref, w_ref, b_ref, cos_ref, sin_ref, q_ref, qt_ref)


def q_project(half, part, parts, whole, h, w, bias, cos_t, sin_t, qw, table=None):
    tokens, d = h.shape
    rows = 512
    nq = rows // TQ
    width = qw // 2
    cols = width // HEAD * TQ
    steps = tokens // rows // parts
    i0 = part * steps
    tab = cols_of(ROT, rows, i0)
    in_specs = [rows_of(rows, d, i0), once((d, width), half), once((1, width), half), tab, tab]
    out_specs = [rows_of(rows, width, i0), pl.BlockSpec((nq, HEAD, cols), lambda i, *_: (i + i0, 0, 0))]
    out_shape = [shape((tokens, width), BF), shape((tokens // TQ, HEAD, cols), BF)]
    args = [h, w, bias, cos_t, sin_t]
    body, alias = with_whole(q_kernel, len(args), args, in_specs, whole)
    if table is not None:
        body, nh, all_w = q_turn_kernel, steps // 2, w.shape[1]
        in_specs.append(rows_of(d // steps, all_w))
        out_specs += [cols_of(all_w, d // steps),
                      pl.BlockSpec((all_w, d // steps), lambda i, s: (0, jnp.clip(i - s[0] % 2 * nh, 0, nh - 1)))]
        out_shape += [shape((all_w, d), BF), shape((all_w, d // 2), BF)]
        args = [table, *args, w]

    return kernel_call(body, 42 // parts, (steps,), in_specs, out_specs, out_shape, args, alias=alias, prefetch=int(table is not None))


def key_bias(start_ref, q0, k0):
    j = k0 + lax.broadcasted_iota(jnp.int32, (TK, TQ), 0)
    i = q0 + lax.broadcasted_iota(jnp.int32, (TK, TQ), 1)
    return jnp.where((j >= start_ref[0]) & (j <= i), 0.0, NEG).astype(F32)


def kv_slots(a_ref, b_ref):
    return ((a_ref, 0, 0), (a_ref, 1, 2), (b_ref, 0, 1), (b_ref, 1, 3))


def kv_spec(chunk, b0=0):
    return pl.BlockSpec((2, 1, chunk, 2 * HEAD), lambda b, *_: (0, b + b0, 0, 0))


def start_spec(b0=0):
    return pl.BlockSpec((1, 1, TQ), lambda b, i, *_: (b + b0, 0, i))


def key_range(s_ref, b, t, nq):
    q0 = s_ref[0] * (nq * TQ) + t * TQ
    return q0, s_ref[1 + b * nq + t] // TK, (q0 + TQ - 1) // TK + 1


def fwd_kernel(s_ref, start_ref, qt_ref, kva_ref, kvb_ref, o_ref, ct_ref, lse_ref, k_s, vt_s, t_s, acc_s, m_s, m8_s, l8_s, e_s):
    b, t, nq = pl.program_id(0), pl.program_id(1), pl.num_programs(1)
    heads = qt_ref.shape[2] // TQ
    chunk = kva_ref.shape[2]

    @pl.when(t == 0)
    def _():
        for ref, i, flip in kv_slots(kva_ref, kvb_ref):
            rows = pl.ds(pl.multiple_of((s_ref[0] ^ flip) * chunk, chunk), chunk)
            k_s[rows, :] = ref[i, 0, :, :HEAD]
            vt_s[:, rows] = ref[i, 0, :, HEAD:].T

    m8_s[...] = jnp.full_like(m8_s, NEG)
    l8_s[...] = jnp.zeros_like(l8_s)
    acc_s[...] = jnp.zeros_like(acc_s)
    q0, lo, hi = key_range(s_ref, b, t, nq)

    def scores(kb, _):
        rows = pl.ds(pl.multiple_of(kb * TK, TK), TK)
        bias = key_bias(start_ref, q0, kb * TK)
        k = k_s[rows, :]
        for h in range(heads):
            sl = tok_slice(h)
            s = mxu(k, qt_ref[0, :, sl]) * SCALE2 + bias
            t_s[rows, sl] = s
            m8_s[:, sl] = jnp.maximum(m8_s[:, sl], jnp.max(s.reshape(TK // 8, 8, TQ), axis=0))
        return 0

    lax.fori_loop(lo, hi, scores, 0)
    m_s[...] = jnp.max(m8_s[...], axis=0, keepdims=True)

    def accumulate(kb, _):
        rows = pl.ds(pl.multiple_of(kb * TK, TK), TK)
        for h in range(heads):
            sl = tok_slice(h)
            e = jnp.exp2(t_s[rows, sl] - m_s[:, sl])
            l8_s[:, sl] += jnp.sum(e.reshape(TK // 8, 8, TQ), axis=0)
            e_s[:, sl] = e.astype(BF)
        acc_s[...] += mxu(vt_s[:, rows], e_s[...])
        return 0

    lax.fori_loop(lo, hi, accumulate, 0)
    l = jnp.sum(l8_s[...], axis=0, keepdims=True)
    lse_ref[0] = m_s[...] + jnp.log2(l)
    l8_s[0:1, :] = 1.0 / l
    for h in range(heads):
        sl = tok_slice(h)
        ct = (acc_s[:, sl] * l8_s[0:1, sl]).astype(BF)
        ct_ref[0, :, sl] = ct
        o_ref[:, head_slice(h)] = ct.T


def attn_fwd(table, start, qt, kva, kvb):
    batch, _, chunk = start.shape
    nq = chunk // TQ
    n, _, cols = qt.shape
    width = cols // TQ * HEAD
    keys = 4 * chunk
    kv, tile = kv_spec(chunk), tiles_of((1, HEAD, cols), nq)
    return kernel_call(
        fwd_kernel, 65, (batch, nq),
        [start_spec(), tile, kv, kv],
        [tiles_of((TQ, width), nq), tile, tiles_of((1, 1, cols), nq)],
        [shape((n * TQ, width), BF), shape((n, HEAD, cols), BF), shape((n, 1, cols), F32)], (table, start, qt, kva, kvb),
        [pltpu.VMEM((keys, HEAD), BF), pltpu.VMEM((HEAD, keys), BF), pltpu.VMEM((keys, cols), F32), pltpu.VMEM((HEAD, cols), F32),
         pltpu.VMEM((1, cols), F32), pltpu.VMEM((8, cols), F32), pltpu.VMEM((8, cols), F32), pltpu.VMEM((TK, cols), BF)],
        prefetch=1)


def bwd_kernel(b0, riding, s_ref, start_ref, qta_ref, qtb_ref, qa_ref, qb_ref, dcta_ref, dctb_ref, cta_ref, ctb_ref, la_ref, lb_ref,
               cos_ref, sin_ref, kva_ref, kvb_ref, *refs):
    nb, nq = pl.num_programs(0), pl.num_programs(1)
    if riding:
        put_sums(pl.program_id(0) * nq + pl.program_id(1), nb * nq, refs[:riding], refs[riding + 5])
    dq_ref, half_ref, dkv0_ref, dkv1_ref, dkvb_ref = refs[riding:riding + 5]
    kv_s, kt_s, dct_s, qd_s, dqt_s, delta_s, pd_s, dkv_s = refs[-8:]
    b, t = pl.program_id(0) + b0, pl.program_id(1)
    heads = dq_ref.shape[1] // HEAD
    chunk = kva_ref.shape[2]

    @pl.when(t == 0)
    def _():
        for ref, i, flip in kv_slots(kva_ref, kvb_ref):
            rows = pl.ds(pl.multiple_of((s_ref[0] ^ flip) * chunk, chunk), chunk)
            kv_s[rows, :] = ref[i, 0]
            kt_s[:, rows] = ref[i, 0, :, :HEAD].T
        dkv_s[...] = jnp.zeros_like(dkv_s)

    def of_head(h, a_ref, b_ref):
        return (a_ref, h) if h < heads // 2 else (b_ref, h - heads // 2)

    for h in range(heads):
        sl = tok_slice(h)
        ref, u = of_head(h, dcta_ref, dctb_ref)
        dct = ref[head_slice(u), :]
        dct_s[:, sl] = dct
        ref, u = of_head(h, qa_ref, qb_ref)
        qd_s[sl, :HEAD] = ref[:, head_slice(u)]
        qd_s[sl, HEAD:] = dct.T
        ref, u = of_head(h, cta_ref, ctb_ref)
        delta_s[:, sl] = jnp.sum(dct.astype(F32) * ref[0, :, tok_slice(u)].astype(F32), axis=0, keepdims=True)
    dqt_s[...] = jnp.zeros_like(dqt_s)
    q0, lo, hi = key_range(s_ref, b, t, nq)

    def step(kb, _):
        rows = pl.ds(pl.multiple_of(kb * TK, TK), TK)
        bias = key_bias(start_ref, q0, kb * TK)
        k = kv_s[rows, :HEAD]
        v = kv_s[rows, HEAD:]
        for h in range(heads):
            sl = tok_slice(h)
            qt, u = of_head(h, qta_ref, qtb_ref)
            lse, _ = of_head(h, la_ref, lb_ref)
            us = tok_slice(u)
            p = jnp.exp2(mxu(k, qt[0, :, us]) * SCALE2 + bias - lse[0, :, us])
            pd_s[TK:, sl] = p.astype(BF)
            pd_s[:TK, sl] = (p * (mxu(v, dct_s[:, sl]) - delta_s[:, sl])).astype(BF)
        dqt_s[...] += mxu(kt_s[:, rows], pd_s[:TK, :])
        both = mxu(pd_s[...], qd_s[...])
        dkv_s[rows, :HEAD] += both[:TK, :HEAD]
        dkv_s[rows, HEAD:] += both[TK:, HEAD:]
        return 0

    lax.fori_loop(lo, hi, step, 0)
    for h in range(heads):
        sl = tok_slice(h)
        top = dqt_s[:ROT, sl] * SCALE
        turned = top * cos_ref[...] - swap_pairs(top) * sin_ref[...]
        dq = jnp.concatenate([turned, dqt_s[ROT:, sl] * SCALE], axis=0).astype(BF).T
        dq_ref[:, head_slice(h)] = dq
        half_ref[:, head_slice(h)] = dq

    @pl.when(t == nq - 1)
    def _():
        for ref, flip in ((dkv0_ref.at[0], 0), (dkv1_ref.at[0], 2), (dkvb_ref.at[0, 0], 1), (dkvb_ref.at[1, 0], 3)):
            rows = pl.ds(pl.multiple_of((s_ref[0] ^ flip) * chunk, chunk), chunk)
            ref[:, :HEAD] = dkv_s[rows, :HEAD] * SCALE
            ref[:, HEAD:] = dkv_s[rows, HEAD:]


def attn_bwd(half, whole, sums, table, start, qts, qs, dcts, cts, lses, cos_t, sin_t, kva, kvb):
    batch, _, chunk = start.shape
    nq = chunk // TQ
    n, _, cols = qts[0].shape
    width = 2 * dcts[0].shape[0]
    keys = 4 * chunk
    nb = batch // 2
    b0 = half * nb
    kv, tile, line = kv_spec(chunk, b0), tiles_of((1, HEAD, cols), nq, b0), tiles_of((1, 1, cols), nq, b0)
    qrow, dct, tab = tiles_of((TQ, width // 2), nq, b0), tile_cols(width // 2, nq, b0), tile_cols(ROT, nq, b0)
    one = shape((nb, chunk, 2 * HEAD), F32)
    one_spec = pl.BlockSpec((1, chunk, 2 * HEAD), lambda b, *_: (b, 0, 0))
    in_specs = [start_spec(b0), tile, tile, qrow, qrow, dct, dct, tile, tile, line, line, tab, tab, kv, kv]
    args = [table, start, *qts, *qs, *dcts, *cts, *lses, cos_t, sin_t, kva, kvb]
    out_specs = [tiles_of((TQ, width), nq, b0), tiles_of((TQ, width), nq), one_spec, one_spec, kv_spec(chunk)]
    out_shape = [shape((n * TQ, width), BF), shape((n * TQ // 2, width), BF), one, one, shape((2, nb, chunk, 2 * HEAD), F32)]
    if sums:
        specs, block, put = ride(nb * nq, lambda b, i, s: b * nq + i, lambda core: core, sums)
        in_specs += specs
        args += sums
        out_specs.append(pl.BlockSpec(block, lambda *g: (put(*g), 0)))
        out_shape.append(shape((4 * sums[0].shape[0], block[1]), F32))
    body, alias = with_whole(functools.partial(bwd_kernel, b0, len(sums)), len(args), args, in_specs, whole)
    return kernel_call(
        body, 80, (nb, nq), in_specs, out_specs, out_shape, args,
        [pltpu.VMEM((keys, 2 * HEAD), BF), pltpu.VMEM((HEAD, keys), BF), pltpu.VMEM((HEAD, 2 * cols), BF), pltpu.VMEM((2 * cols, 2 * HEAD), BF),
         pltpu.VMEM((HEAD, 2 * cols), F32), pltpu.VMEM((1, 2 * cols), F32), pltpu.VMEM((2 * TK, 2 * cols), BF), pltpu.VMEM((keys, 2 * HEAD), F32)],
        prefetch=1, alias=alias)


def first_tile(total, a_s, b_s, w_ref, piece_refs, places, w_s, p_s, sems):
    n = w_s.shape[0] // 256
    part = piece_refs[0].shape[1]

    def copies(k):
        rows = pl.ds(pl.multiple_of(k * 256, 256), 256)
        moves = [(w_ref.at[rows, :], w_s.at[rows, :])]
        moves += [(ref.at[rows, :], p_s.at[rows, pl.ds(pl.multiple_of(c * part, part), part)]) for ref, c in zip(piece_refs, places)]
        return [pltpu.make_async_copy(src, dst, sems.at[u, k]) for u, (src, dst) in enumerate(moves)]

    ahead = 3
    for k in range(ahead):
        for copy in copies(k):
            copy.start()
    total[...] = jnp.zeros_like(total)

    def add(k, _):
        for copy in copies(k):
            copy.wait()

        @pl.when(k + ahead < n)
        def _():
            for copy in copies(k + ahead):
                copy.start()

        rows = pl.ds(pl.multiple_of(k * 256, 256), 256)
        for c in range(0, total.shape[1], COLS):
            cs = slice(c, c + COLS)
            total[:, cs] += mxu(a_s[:, rows], w_s[rows, cs]) + mxu(b_s[:, rows], p_s[rows, cs])
        return 0

    lax.fori_loop(0, n, add, 0)


def out_kernel(s_ref, x_ref, ca_ref, cb_ref, pa_ref, pb_ref, w_ref, p0_ref, p1_ref, p2_ref, p3_ref, *refs):
    put_ref, o_ref, w_s, p_s, c_s, d_s, total_s, sems = refs[-8:]
    put_sums(pl.program_id(0), pl.num_programs(0), refs[:-8], put_ref)
    k = ca_ref.shape[1]
    first = pl.program_id(0) == 0
    c_s[:, :k], c_s[:, k:] = ca_ref[...], cb_ref[...]
    d_s[:, :k], d_s[:, k:] = pa_ref[...], pb_ref[...]

    def finish(cs, acc):
        o_ref[:, cs] = (x_ref[:, cs].astype(F32) + acc).astype(BF)

    tiles = [slice(c, c + COLS) for c in range(0, o_ref.shape[1], COLS)]

    @pl.when(first)
    def _():
        first_tile(total_s, c_s, d_s, w_ref, (p0_ref, p1_ref, p2_ref, p3_ref), [s_ref[0] ^ flip for flip in (0, 2, 1, 3)], w_s, p_s, sems)
        for cs in tiles:
            finish(cs, total_s[:, cs])

    @pl.when(jnp.logical_not(first))
    def _():
        for cs in tiles:
            finish(cs, mxu(c_s[...], w_s[:, cs]) + mxu(d_s[...], p_s[:, cs]))


def out_project(table, x, ctx, peer, w, pieces, sums, whole):
    tokens, d = x.shape
    k = w.shape[0]
    tm = 256
    n = tokens // tm
    row, crow = rows_of(tm, d), rows_of(tm, k // 2)
    specs, block, put = ride(n, lambda i, s: i, lambda core: 2 + core, sums)
    in_specs = [row, crow, crow, crow, crow] + [ANYWHERE] * 5 + specs
    args = [table, x, *ctx, *peer, w, *pieces, *sums]
    body, alias = with_whole(out_kernel, len(args), args, in_specs, [whole])
    return kernel_call(
        body, 150, (n,), in_specs, [pl.BlockSpec(block, lambda *g: (put(*g), 0)), row],
        [shape(whole.shape, F32), shape((tokens, d), BF)], args,
        [pltpu.VMEM((k, d), BF), pltpu.VMEM((k, d), BF), pltpu.VMEM((tm, k), BF), pltpu.VMEM((tm, k), BF), pltpu.VMEM((tm, d), F32),
         pltpu.SemaphoreType.DMA((5, k // 256))], prefetch=1, alias=alias)


def finish_kernel(a_ref, b_ref, c_ref, cos_ref, sin_ref, o_ref):
    dkv = a_ref[0] + b_ref[0, 0] + c_ref[0]
    k = dkv[:, :HEAD].T
    top = k[:ROT]
    turned = top * cos_ref[...] - swap_pairs(top) * sin_ref[...]
    o_ref[:, :HEAD] = jnp.concatenate([turned, k[ROT:]], axis=0).T.astype(BF)
    o_ref[:, HEAD:] = dkv[:, HEAD:].astype(BF)


def finish_dkv(half, own, core, away, cos_t, sin_t):
    nb, chunk, width = own.shape
    one = pl.BlockSpec((1, chunk, width), lambda b: (b, 0, 0))
    tab = cols_of(ROT, chunk, half * nb)
    return kernel_call(
        finish_kernel, 4, (nb,), [one, kv_spec(chunk), one, tab, tab], rows_of(chunk, width),
        shape((nb * chunk, width), BF), (own, core, away, cos_t, sin_t))


def dh_kernel(s_ref, x_ref, g_ref, r_ref, gain_ref, qa_ref, ka_ref, qb_ref, kb_ref, w_ref, p0_ref, p1_ref,
              gx_ref, gg_ref, gb_ref, dh_s, gg8_s, gb8_s, w_s, p_s, a_s, b_s, sems):
    i = pl.program_id(0)
    qw = qa_ref.shape[1]
    tm, d = x_ref.shape
    a_s[:, :qw], a_s[:, qw:] = qa_ref[...], ka_ref[...]
    b_s[:, :qw], b_s[:, qw:] = qb_ref[...], kb_ref[...]

    @pl.when(i == 0)
    def _():
        gg8_s[...] = jnp.zeros_like(gg8_s)
        gb8_s[...] = jnp.zeros_like(gb8_s)
        core = s_ref[0] % 2
        first_tile(dh_s, a_s, b_s, w_ref, (p0_ref, p1_ref), (core, 1 - core), w_s, p_s, sems)

    @pl.when(i > 0)
    def _():
        for c in range(0, d, COLS):
            cs = slice(c, c + COLS)
            dh_s[:, cs] = mxu(a_s[...], w_s[:, cs]) + mxu(b_s[...], p_s[:, cs])

    def norm(k, _):
        n = 128
        rs = pl.ds(pl.multiple_of(k * n, n), n)
        r = jnp.broadcast_to(r_ref[rs, :], (n, HEAD))
        total = jnp.zeros((n, HEAD), F32)
        for c in range(0, d, HEAD):
            cs = slice(c, c + HEAD)
            prod = dh_s[rs, cs] * (x_ref[rs, cs].astype(F32) * r)
            gg8_s[:, cs] += jnp.sum(prod.reshape(n // 8, 8, HEAD), axis=0)
            total += prod * gain_ref[:, cs]
        mean = jnp.sum(total, axis=1, keepdims=True) * (1.0 / d)
        r_mean = jnp.broadcast_to(r_ref[rs, :] * mean, (n, HEAD))
        for c in range(0, d, HEAD):
            cs = slice(c, c + HEAD)
            part_x = dh_s[rs, cs] * gain_ref[:, cs] - x_ref[rs, cs].astype(F32) * r_mean
            gx_ref[rs, cs] = (g_ref[rs, cs].astype(F32) + r * part_x).astype(BF)
        for c in range(0, a_s.shape[1], HEAD):
            cs = slice(c, c + HEAD)
            gb8_s[:, cs] += jnp.sum(a_s[rs, cs].astype(F32).reshape(n // 8, 8, HEAD), axis=0)
        return 0

    lax.fori_loop(0, tm // 128, norm, 0)

    @pl.when(i == pl.num_programs(0) - 1)
    def _():
        gg_ref[...] = jnp.sum(gg8_s[...], axis=0, keepdims=True)
        gb_ref[...] = jnp.sum(gb8_s[...], axis=0, keepdims=True)


def dh_norm(half, whole, table, x, g, r, gain, qa, ka, qb, kb, wt, pieces):
    tokens, d = x.shape
    tm = 256
    nt = tokens // tm // 2
    i0 = half * nt
    qw, kw = qa.shape[1], ka.shape[1]
    row = rows_of(tm, d, i0)
    in_specs = [row, row, rows_of(tm, 1, i0), once((1, d)), rows_of(tm, qw, i0), rows_of(tm, kw), rows_of(tm, qw), rows_of(tm, kw)] + [ANYWHERE] * 3
    args = [table, x, g, r, gain, qa, ka, qb, kb, wt, *pieces]
    body, alias = with_whole(dh_kernel, len(args), args, in_specs, whole)
    all_w = qw + kw
    return kernel_call(
        body, 100, (nt,), in_specs, [row, once((1, d)), once((1, all_w))],
        [shape((tokens, d), BF), shape((1, d), F32), shape((1, all_w), F32)], args,
        [pltpu.VMEM((tm, d), F32), pltpu.VMEM((8, d), F32), pltpu.VMEM((8, all_w), F32), pltpu.VMEM((all_w, d), BF), pltpu.VMEM((all_w, d), BF),
         pltpu.VMEM((tm, all_w), BF), pltpu.VMEM((tm, all_w), BF), pltpu.SemaphoreType.DMA((3, all_w // 256))],
        prefetch=1, alias=alias)


def place_kernel(s_ref, a_ref, b_ref, c_ref, d_ref, o_ref):
    put_sums(pl.program_id(0), pl.num_programs(0), (a_ref, b_ref, c_ref, d_ref), o_ref)


def place(table, sums, quarter, column, whole, dims):
    steps = 8
    in_specs, block, put = ride(steps, lambda i, s: i, quarter, sums)
    args = [table, *sums]
    body, alias = with_whole(place_kernel, len(args), args, in_specs, whole)
    return kernel_call(
        body, 20, (steps,), in_specs, pl.BlockSpec(block, lambda *g: (put(*g), column)), shape(dims, F32), args, prefetch=1, alias=alias)


def solution(mesh):
    over_tp = [(i, 1 - i) for i in range(2)]
    over_x = [(i, i ^ 2) for i in range(4)]
    over_core = [(i, i ^ 1) for i in range(4)]

    def send_tp(v):
        return lax.ppermute(v, 'tp', over_tp)

    def send_x(v, pairs=over_x):
        return lax.ppermute(v, 'cp', pairs)

    def send_core(v):
        return lax.ppermute(v, 'cp', over_core)

    def body(x_blk, grad_blk, norm_gain, w_qkv, b_qkv, w_out, doc_blk, pos_blk):
        batch, chunk, d = x_blk.shape
        tokens = batch * chunk
        qw = w_out.shape[0]
        cp = lax.axis_index('cp')
        core = cp % 2
        x = x_blk.reshape(tokens, d)
        g = grad_blk.reshape(tokens, d)
        gain = norm_gain[None].astype(F32)
        bias = b_qkv[None].astype(F32)

        start = cp * chunk + jnp.arange(chunk, dtype=jnp.int32)[None] - pos_blk
        table = jnp.concatenate([cp[None].astype(jnp.int32), start[:, ::TQ].reshape(-1)])
        start = start[:, None, :]
        me = table[:1]

        inv_freq = 1.0 / ROPE_BASE ** (jnp.arange(0, ROT, 2, dtype=F32) / ROT)
        angles = pos_blk.reshape(1, tokens).astype(F32) * jnp.repeat(inv_freq, 2)[:, None]
        sign = jnp.where(jnp.arange(ROT) % 2 == 0, -1.0, 1.0)[:, None]
        cos_t = jnp.cos(angles)
        sin_t = jnp.sin(angles) * sign

        wo0 = send_tp(lax.dynamic_slice_in_dim(w_out, cp * (d // 4), d // 4, 1))
        h, inv_rms, kv = prep(x, gain, w_qkv, bias, cos_t, sin_t, qw)
        kv_own = kv.reshape(batch, chunk, 2 * HEAD)
        kva = jnp.stack([kv_own, send_x(kv_own, over_x[:2])])
        kvb = send_core(kva)
        q_args = (h, w_qkv, bias, cos_t, sin_t, qw)
        qa, qta, wq_t, wq_half = q_project(0, 0, 1, None, *q_args, table=me)
        wq0 = send_tp(wq_half)
        wo1 = send_x(wo0)
        wo_pieces = (wo0, wo1, send_core(wo0), send_core(wo1))
        wq_pieces = (wq0, send_core(wq0))

        ctx_a, ct_a, lse_a = attn_fwd(table, start, qta, kva, kvb)
        qb, qtb = q_project(1, 1, 2, q_project(1, 0, 2, None, *q_args), *q_args)
        ctx_b, ct_b, lse_b = attn_fwd(table, start, qtb, kva, kvb)
        peer_ctx = (send_tp(ctx_a), send_tp(ctx_b))

        def part(lhs, rhs, first, k):
            cols = lax.dynamic_slice_in_dim(lhs, first * k, k, 1)
            return lax.dot_general(cols, rhs, (((0,), (0,)), ((), ())), preferred_element_type=F32)

        def across(v):
            other = send_x(v)
            return [v, other, send_core(v), send_core(other)]

        go = []
        for ctx in (ctx_a, ctx_b):
            k = ctx.shape[1] // 2
            got = send_core(part(ctx, g, 1 - core, k))
            mine = part(ctx, g, core, k) + got
            go.append(across(mine))

        def grad_ctx(w):
            return lax.dot_general(w, g, (((1,), (1,)), ((), ())), preferred_element_type=F32).astype(BF)

        dctx_t = (grad_ctx(w_out[:qw // 2]), grad_ctx(w_out[qw // 2:]))

        attn_args = (table, start, (qta, qtb), (qa, qb), dctx_t, (ct_a, ct_b), (lse_a, lse_b), cos_t, sin_t, kva, kvb)

        def own_dkv(half, own, away, others):
            got = send_core(others)
            return finish_dkv(half, own, got, send_x(away + got[1], over_x[2:]), cos_t, sin_t)

        dq, dq_a, *dkv_parts, gw_out = attn_bwd(0, None, go[0], *attn_args)
        dqp_a = send_tp(dq_a)
        dkv_a = own_dkv(0, *dkv_parts)
        dq, dq_b, *dkv_parts = attn_bwd(1, [dq], [], *attn_args)
        dqp_b = send_tp(dq_b)
        dkv_b = own_dkv(1, *dkv_parts)
        dkvp_a = send_tp(dkv_a)
        dkvp_b = send_tp(dkv_b)
        dkv = jnp.concatenate([dkv_a, dkv_b], axis=0)

        k = d // 4
        got = [send_core(part(h, dq, 2 * (1 - core) + i, k)) for i in range(2)]
        mine = [part(h, dq, 2 * core + i, k) + got[i] for i in range(2)]
        gq = [across(mine[i]) for i in range(2)]
        got = send_core(part(h, dkv, 1 - core, 2 * k))
        gkv = across(part(h, dkv, core, 2 * k) + got)
        dims = (d, w_qkv.shape[1])
        gw_qkv = place(me, gq[0], lambda core: 2 * core, 0, None, dims)
        gw_qkv = place(me, gq[1], lambda core: 2 * core + 1, 0, [gw_qkv], dims)
        gw_qkv = place(me, gkv, lambda core: core, qw // gkv[0].shape[1], [gw_qkv], dims)

        gw_out, out = out_project(me, x, (ctx_a, ctx_b), peer_ctx, w_out, wo_pieces, go[1], gw_out)

        dh_args = (me, x, g, inv_rms, gain, dq)
        grad_x, gain_a, bias_a = dh_norm(0, None, *dh_args, dkv_a, dqp_a, dkvp_a, wq_t, wq_pieces)
        grad_x, gain_b, bias_b = dh_norm(1, [grad_x], *dh_args, dkv_b, dqp_b, dkvp_b, wq_t, wq_pieces)
        nb = bias_a.shape[1]
        small = jnp.concatenate([bias_a + bias_b, gain_a + gain_b], axis=1).reshape(-1, HEAD)
        small = small + send_core(small)
        small = (small + send_x(small)).reshape(-1)
        return out.reshape(x_blk.shape), grad_x.reshape(x_blk.shape), small[nb:], gw_qkv, small[:nb], gw_out

    seq, rep, cols = P(None, 'cp', None), P(), P(None, 'tp')
    specs_in = (seq, seq, rep, cols, P('tp'), P('tp', None), P(None, 'cp'), P(None, 'cp'))
    specs_out = (seq, seq, rep, cols, P('tp'), P('tp', None))
    return jax.shard_map(body, mesh=mesh, in_specs=specs_in, out_specs=specs_out, check_vma=False)
```

time: 6880 us -> 1950 us (0.28)
  waiting for transfers between devices: 4190 us -> 695 us
  starting transfers between devices: 991 us -> 148 us
  Pallas kernels: 0 us -> 757 us
  matrix products: 898 us -> 310 us
  local copies, waits for them, and re-layouts: 380 us -> 9.24 us
  other arithmetic: 353 us -> 21.6 us
    psum x3 -> x0, waiting for transfers between devices: 3710 us -> none  [the longest x1 1410 us: body(): lax.psum(jnp.dot(context_flat, w_out, preferred_element_type=jnp.float32)...]
    ppermute x16 -> x40, starting transfers between devices: 991 us -> 148 us  [the longest x22 87.7 us: send_core(): return lax.ppermute(v, 'cp', over_core)]
    pallas_call x0 -> x16, Pallas kernels: none -> 757 us  [kernel_call(): pl.pallas_call(body, grid_spec=pltpu.PrefetchScalarGridSpec(num_scalar_pr...]
    dot_general x13 -> x12, matrix products: 898 us -> 310 us  [the longest x10 224 us: part(): lax.dot_general(cols, rhs, (((0,), (0,)), ((), ())), preferred_element_ty...]
    ppermute x16 -> x40, waiting for transfers between devices: 482 us -> 695 us  [the longest x10 416 us: send_x(): return lax.ppermute(v, 'cp', pairs)]
    reduce_sum x5 -> x0, other arithmetic: 125 us -> none  [the longest x1 41.2 us: fwd_update(): l_new = alpha * l_acc + jnp.sum(probs, axis=-1)]
    convert_element_type x4 -> x1, other arithmetic: 85 us -> 1.3 us  [body(): gain = norm_gain[None].astype(F32)]
    reshape x6 -> x1, local copies, waits for them, and re-layouts: 77.6 us -> 0.08 us  [body(): start[:, ::TQ].reshape(-1)]
  transfers between devices with their start and end apart: 19 -> 40, of which waited for: 12 -> 9; matrix products, arithmetic and copies ran while one was open for 9% -> 16% of each run, Pallas kernels for 0% -> 35%
where the time goes in v1:
time: 1950 us; the launch traced here: 1940 us
  Pallas kernels  757 us (39%)
  waiting for transfers between devices  695 us (36%)
  matrix products  310 us (16%)
  starting transfers between devices  148 us (8%)
  other arithmetic  21.6 us (1%)
    pallas_call x16, Pallas kernels, kernel_call(): pl.pallas_call(body, grid_spec=pltpu.PrefetchScalarGridSpec(num_scalar_pr...  757 us
    ppermute x10, waiting for transfers between devices, send_x(): return lax.ppermute(v, 'cp', pairs)  416 us
    ppermute x8, waiting for transfers between devices, send_tp(): return lax.ppermute(v, 'tp', over_tp)  276 us
    dot_general x10, matrix products, part(): lax.dot_general(cols, rhs, (((0,), (0,)), ((), ())), preferred_element_ty...  224 us
    ppermute x22, starting transfers between devices, send_core(): return lax.ppermute(v, 'cp', over_core)  87.7 us
    dot_general x2, matrix products, grad_ctx(): lax.dot_general(w, g, (((1,), (1,)), ((), ())), preferred_element_type=F32)  85.8 us
    ppermute x10, starting transfers between devices, send_x(): return lax.ppermute(v, 'cp', pairs)  51.2 us
  transfers between devices with their start and end apart: 40, of which 9 were waited for; matrix products, arithmetic and copies ran while one was open for 16% of the time, Pallas kernels for 35%

profile of v1, /device:TPU:0, one launch (start us, length us, event | category | flops | bytes accessed | tf_op | source)
XLA Modules:
  0.0 1941.8 jit_solution(12163069547091430684)
XLA Ops:
  9.7 33.1 %shard_map.118 = (bf16[4096,4096]{1,0:T(8,128)(2,1)}, f32[4096,1]{1,0:T(8,128)}, bf16[4096,256]{1,0:T(8,128)(2,1)}) custom-call(bf16[4096,4096]{1,0:T(8,128)(2,1)} %bitcast.54, f32[1,4096]{1,0:T(1,128)} %bitcast.43, bf16[4096,2304]{1,0:T(8,128)(2,1)} %refs_1_.1, f32[1,2304]{1,0:T(1,128)} %reshape.74.b_ref.refs_2_, ...), custom_call_target="tpu_custom_call" | custom-call | flops 27888001024 | bytes 28000000 | tf_op jit(solution)/shard_map/pallas_call | solution.py:38
  48.4 44.9 %collective-permute-done = bf16[8,512,256]{2,1,0:T(8,128)(2,1)S(1)} collective-permute-done((bf16[8,512,256]{2,1,0:T(8,128)(2,1)}, bf16[8,512,256]{2,1,0:T(8,128)(2,1)S(1)}, u32[]{:S(2)}, u32[]{:S(2)}) %collective-permute-start) | collective-permute-done | bytes 2097184 | tf_op jit(solution)/shard_map/ppermute | solution.py:574
  98.7 53.3 %shard_map.119 = (bf16[4096,1024]{1,0:T(8,128)(2,1)}, bf16[16,128,2048]{2,1,0:T(8,128)(2,1)}, bf16[2304,4096]{1,0:T(8,128)(2,1)}, bf16[2304,2048]{1,0:T(8,128)(2,1)}) custom-call(s32[1]{0:T(128)} %bitcast.s_ref.refs_0_, bf16[4096,4096]{1,0:T(8,128)(2,1)} %get-tuple-element.42.h_ref.refs_0_, bf16[4096,2304]{1,0:T(8,128)(2,1)} %refs_1_.1, ...), custom_call_target="tpu_custom_call" | custom-call | flops 41832001536 | bytes 42000000 | tf_op jit(solution)/shard_map/pallas_call | solution.py:38
  152.0 34.6 %shard_map.120 = (bf16[4096,1024]{1,0:T(8,128)(2,1)}, bf16[16,128,2048]{2,1,0:T(8,128)(2,1)}, f32[16,1,2048]{2,1,0:T(1,128)}) custom-call(s32[17]{0:T(128)} %pad_add_fusion.s_ref.refs_0_, s32[8,1,512]{2,1,0:T(1,128)} %broadcast_in_dim.22.start_ref.refs_1_, bf16[16,128,2048]{2,1,0:T(8,128)(2,1)} %get-tuple-element.43.qt_ref.qta_ref.refs_2_, ...), custom_call_target="tpu_custom_call" | custom-call | flops 64739999744 | bytes 65000000 | tf_op jit(solution)/shard_map/pallas_call | solution.py:38
  186.6 24.1 %fusion.22 = f32[512,4096]{1,0:T(8,128)} fusion(bf16[4096,4096]{1,0:T(8,128)(2,1)} %bitcast.46, bf16[4096,1024]{1,0:T(8,128)(2,1)} %get-tuple-element.45.refs_2_, s32[]{:T(128)S(6)} %select_n.55), kind=kOutput, calls=%fused_computation.21 | convolution fusion | flops 17179869184 | bytes 46137348 | tf_op jit(solution)/shard_map/dot_general | solution.py:620
  210.7 18.3 collective-permute-start.12
  235.6 25.7 %shard_map.121 = (bf16[4096,1024]{1,0:T(8,128)(2,1)}, bf16[16,128,2048]{2,1,0:T(8,128)(2,1)}) custom-call(bf16[4096,4096]{1,0:T(8,128)(2,1)} %get-tuple-element.42.h_ref.refs_0_, bf16[4096,2304]{1,0:T(8,128)(2,1)} %refs_1_.1, f32[1,2304]{1,0:T(1,128)} %reshape.74.b_ref.refs_2_, f32[64,4096]{1,0:T(8,128)} %get-tuple-element.79.cos_ref.refs_3_.refs_12_, ...), custom_call_target="tpu_custom_call" | custom-call | flops 20916000768 | bytes 21000000 | tf_op jit(solution)/shard_map/pallas_call | solution.py:38
  261.3 25.5 %shard_map.122 = (bf16[4096,1024]{1,0:T(8,128)(2,1)}, bf16[16,128,2048]{2,1,0:T(8,128)(2,1)}) custom-call(bf16[4096,4096]{1,0:T(8,128)(2,1)} %get-tuple-element.42.h_ref.refs_0_, bf16[4096,2304]{1,0:T(8,128)(2,1)} %refs_1_.1, f32[1,2304]{1,0:T(1,128)} %reshape.74.b_ref.refs_2_, ...), custom_call_target="tpu_custom_call", output_to_operand_aliasing={{0}: (5, {}), {1}: (6, {})} | custom-call | flops 20916000768 | bytes 21000000 | tf_op jit(solution)/shard_map/pallas_call | solution.py:38
  286.8 28.6 %convolution_add_fusion.refs_0_ = f32[512,4096]{1,0:T(8,128)} fusion(f32[512,4096]{1,0:T(8,128)} %collective-permute-done.12, bf16[4096,4096]{1,0:T(8,128)(2,1)} %bitcast.47, bf16[4096,1024]{1,0:T(8,128)(2,1)} %get-tuple-element.45.refs_2_, s32[]{:T(128)S(6)} %select_n.54), kind=kOutput, calls=%fused_computation.18 | convolution fusion | flops 17181966336 | bytes 54525956 | tf_op jit(solution)/shard_map/dot_general | solution.py:620
  323.9 43.1 %fusion.16.dcta_ref.refs_6_ = bf16[1024,4096]{1,0:T(8,128)(2,1)} fusion(bf16[4096,4096]{1,0:T(8,128)(2,1)} %bitcast.48, bf16[2048,4096]{1,0:T(8,128)(2,1)} %refs_6_.1), kind=kOutput, calls=%fused_computation.16 | convolution fusion | flops 34363932672 | bytes 50331648 | tf_op jit(solution)/shard_map/dot_general | solution.py:634
  366.9 42.7 %fusion.19.dctb_ref.refs_7_ = bf16[1024,4096]{1,0:T(8,128)(2,1)} fusion(bf16[4096,4096]{1,0:T(8,128)(2,1)} %bitcast.49, bf16[2048,4096]{1,0:T(8,128)(2,1)} %refs_6_.1), kind=kOutput, calls=%fused_computation.17 | convolution fusion | flops 34363932672 | bytes 50331648 | tf_op jit(solution)/shard_map/dot_general | solution.py:634
  409.6 95.2 %collective-permute-done.13.refs_1_ = f32[512,4096]{1,0:T(8,128)} collective-permute-done((f32[512,4096]{1,0:T(8,128)}, f32[512,4096]{1,0:T(8,128)}, u32[]{:S(2)}, u32[]{:S(2)}) %collective-permute-start.13) | collective-permute-done | bytes 8388640 | tf_op jit(solution)/shard_map/ppermute | solution.py:574
  504.8 34.6 %shard_map.123 = (bf16[4096,1024]{1,0:T(8,128)(2,1)}, bf16[16,128,2048]{2,1,0:T(8,128)(2,1)}, f32[16,1,2048]{2,1,0:T(1,128)}) custom-call(s32[17]{0:T(128)} %pad_add_fusion.s_ref.refs_0_, s32[8,1,512]{2,1,0:T(1,128)} %broadcast_in_dim.22.start_ref.refs_1_, bf16[16,128,2048]{2,1,0:T(8,128)(2,1)} %get-tuple-element.48.qt_ref.qtb_ref.refs_3_, ...), custom_call_target="tpu_custom_call" | custom-call | flops 64739999744 | bytes 65000000 | tf_op jit(solution)/shard_map/pallas_call | solution.py:38
  539.4 24.1 %fusion.25 = f32[512,4096]{1,0:T(8,128)} fusion(bf16[4096,4096]{1,0:T(8,128)(2,1)} %bitcast.50, bf16[4096,1024]{1,0:T(8,128)(2,1)} %get-tuple-element.49.refs_3_, s32[]{:T(128)S(6)} %select_n.55), kind=kOutput, calls=%fused_computation.24 | convolution fusion | flops 17179869184 | bytes 46137348 | tf_op jit(solution)/shard_map/dot_general | solution.py:620
  563.5 18.3 collective-permute-start.8
  581.9 59.1 %shard_map.124 = (bf16[4096,2048]{1,0:T(8,128)(2,1)}, bf16[2048,2048]{1,0:T(8,128)(2,1)}, f32[4,512,256]{2,1,0:T(8,128)}, f32[4,512,256]{2,1,0:T(8,128)}, f32[2,...) custom-call(s32[17]{0:T(128)} %pad_add_fusion.s_ref.refs_0_, s32[8,1,512]{2,1,0:T(1,128)} %broadcast_in_dim.22.start_ref.refs_1_, ...), custom_call_target="tpu_custom_call" | custom-call | flops 79679995904 | bytes 80000000 | tf_op jit(solution)/shard_map/pallas_call | solution.py:38
  641.0 24.3 %collective-permute-start.22 = (f32[2,4,512,256]{3,2,1,0:T(8,128)}, f32[2,4,512,256]{3,2,1,0:T(8,128)}, u32[]{:S(2)}, u32[]{:S(2)}) collective-permute-start(f32[2,4,512,256]{3,2,1,0:T(8,128)} %get-tuple-element.68), channel_id=1, source_target_pairs={{0,1},{1,0},{2,3},{3,2},{4,5},{5,4},{6,7},{7,6}} | collective-permute-start | bytes 12582920 | tf_op jit(solution)/shard_map/ppermute | solution.py:577
  665.3 51.2 %shard_map.126 = (bf16[4096,2048]{1,0:T(8,128)(2,1)}, bf16[2048,2048]{1,0:T(8,128)(2,1)}, f32[4,512,256]{2,1,0:T(8,128)}, f32[4,512,256]{2,1,0:T(8,128)}, f32[2,4,512,256]{3,2,1,0:T(8,128)}) custom-call(s32[17]{0:T(128)} %pad_add_fusion.s_ref.refs_0_, s32[8,1,512]{2,1,0:T(1,128)} %broadcast_in_dim.22.start_ref.refs_1_, ...), custom_call_target="tpu_custom_call", output_to_operand_aliasing={{0}: (16, {})} | custom-call | flops 79679995904 | bytes 80000000 | tf_op jit(solution)/shard_map/pallas_call | solution.py:38
  716.4 23.7 %collective-permute-start.16 = (f32[2,4,512,256]{3,2,1,0:T(8,128)}, f32[2,4,512,256]{3,2,1,0:T(8,128)}, u32[]{:S(2)}, u32[]{:S(2)}) collective-permute-start(f32[2,4,512,256]{3,2,1,0:T(8,128)} %get-tuple-element.62), channel_id=1, source_target_pairs={{0,1},{1,0},{2,3},{3,2},{4,5},{5,4},{6,7},{7,6}} | collective-permute-start | bytes 12582920 | tf_op jit(solution)/shard_map/ppermute | solution.py:577
  740.2 32.4 %collective-permute-start.5 = (bf16[2048,1024]{1,0:T(8,128)(2,1)}, bf16[2048,1024]{1,0:T(8,128)(2,1)}, u32[]{:S(2)}, u32[]{:S(2)}) collective-permute-start(bf16[2048,1024]{1,0:T(8,128)(2,1)} %collective-permute-done.4.refs_7_), channel_id=1, source_target_pairs={{0,2},{1,3},{2,0},{3,1},{4,6},{5,7},{6,4},{7,5}} | collective-permute-start | bytes 12582920 | tf_op jit(solution)/shard_map/ppermute | solution.py:574
  779.4 28.6 %convolution_add_fusion.1.refs_11_ = f32[512,4096]{1,0:T(8,128)} fusion(f32[512,4096]{1,0:T(8,128)} %collective-permute-done.8, bf16[4096,4096]{1,0:T(8,128)(2,1)} %bitcast.51, bf16[4096,1024]{1,0:T(8,128)(2,1)} %get-tuple-element.49.refs_3_, s32[]{:T(128)S(6)} %select_n.54), kind=kOutput, calls=%fused_computation.19 | convolution fusion | flops 17181966336 | bytes 54525956 | tf_op jit(solution)/shard_map/dot_general | solution.py:620
  811.1 97.5 %collective-permute-done.23.c_ref = f32[4,512,256]{2,1,0:T(8,128)} collective-permute-done((f32[4,512,256]{2,1,0:T(8,128)}, f32[4,512,256]{2,1,0:T(8,128)}, u32[]{:S(2)}, u32[]{:S(2)}) %collective-permute-start.23) | collective-permute-done | bytes 2097184 | tf_op jit(solution)/shard_map/ppermute | solution.py:574
  909.9 24.4 %fusion.4 = f32[1024,2048]{1,0:T(8,128)} fusion(bf16[4096,2048]{1,0:T(8,128)(2,1)} %get-tuple-element.60.qa_ref.refs_5_, bf16[4096,4096]{1,0:T(8,128)(2,1)} %get-tuple-element.42.h_ref.refs_0_, s32[]{:T(128)S(6)} %select_n.57), kind=kOutput, calls=%fused_computation.4 | convolution fusion | flops 17179869184 | bytes 33554436 | tf_op jit(solution)/shard_map/dot_general | solution.py:620
  959.3 24.1 %fusion.8 = f32[1024,2048]{1,0:T(8,128)} fusion(bf16[4096,2048]{1,0:T(8,128)(2,1)} %get-tuple-element.60.qa_ref.refs_5_, bf16[4096,4096]{1,0:T(8,128)(2,1)} %get-tuple-element.42.h_ref.refs_0_, s32[]{:T(128)S(6)} %select_n.59), kind=kOutput, calls=%fused_computation.8 | convolution fusion | flops 17179869184 | bytes 33554436 | tf_op jit(solution)/shard_map/dot_general | solution.py:620
  991.4 113.6 %shard_map.129 = (bf16[4096,4096]{1,0:T(8,128)(2,1)}, f32[1,4096]{1,0:T(1,128)}, f32[1,2304]{1,0:T(1,128)}) custom-call(s32[1]{0:T(128)} %bitcast.s_ref.refs_0_, bf16[4096,4096]{1,0:T(8,128)(2,1)} %bitcast.55, bf16[4096,4096]{1,0:T(8,128)(2,1)} %bitcast.52, f32[4096,1]{1,0:T(8,128)} %get-tuple-element.58.r_ref.refs_3_, f32[1,4096]{1,0:T(1,128)} %bitcast.44, ...), custom_call_target="tpu_custom_call" | custom-call | flops 99599998976 | bytes 100000000 | tf_op jit(solution)/shard_map/pallas_call | solution.py:38
  1105.1 25.3 %fusion.31.a_ref = f32[1024,2048]{1,0:T(8,128)} fusion(f32[1024,2048]{1,0:T(8,128)} %collective-permute-done.36, bf16[4096,2048]{1,0:T(8,128)(2,1)} %get-tuple-element.60.qa_ref.refs_5_, bf16[4096,4096]{1,0:T(8,128)(2,1)} %get-tuple-element.42.h_ref.refs_0_, s32[]{:T(128)S(6)} %select_n.56), kind=kOutput, calls=%fused_computation.28 | convolution fusion | flops 17181966336 | bytes 41943044 | tf_op jit(solution)/shard_map/dot_general | solution.py:620
  1130.9 24.8 %fusion.28.refs_1_ = f32[1024,2048]{1,0:T(8,128)} fusion(f32[1024,2048]{1,0:T(8,128)} %collective-permute-done.32, bf16[4096,2048]{1,0:T(8,128)(2,1)} %get-tuple-element.60.qa_ref.refs_5_, bf16[4096,4096]{1,0:T(8,128)(2,1)} %get-tuple-element.42.h_ref.refs_0_, s32[]{:T(128)S(6)} %select_n.58), kind=kOutput, calls=%fused_computation.27 | convolution fusion | flops 17181966336 | bytes 41943044 | tf_op jit(solution)/shard_map/dot_general | solution.py:620
  1173.0 201.6 %collective-permute-done.19.refs_8_ = bf16[2048,256]{1,0:T(8,128)(2,1)S(1)} collective-permute-done((bf16[2048,256]{1,0:T(8,128)(2,1)S(1)}, bf16[2048,256]{1,0:T(8,128)(2,1)S(1)}, u32[]{:S(2)}, u32[]{:S(2)}) %collective-permute-start.19) | collective-permute-done | bytes 1048608 | tf_op jit(solution)/shard_map/ppermute | solution.py:571
  1377.7 113.6 %shard_map.130 = (bf16[4096,4096]{1,0:T(8,128)(2,1)}, f32[1,4096]{1,0:T(1,128)}, f32[1,2304]{1,0:T(1,128)}) custom-call(s32[1]{0:T(128)} %bitcast.s_ref.refs_0_, bf16[4096,4096]{1,0:T(8,128)(2,1)} %bitcast.56, bf16[4096,4096]{1,0:T(8,128)(2,1)} %bitcast.53, f32[4096,1]{1,0:T(8,128)} %get-tuple-element.58.r_ref.refs_3_, ...), custom_call_target="tpu_custom_call", output_to_operand_aliasing={{0}: (12, {})} | custom-call | flops 99599998976 | bytes 100000000 | tf_op jit(solution)/shard_map/pallas_call | solution.py:38
  1492.9 59.0 %collective-permute-done.2.refs_4_ = bf16[4096,1024]{1,0:T(8,128)(2,1)} collective-permute-done((bf16[4096,1024]{1,0:T(8,128)(2,1)}, bf16[4096,1024]{1,0:T(8,128)(2,1)}, u32[]{:S(2)}, u32[]{:S(2)}) %collective-permute-start.2) | collective-permute-done | bytes 8388640 | tf_op jit(solution)/shard_map/ppermute | solution.py:571
  1576.7 159.9 %collective-permute-done.27 = f32[50,128]{1,0:T(8,128)} collective-permute-done((f32[50,128]{1,0:T(8,128)S(1)}, f32[50,128]{1,0:T(8,128)}, u32[]{:S(2)}, u32[]{:S(2)}) %collective-permute-start.27) | collective-permute-done | bytes 25632 | tf_op jit(solution)/shard_map/ppermute | solution.py:574
  1737.2 157.2 %shard_map.125 = (f32[2048,4096]{1,0:T(8,128)}, bf16[4096,4096]{1,0:T(8,128)(2,1)}) custom-call(s32[1]{0:T(128)} %bitcast.s_ref.refs_0_, bf16[4096,4096]{1,0:T(8,128)(2,1)} %bitcast.57, bf16[4096,1024]{1,0:T(8,128)(2,1)} %get-tuple-element.45.refs_2_, bf16[4096,1024]{1,0:T(8,128)(2,1)} %get-tuple-element.49.refs_3_, ...), custom_call_target="tpu_custom_call", output_to_operand_aliasing={{0}: (15, {})} | custom-call | flops 149399994368 | bytes 150000000 | tf_op jit(solution)/shard_map/pallas_call | solution.py:38
  (117 shorter events, 174.5 us)
Async XLA Ops:
  97.3 54.7 %collective-permute-start.1 = (bf16[2,8,512,256]{3,2,1,0:T(8,128)(2,1)}, bf16[2,8,512,256]{3,2,1,0:T(8,128)(2,1)}, u32[]{:S(2)}, u32[]{:S(2)}) collective-permute-start(bf16[2,8,512,256]{3,2,1,0:T(8,128)(2,1)} %pad_maximum_fusion.kva_ref.refs_14_), channel_id=1, source_target_pairs={{0,1},{1,0},{2,3},{3,2},{4,5},{5,4},{6,7},{7,6}} | collective-permute-start | bytes 12582920 | tf_op jit(solution)/shard_map/ppermute | solution.py:577
  210.7 76.1 %collective-permute-start.12 = (f32[512,4096]{1,0:T(8,128)}, f32[512,4096]{1,0:T(8,128)}, u32[]{:S(2)}, u32[]{:S(2)}) collective-permute-start(f32[512,4096]{1,0:T(8,128)} %fusion.22), channel_id=1, source_target_pairs={{0,1},{1,0},{2,3},{3,2},{4,5},{5,4},{6,7},{7,6}} | collective-permute-start | bytes 25165832 | tf_op jit(solution)/shard_map/ppermute | solution.py:577
  229.0 511.2 %collective-permute-start.20 = (bf16[2304,2048]{1,0:T(8,128)(2,1)}, bf16[2304,2048]{1,0:T(8,128)(2,1)}, u32[]{:S(2)}, u32[]{:S(2)}) collective-permute-start(bf16[2304,2048]{1,0:T(8,128)(2,1)} %get-tuple-element.66), channel_id=1, source_target_pairs={{0,4},{4,0},{1,5},{5,1},{2,6},{6,2},{3,7},{7,3}} | collective-permute-start | bytes 28311560 | tf_op jit(solution)/shard_map/ppermute | solution.py:571
  235.1 505.1 %collective-permute-start.4 = (bf16[2048,1024]{1,0:T(8,128)(2,1)}, bf16[2048,1024]{1,0:T(8,128)(2,1)}, u32[]{:S(2)}, u32[]{:S(2)}) collective-permute-start(bf16[2048,1024]{1,0:T(8,128)(2,1)} %constant_dynamic-slice_fusion), channel_id=1, source_target_pairs={{0,4},{4,0},{1,5},{5,1},{2,6},{6,2},{3,7},{7,3}} | collective-permute-start | bytes 12582920 | tf_op jit(solution)/shard_map/ppermute | solution.py:571
  315.4 189.4 %collective-permute-start.13 = (f32[512,4096]{1,0:T(8,128)}, f32[512,4096]{1,0:T(8,128)}, u32[]{:S(2)}, u32[]{:S(2)}) collective-permute-start(f32[512,4096]{1,0:T(8,128)} %convolution_add_fusion.refs_0_), channel_id=1, source_target_pairs={{0,2},{1,3},{2,0},{3,1},{4,6},{5,7},{6,4},{7,5}} | collective-permute-start | bytes 25165832 | tf_op jit(solution)/shard_map/ppermute | solution.py:574
  409.6 172.3 %collective-permute-start.14 = (f32[512,4096]{1,0:T(8,128)}, f32[512,4096]{1,0:T(8,128)}, u32[]{:S(2)}, u32[]{:S(2)}) collective-permute-start(f32[512,4096]{1,0:T(8,128)} %convolution_add_fusion.refs_0_), channel_id=1, source_target_pairs={{0,1},{1,0},{2,3},{3,2},{4,5},{5,4},{6,7},{7,6}} | collective-permute-start | bytes 25165832 | tf_op jit(solution)/shard_map/ppermute | solution.py:577
  504.8 77.1 %collective-permute-start.15 = (f32[512,4096]{1,0:T(8,128)}, f32[512,4096]{1,0:T(8,128)}, u32[]{:S(2)}, u32[]{:S(2)}) collective-permute-start(f32[512,4096]{1,0:T(8,128)} %collective-permute-done.13.refs_1_), channel_id=1, source_target_pairs={{0,1},{1,0},{2,3},{3,2},{4,5},{5,4},{6,7},{7,6}} | collective-permute-start | bytes 25165832 | tf_op jit(solution)/shard_map/ppermute | solution.py:577
  563.5 214.4 %collective-permute-start.8 = (f32[512,4096]{1,0:T(8,128)}, f32[512,4096]{1,0:T(8,128)}, u32[]{:S(2)}, u32[]{:S(2)}) collective-permute-start(f32[512,4096]{1,0:T(8,128)} %fusion.25), channel_id=1, source_target_pairs={{0,1},{1,0},{2,3},{3,2},{4,5},{5,4},{6,7},{7,6}} | collective-permute-start | bytes 25165832 | tf_op jit(solution)/shard_map/ppermute | solution.py:577
  641.0 131.6 %collective-permute-start.22 = (f32[2,4,512,256]{3,2,1,0:T(8,128)}, f32[2,4,512,256]{3,2,1,0:T(8,128)}, u32[]{:S(2)}, u32[]{:S(2)}) collective-permute-start(f32[2,4,512,256]{3,2,1,0:T(8,128)} %get-tuple-element.68), channel_id=1, source_target_pairs={{0,1},{1,0},{2,3},{3,2},{4,5},{5,4},{6,7},{7,6}} | collective-permute-start | bytes 12582920 | tf_op jit(solution)/shard_map/ppermute | solution.py:577
  716.4 91.5 %collective-permute-start.16 = (f32[2,4,512,256]{3,2,1,0:T(8,128)}, f32[2,4,512,256]{3,2,1,0:T(8,128)}, u32[]{:S(2)}, u32[]{:S(2)}) collective-permute-start(f32[2,4,512,256]{3,2,1,0:T(8,128)} %get-tuple-element.62), channel_id=1, source_target_pairs={{0,1},{1,0},{2,3},{3,2},{4,5},{5,4},{6,7},{7,6}} | collective-permute-start | bytes 12582920 | tf_op jit(solution)/shard_map/ppermute | solution.py:577
  740.2 249.2 %collective-permute-start.21 = (bf16[2304,2048]{1,0:T(8,128)(2,1)}, bf16[2304,2048]{1,0:T(8,128)(2,1)}, u32[]{:S(2)}, u32[]{:S(2)}) collective-permute-start(bf16[2304,2048]{1,0:T(8,128)(2,1)} %collective-permute-done.20.p0_ref.refs_10_), channel_id=1, source_target_pairs={{0,1},{1,0},{2,3},{3,2},{4,5},{5,4},{6,7},{7,6}} | collective-permute-start | bytes 28311560 | tf_op jit(solution)/shard_map/ppermute | solution.py:577
  740.2 248.6 %collective-permute-start.5 = (bf16[2048,1024]{1,0:T(8,128)(2,1)}, bf16[2048,1024]{1,0:T(8,128)(2,1)}, u32[]{:S(2)}, u32[]{:S(2)}) collective-permute-start(bf16[2048,1024]{1,0:T(8,128)(2,1)} %collective-permute-done.4.refs_7_), channel_id=1, source_target_pairs={{0,2},{1,3},{2,0},{3,1},{4,6},{5,7},{6,4},{7,5}} | collective-permute-start | bytes 12582920 | tf_op jit(solution)/shard_map/ppermute | solution.py:574
  772.6 217.4 %collective-permute-start.24 = (bf16[2048,2048]{1,0:T(8,128)(2,1)}, bf16[2048,2048]{1,0:T(8,128)(2,1)}, u32[]{:S(2)}, u32[]{:S(2)}) collective-permute-start(bf16[2048,2048]{1,0:T(8,128)(2,1)} %get-tuple-element.70), channel_id=1, source_target_pairs={{0,4},{4,0},{1,5},{5,1},{2,6},{6,2},{3,7},{7,3}} | collective-permute-start | bytes 25165832 | tf_op jit(solution)/shard_map/ppermute | solution.py:571
  777.9 130.7 %collective-permute-start.23 = (f32[4,512,256]{2,1,0:T(8,128)}, f32[4,512,256]{2,1,0:T(8,128)}, u32[]{:S(2)}, u32[]{:S(2)}) collective-permute-start(f32[4,512,256]{2,1,0:T(8,128)} %fusion.37), channel_id=1, source_target_pairs={{2,0},{3,1},{6,4},{7,5}} | collective-permute-start | bytes 6291464 | tf_op jit(solution)/shard_map/ppermute | solution.py:574
  807.9 181.5 %collective-permute-start.6 = (bf16[2048,1024]{1,0:T(8,128)(2,1)}, bf16[2048,1024]{1,0:T(8,128)(2,1)}, u32[]{:S(2)}, u32[]{:S(2)}) collective-permute-start(bf16[2048,1024]{1,0:T(8,128)(2,1)} %collective-permute-done.4.refs_7_), channel_id=1, source_target_pairs={{0,1},{1,0},{2,3},{3,2},{4,5},{5,4},{6,7},{7,6}} | collective-permute-start | bytes 12582920 | tf_op jit(solution)/shard_map/ppermute | solution.py:577
  988.9 183.6 %collective-permute-start.3 = (bf16[4096,1024]{1,0:T(8,128)(2,1)}, bf16[4096,1024]{1,0:T(8,128)(2,1)}, u32[]{:S(2)}, u32[]{:S(2)}) collective-permute-start(bf16[4096,1024]{1,0:T(8,128)(2,1)} %get-tuple-element.49.refs_3_), channel_id=1, source_target_pairs={{0,4},{4,0},{1,5},{5,1},{2,6},{6,2},{3,7},{7,3}} | collective-permute-start | bytes 25165832 | tf_op jit(solution)/shard_map/ppermute | solution.py:571
  989.4 183.1 %collective-permute-start.9 = (f32[512,4096]{1,0:T(8,128)}, f32[512,4096]{1,0:T(8,128)}, u32[]{:S(2)}, u32[]{:S(2)}) collective-permute-start(f32[512,4096]{1,0:T(8,128)} %convolution_add_fusion.1.refs_11_), channel_id=1, source_target_pairs={{0,2},{1,3},{2,0},{3,1},{4,6},{5,7},{6,4},{7,5}} | collective-permute-start | bytes 25165832 | tf_op jit(solution)/shard_map/ppermute | solution.py:574
  989.4 115.7 %collective-permute-start.36 = (f32[1024,2048]{1,0:T(8,128)}, f32[1024,2048]{1,0:T(8,128)}, u32[]{:S(2)}, u32[]{:S(2)}) collective-permute-start(f32[1024,2048]{1,0:T(8,128)} %fusion.4), channel_id=1, source_target_pairs={{0,1},{1,0},{2,3},{3,2},{4,5},{5,4},{6,7},{7,6}} | collective-permute-start | bytes 25165832 | tf_op jit(solution)/shard_map/ppermute | solution.py:577
  989.4 140.9 %collective-permute-start.32 = (f32[1024,2048]{1,0:T(8,128)}, f32[1024,2048]{1,0:T(8,128)}, u32[]{:S(2)}, u32[]{:S(2)}) collective-permute-start(f32[1024,2048]{1,0:T(8,128)} %fusion.8), channel_id=1, source_target_pairs={{0,1},{1,0},{2,3},{3,2},{4,5},{5,4},{6,7},{7,6}} | collective-permute-start | bytes 25165832 | tf_op jit(solution)/shard_map/ppermute | solution.py:577
  989.9 385.7 %collective-permute-start.18 = (bf16[2048,2048]{1,0:T(8,128)(2,1)}, bf16[2048,2048]{1,0:T(8,128)(2,1)}, u32[]{:S(2)}, u32[]{:S(2)}) collective-permute-start(bf16[2048,2048]{1,0:T(8,128)(2,1)} %get-tuple-element.64), channel_id=1, source_target_pairs={{0,4},{4,0},{1,5},{5,1},{2,6},{6,2},{3,7},{7,3}} | collective-permute-start | bytes 25165832 | tf_op jit(solution)/shard_map/ppermute | solution.py:571
  1130.4 244.3 %collective-permute-start.19 = (bf16[2048,256]{1,0:T(8,128)(2,1)S(1)}, bf16[2048,256]{1,0:T(8,128)(2,1)S(1)}, u32[]{:S(2)}, u32[]{:S(2)}) collective-permute-start(bf16[2048,256]{1,0:T(8,128)(2,1)S(1)} %copy-done.5), channel_id=1, source_target_pairs={{0,4},{4,0},{1,5},{5,1},{2,6},{6,2},{3,7},{7,3}} | collective-permute-start | bytes 3145736 | tf_op jit(solution)/shard_map/ppermute | solution.py:571
  1155.7 396.1 %collective-permute-start.2 = (bf16[4096,1024]{1,0:T(8,128)(2,1)}, bf16[4096,1024]{1,0:T(8,128)(2,1)}, u32[]{:S(2)}, u32[]{:S(2)}) collective-permute-start(bf16[4096,1024]{1,0:T(8,128)(2,1)} %get-tuple-element.45.refs_2_), channel_id=1, source_target_pairs={{0,4},{4,0},{1,5},{5,1},{2,6},{6,2},{3,7},{7,3}} | collective-permute-start | bytes 25165832 | tf_op jit(solution)/shard_map/ppermute | solution.py:571
  1172.5 403.7 %collective-permute-start.10 = (f32[512,4096]{1,0:T(8,128)}, f32[512,4096]{1,0:T(8,128)}, u32[]{:S(2)}, u32[]{:S(2)}) collective-permute-start(f32[512,4096]{1,0:T(8,128)} %convolution_add_fusion.1.refs_11_), channel_id=1, source_target_pairs={{0,1},{1,0},{2,3},{3,2},{4,5},{5,4},{6,7},{7,6}} | collective-permute-start | bytes 25165832 | tf_op jit(solution)/shard_map/ppermute | solution.py:577
  1172.5 404.1 %collective-permute-start.11 = (f32[512,4096]{1,0:T(8,128)}, f32[512,4096]{1,0:T(8,128)}, u32[]{:S(2)}, u32[]{:S(2)}) collective-permute-start(f32[512,4096]{1,0:T(8,128)} %collective-permute-done.9.refs_12_), channel_id=1, source_target_pairs={{0,1},{1,0},{2,3},{3,2},{4,5},{5,4},{6,7},{7,6}} | collective-permute-start | bytes 25165832 | tf_op jit(solution)/shard_map/ppermute | solution.py:577
  1375.6 361.0 %collective-permute-start.37 = (f32[1024,2048]{1,0:T(8,128)}, f32[1024,2048]{1,0:T(8,128)}, u32[]{:S(2)}, u32[]{:S(2)}) collective-permute-start(f32[1024,2048]{1,0:T(8,128)} %fusion.31.a_ref), channel_id=1, source_target_pairs={{0,2},{1,3},{2,0},{3,1},{4,6},{5,7},{6,4},{7,5}} | collective-permute-start | bytes 25165832 | tf_op jit(solution)/shard_map/ppermute | solution.py:574
  1375.7 361.0 %collective-permute-start.33 = (f32[1024,2048]{1,0:T(8,128)}, f32[1024,2048]{1,0:T(8,128)}, u32[]{:S(2)}, u32[]{:S(2)}) collective-permute-start(f32[1024,2048]{1,0:T(8,128)} %fusion.28.refs_1_), channel_id=1, source_target_pairs={{0,2},{1,3},{2,0},{3,1},{4,6},{5,7},{6,4},{7,5}} | collective-permute-start | bytes 25165832 | tf_op jit(solution)/shard_map/ppermute | solution.py:574
  1565.3 171.4 %collective-permute-start.27 = (f32[50,128]{1,0:T(8,128)S(1)}, f32[50,128]{1,0:T(8,128)}, u32[]{:S(2)}, u32[]{:S(2)}) collective-permute-start(f32[50,128]{1,0:T(8,128)S(1)} %bitcast_add_fusion), channel_id=1, source_target_pairs={{0,2},{1,3},{2,0},{3,1},{4,6},{5,7},{6,4},{7,5}} | collective-permute-start | bytes 76808 | tf_op jit(solution)/shard_map/ppermute | solution.py:574
  1576.2 320.2 %collective-permute-start.38 = (f32[1024,2048]{1,0:T(8,128)}, f32[1024,2048]{1,0:T(8,128)}, u32[]{:S(2)}, u32[]{:S(2)}) collective-permute-start(f32[1024,2048]{1,0:T(8,128)} %fusion.31.a_ref), channel_id=1, source_target_pairs={{0,1},{1,0},{2,3},{3,2},{4,5},{5,4},{6,7},{7,6}} | collective-permute-start | bytes 25165832 | tf_op jit(solution)/shard_map/ppermute | solution.py:577
  1576.6 338.6 %collective-permute-start.34 = (f32[1024,2048]{1,0:T(8,128)}, f32[1024,2048]{1,0:T(8,128)}, u32[]{:S(2)}, u32[]{:S(2)}) collective-permute-start(f32[1024,2048]{1,0:T(8,128)} %fusion.28.refs_1_), channel_id=1, source_target_pairs={{0,1},{1,0},{2,3},{3,2},{4,5},{5,4},{6,7},{7,6}} | collective-permute-start | bytes 25165832 | tf_op jit(solution)/shard_map/ppermute | solution.py:577
  1736.6 159.8 %collective-permute-start.29 = (f32[2048,256]{1,0:T(8,128)}, f32[2048,256]{1,0:T(8,128)}, u32[]{:S(2)}, u32[]{:S(2)}) collective-permute-start(f32[2048,256]{1,0:T(8,128)} %fusion.34.refs_1_), channel_id=1, source_target_pairs={{0,2},{1,3},{2,0},{3,1},{4,6},{5,7},{6,4},{7,5}} | collective-permute-start | bytes 6291464 | tf_op jit(solution)/shard_map/ppermute | solution.py:574
  1736.7 160.3 %collective-permute-start.39 = (f32[1024,2048]{1,0:T(8,128)}, f32[1024,2048]{1,0:T(8,128)}, u32[]{:S(2)}, u32[]{:S(2)}) collective-permute-start(f32[1024,2048]{1,0:T(8,128)} %collective-permute-done.37.b_ref), channel_id=1, source_target_pairs={{0,1},{1,0},{2,3},{3,2},{4,5},{5,4},{6,7},{7,6}} | collective-permute-start | bytes 25165832 | tf_op jit(solution)/shard_map/ppermute | solution.py:577
  1736.7 178.5 %collective-permute-start.35 = (f32[1024,2048]{1,0:T(8,128)}, f32[1024,2048]{1,0:T(8,128)}, u32[]{:S(2)}, u32[]{:S(2)}) collective-permute-start(f32[1024,2048]{1,0:T(8,128)} %collective-permute-done.33.refs_2_), channel_id=1, source_target_pairs={{0,1},{1,0},{2,3},{3,2},{4,5},{5,4},{6,7},{7,6}} | collective-permute-start | bytes 25165832 | tf_op jit(solution)/shard_map/ppermute | solution.py:577
  (16 other events, 476.4 us)

commit v2 on v1

--- a/solution.py
+++ b/solution.py
@@ -140,9 +140,9 @@
         (x, gain, w, bias, cos_t, sin_t))
 
 
-def q_kernel(h_ref, w_ref, b_ref, cos_ref, sin_ref, q_ref, qt_ref):
+def q_kernel(h_ref, w_ref, b_ref, cos_ref, sin_ref, qt_ref):
     nq = qt_ref.shape[0]
-    for n in range(q_ref.shape[1] // COLS):
+    for n in range(w_ref.shape[1] // COLS):
         c0 = n * COLS
         p = (mxu(h_ref[...], w_ref[:, c0:c0 + COLS]) + b_ref[:, c0:c0 + COLS]).astype(BF)
         for u in range(4):
@@ -152,12 +152,12 @@
                 tile = p[ts, hs].T
                 top = tile[:ROT].astype(F32)
                 turned = (top * cos_ref[:, ts] + swap_pairs(top) * sin_ref[:, ts]).astype(BF)
-                tile = jnp.concatenate([turned, tile[ROT:]], axis=0)
-                qt_ref[t, :, (c0 // HEAD + u) * TQ:(c0 // HEAD + u + 1) * TQ] = tile
-                q_ref[ts, c0 + u * HEAD:c0 + (u + 1) * HEAD] = tile.T
-
-
-def q_turn_kernel(s_ref, h_ref, w_ref, b_ref, cos_ref, sin_ref, rows_ref, q_ref, qt_ref, t_ref, half_ref):
+                sl = tok_slice(c0 // HEAD + u)
+                qt_ref[t, :ROT, sl] = turned
+                qt_ref[t, ROT:, sl] = tile[ROT:]
+
+
+def q_turn_kernel(s_ref, h_ref, w_ref, b_ref, cos_ref, sin_ref, rows_ref, qt_ref, t_ref, half_ref):
     t = rows_ref[...].T
     t_ref[...] = t
 
@@ -165,7 +165,7 @@
     def _():
         half_ref[...] = t
 
-    q_kernel(h_ref, w_ref, b_ref, cos_ref, sin_ref, q_ref, qt_ref)
+    q_kernel(h_ref, w_ref, b_ref, cos_ref, sin_ref, qt_ref)
 
 
 def q_project(half, part, parts, whole, h, w, bias, cos_t, sin_t, qw, table=None):
@@ -178,8 +178,8 @@
     i0 = part * steps
     tab = cols_of(ROT, rows, i0)
     in_specs = [rows_of(rows, d, i0), once((d, width), half), once((1, width), half), tab, tab]
-    out_specs = [rows_of(rows, width, i0), pl.BlockSpec((nq, HEAD, cols), lambda i, *_: (i + i0, 0, 0))]
-    out_shape = [shape((tokens, width), BF), shape((tokens // TQ, HEAD, cols), BF)]
+    out_specs = [pl.BlockSpec((nq, HEAD, cols), lambda i, *_: (i + i0, 0, 0))]
+    out_shape = [shape((tokens // TQ, HEAD, cols), BF)]
     args = [h, w, bias, cos_t, sin_t]
     body, alias = with_whole(q_kernel, len(args), args, in_specs, whole)
     if table is not None:
@@ -193,9 +193,21 @@
     return kernel_call(body, 42 // parts, (steps,), in_specs, out_specs, out_shape, args, alias=alias, prefetch=int(table is not None))
 
 
-def key_bias(start_ref, q0, k0):
-    j = k0 + lax.broadcasted_iota(jnp.int32, (TK, TQ), 0)
-    i = q0 + lax.broadcasted_iota(jnp.int32, (TK, TQ), 1)
+def for_keys(lo, hi, step):
+    def pair(i, _):
+        step(pl.multiple_of((lo + 2 * i) * TK, TK), 2 * TK)
+        return 0
+
+    lax.fori_loop(0, (hi - lo) // 2, pair, 0)
+
+    @pl.when((hi - lo) % 2 == 1)
+    def _():
+        step(pl.multiple_of((hi - 1) * TK, TK), TK)
+
+
+def key_bias(start_ref, q0, k0, n):
+    j = k0 + lax.broadcasted_iota(jnp.int32, (n, TQ), 0)
+    i = q0 + lax.broadcasted_iota(jnp.int32, (n, TQ), 1)
     return jnp.where((j >= start_ref[0]) & (j <= i), 0.0, NEG).astype(F32)
 
 
@@ -233,31 +245,29 @@
     acc_s[...] = jnp.zeros_like(acc_s)
     q0, lo, hi = key_range(s_ref, b, t, nq)
 
-    def scores(kb, _):
-        rows = pl.ds(pl.multiple_of(kb * TK, TK), TK)
-        bias = key_bias(start_ref, q0, kb * TK)
+    def scores(k0, n):
+        rows = pl.ds(k0, n)
+        bias = key_bias(start_ref, q0, k0, n)
         k = k_s[rows, :]
         for h in range(heads):
             sl = tok_slice(h)
             s = mxu(k, qt_ref[0, :, sl]) * SCALE2 + bias
             t_s[rows, sl] = s
-            m8_s[:, sl] = jnp.maximum(m8_s[:, sl], jnp.max(s.reshape(TK // 8, 8, TQ), axis=0))
-        return 0
-
-    lax.fori_loop(lo, hi, scores, 0)
+            m8_s[:, sl] = jnp.maximum(m8_s[:, sl], jnp.max(s.reshape(n // 8, 8, TQ), axis=0))
+
+    for_keys(lo, hi, scores)
     m_s[...] = jnp.max(m8_s[...], axis=0, keepdims=True)
 
-    def accumulate(kb, _):
-        rows = pl.ds(pl.multiple_of(kb * TK, TK), TK)
+    def accumulate(k0, n):
+        rows = pl.ds(k0, n)
         for h in range(heads):
             sl = tok_slice(h)
             e = jnp.exp2(t_s[rows, sl] - m_s[:, sl])
-            l8_s[:, sl] += jnp.sum(e.reshape(TK // 8, 8, TQ), axis=0)
-            e_s[:, sl] = e.astype(BF)
-        acc_s[...] += mxu(vt_s[:, rows], e_s[...])
-        return 0
-
-    lax.fori_loop(lo, hi, accumulate, 0)
+            l8_s[:, sl] += jnp.sum(e.reshape(n // 8, 8, TQ), axis=0)
+            e_s[:n, sl] = e.astype(BF)
+        acc_s[...] += mxu(vt_s[:, rows], e_s[:n, :])
+
+    for_keys(lo, hi, accumulate)
     l = jnp.sum(l8_s[...], axis=0, keepdims=True)
     lse_ref[0] = m_s[...] + jnp.log2(l)
     l8_s[0:1, :] = 1.0 / l
@@ -281,17 +291,17 @@
         [tiles_of((TQ, width), nq), tile, tiles_of((1, 1, cols), nq)],
         [shape((n * TQ, width), BF), shape((n, HEAD, cols), BF), shape((n, 1, cols), F32)], (table, start, qt, kva, kvb),
         [pltpu.VMEM((keys, HEAD), BF), pltpu.VMEM((HEAD, keys), BF), pltpu.VMEM((keys, cols), F32), pltpu.VMEM((HEAD, cols), F32),
-         pltpu.VMEM((1, cols), F32), pltpu.VMEM((8, cols), F32), pltpu.VMEM((8, cols), F32), pltpu.VMEM((TK, cols), BF)],
+         pltpu.VMEM((1, cols), F32), pltpu.VMEM((8, cols), F32), pltpu.VMEM((8, cols), F32), pltpu.VMEM((2 * TK, cols), BF)],
         prefetch=1)
 
 
-def bwd_kernel(b0, riding, s_ref, start_ref, qta_ref, qtb_ref, qa_ref, qb_ref, dcta_ref, dctb_ref, cta_ref, ctb_ref, la_ref, lb_ref,
+def bwd_kernel(b0, riding, s_ref, start_ref, qta_ref, qtb_ref, dcta_ref, dctb_ref, cta_ref, ctb_ref, la_ref, lb_ref,
                cos_ref, sin_ref, kva_ref, kvb_ref, *refs):
     nb, nq = pl.num_programs(0), pl.num_programs(1)
     if riding:
         put_sums(pl.program_id(0) * nq + pl.program_id(1), nb * nq, refs[:riding], refs[riding + 5])
     dq_ref, half_ref, dkv0_ref, dkv1_ref, dkvb_ref = refs[riding:riding + 5]
-    kv_s, kt_s, dct_s, qd_s, dqt_s, delta_s, pd_s, dkv_s = refs[-8:]
+    kv_s, kt_s, dct_s, dqt_s, delta_s, ds_s, dsn_s, pn_s, dkvt_s = refs[-9:]
     b, t = pl.program_id(0) + b0, pl.program_id(1)
     heads = dq_ref.shape[1] // HEAD
     chunk = kva_ref.shape[2]
@@ -302,7 +312,7 @@
             rows = pl.ds(pl.multiple_of((s_ref[0] ^ flip) * chunk, chunk), chunk)
             kv_s[rows, :] = ref[i, 0]
             kt_s[:, rows] = ref[i, 0, :, :HEAD].T
-        dkv_s[...] = jnp.zeros_like(dkv_s)
+        dkvt_s[...] = jnp.zeros_like(dkvt_s)
 
     def of_head(h, a_ref, b_ref):
         return (a_ref, h) if h < heads // 2 else (b_ref, h - heads // 2)
@@ -312,17 +322,15 @@
         ref, u = of_head(h, dcta_ref, dctb_ref)
         dct = ref[head_slice(u), :]
         dct_s[:, sl] = dct
-        ref, u = of_head(h, qa_ref, qb_ref)
-        qd_s[sl, :HEAD] = ref[:, head_slice(u)]
-        qd_s[sl, HEAD:] = dct.T
         ref, u = of_head(h, cta_ref, ctb_ref)
         delta_s[:, sl] = jnp.sum(dct.astype(F32) * ref[0, :, tok_slice(u)].astype(F32), axis=0, keepdims=True)
     dqt_s[...] = jnp.zeros_like(dqt_s)
     q0, lo, hi = key_range(s_ref, b, t, nq)
 
     def step(kb, _):
-        rows = pl.ds(pl.multiple_of(kb * TK, TK), TK)
-        bias = key_bias(start_ref, q0, kb * TK)
+        k0 = pl.multiple_of(kb * TK, TK)
+        rows = pl.ds(k0, TK)
+        bias = key_bias(start_ref, q0, k0, TK)
         k = kv_s[rows, :HEAD]
         v = kv_s[rows, HEAD:]
         for h in range(heads):
@@ -331,12 +339,14 @@
             lse, _ = of_head(h, la_ref, lb_ref)
             us = tok_slice(u)
             p = jnp.exp2(mxu(k, qt[0, :, us]) * SCALE2 + bias - lse[0, :, us])
-            pd_s[TK:, sl] = p.astype(BF)
-            pd_s[:TK, sl] = (p * (mxu(v, dct_s[:, sl]) - delta_s[:, sl])).astype(BF)
-        dqt_s[...] += mxu(kt_s[:, rows], pd_s[:TK, :])
-        both = mxu(pd_s[...], qd_s[...])
-        dkv_s[rows, :HEAD] += both[:TK, :HEAD]
-        dkv_s[rows, HEAD:] += both[TK:, HEAD:]
+            ds = (p * (mxu(v, dct_s[:, sl]) - delta_s[:, sl])).astype(BF)
+            pn_s[sl, :] = p.astype(BF).T
+            dsn_s[sl, :] = ds.T
+            ds_s[:, sl] = ds
+        dqt_s[...] += mxu(kt_s[:, rows], ds_s[...])
+        half = dsn_s.shape[0] // 2
+        dkvt_s[:HEAD, rows] += mxu(qta_ref[0], dsn_s[:half, :]) + mxu(qtb_ref[0], dsn_s[half:, :])
+        dkvt_s[HEAD:, rows] += mxu(dct_s[...], pn_s[...])
         return 0
 
     lax.fori_loop(lo, hi, step, 0)
@@ -352,11 +362,11 @@
     def _():
         for ref, flip in ((dkv0_ref.at[0], 0), (dkv1_ref.at[0], 2), (dkvb_ref.at[0, 0], 1), (dkvb_ref.at[1, 0], 3)):
             rows = pl.ds(pl.multiple_of((s_ref[0] ^ flip) * chunk, chunk), chunk)
-            ref[:, :HEAD] = dkv_s[rows, :HEAD] * SCALE
-            ref[:, HEAD:] = dkv_s[rows, HEAD:]
-
-
-def attn_bwd(half, whole, sums, table, start, qts, qs, dcts, cts, lses, cos_t, sin_t, kva, kvb):
+            ref[:, :HEAD] = (dkvt_s[:HEAD, rows] * SCALE).T
+            ref[:, HEAD:] = dkvt_s[HEAD:, rows].T
+
+
+def attn_bwd(half, whole, sums, table, start, qts, dcts, cts, lses, cos_t, sin_t, kva, kvb):
     batch, _, chunk = start.shape
     nq = chunk // TQ
     n, _, cols = qts[0].shape
@@ -365,11 +375,11 @@
     nb = batch // 2
     b0 = half * nb
     kv, tile, line = kv_spec(chunk, b0), tiles_of((1, HEAD, cols), nq, b0), tiles_of((1, 1, cols), nq, b0)
-    qrow, dct, tab = tiles_of((TQ, width // 2), nq, b0), tile_cols(width // 2, nq, b0), tile_cols(ROT, nq, b0)
+    dct, tab = tile_cols(width // 2, nq, b0), tile_cols(ROT, nq, b0)
     one = shape((nb, chunk, 2 * HEAD), F32)
     one_spec = pl.BlockSpec((1, chunk, 2 * HEAD), lambda b, *_: (b, 0, 0))
-    in_specs = [start_spec(b0), tile, tile, qrow, qrow, dct, dct, tile, tile, line, line, tab, tab, kv, kv]
-    args = [table, start, *qts, *qs, *dcts, *cts, *lses, cos_t, sin_t, kva, kvb]
+    in_specs = [start_spec(b0), tile, tile, dct, dct, tile, tile, line, line, tab, tab, kv, kv]
+    args = [table, start, *qts, *dcts, *cts, *lses, cos_t, sin_t, kva, kvb]
     out_specs = [tiles_of((TQ, width), nq, b0), tiles_of((TQ, width), nq), one_spec, one_spec, kv_spec(chunk)]
     out_shape = [shape((n * TQ, width), BF), shape((n * TQ // 2, width), BF), one, one, shape((2, nb, chunk, 2 * HEAD), F32)]
     if sums:
@@ -381,8 +391,9 @@
     body, alias = with_whole(functools.partial(bwd_kernel, b0, len(sums)), len(args), args, in_specs, whole)
     return kernel_call(
         body, 80, (nb, nq), in_specs, out_specs, out_shape, args,
-        [pltpu.VMEM((keys, 2 * HEAD), BF), pltpu.VMEM((HEAD, keys), BF), pltpu.VMEM((HEAD, 2 * cols), BF), pltpu.VMEM((2 * cols, 2 * HEAD), BF),
-         pltpu.VMEM((HEAD, 2 * cols), F32), pltpu.VMEM((1, 2 * cols), F32), pltpu.VMEM((2 * TK, 2 * cols), BF), pltpu.VMEM((keys, 2 * HEAD), F32)],
+        [pltpu.VMEM((keys, 2 * HEAD), BF), pltpu.VMEM((HEAD, keys), BF), pltpu.VMEM((HEAD, 2 * cols), BF),
+         pltpu.VMEM((HEAD, 2 * cols), F32), pltpu.VMEM((1, 2 * cols), F32), pltpu.VMEM((TK, 2 * cols), BF),
+         pltpu.VMEM((2 * cols, TK), BF), pltpu.VMEM((2 * cols, TK), BF), pltpu.VMEM((2 * HEAD, keys), F32)],
         prefetch=1, alias=alias)
 
 
@@ -604,14 +615,14 @@
         kva = jnp.stack([kv_own, send_x(kv_own, over_x[:2])])
         kvb = send_core(kva)
         q_args = (h, w_qkv, bias, cos_t, sin_t, qw)
-        qa, qta, wq_t, wq_half = q_project(0, 0, 1, None, *q_args, table=me)
+        qta, wq_t, wq_half = q_project(0, 0, 1, None, *q_args, table=me)
         wq0 = send_tp(wq_half)
         wo1 = send_x(wo0)
         wo_pieces = (wo0, wo1, send_core(wo0), send_core(wo1))
         wq_pieces = (wq0, send_core(wq0))
 
         ctx_a, ct_a, lse_a = attn_fwd(table, start, qta, kva, kvb)
-        qb, qtb = q_project(1, 1, 2, q_project(1, 0, 2, None, *q_args), *q_args)
+        qtb, = q_project(1, 1, 2, q_project(1, 0, 2, None, *q_args), *q_args)
         ctx_b, ct_b, lse_b = attn_fwd(table, start, qtb, kva, kvb)
         peer_ctx = (send_tp(ctx_a), send_tp(ctx_b))
 
@@ -635,7 +646,7 @@
 
         dctx_t = (grad_ctx(w_out[:qw // 2]), grad_ctx(w_out[qw // 2:]))
 
-        attn_args = (table, start, (qta, qtb), (qa, qb), dctx_t, (ct_a, ct_b), (lse_a, lse_b), cos_t, sin_t, kva, kvb)
+        attn_args = (table, start, (qta, qtb), dctx_t, (ct_a, ct_b), (lse_a, lse_b), cos_t, sin_t, kva, kvb)
 
         def own_dkv(half, own, away, others):
             got = send_core(others)

time: 1950 us -> 1900 us (0.974)
  starting transfers between devices: 148 us -> 122 us
    ppermute x22, starting transfers between devices: 87.7 us -> 67.9 us  [send_core(): return lax.ppermute(v, 'cp', over_core)]
where the time goes in v2:
time: 1900 us
  Pallas kernels  738 us (39%)
  waiting for transfers between devices  695 us (37%)
  matrix products  310 us (16%)
  starting transfers between devices  122 us (6%)
  other arithmetic  21.6 us (1%)
    pallas_call x16, Pallas kernels, kernel_call(): pl.pallas_call(body, grid_spec=pltpu.PrefetchScalarGridSpec(num_scalar_pr...  738 us
    ppermute x10, waiting for transfers between devices, send_x(): return lax.ppermute(v, 'cp', pairs)  416 us
    ppermute x8, waiting for transfers between devices, send_tp(): return lax.ppermute(v, 'tp', over_tp)  276 us
    dot_general x10, matrix products, part(): lax.dot_general(cols, rhs, (((0,), (0,)), ((), ())), preferred_element_ty...  224 us
    dot_general x2, matrix products, grad_ctx(): lax.dot_general(w, g, (((1,), (1,)), ((), ())), preferred_element_type=F32)  85.8 us
    ppermute x22, starting transfers between devices, send_core(): return lax.ppermute(v, 'cp', over_core)  67.9 us
    ppermute x10, starting transfers between devices, send_x(): return lax.ppermute(v, 'cp', pairs)  45.3 us
  transfers between devices with their start and end apart: 40, of which 9 were waited for; matrix products, arithmetic and copies ran while one was open for 16% of the time, Pallas kernels for 35%

profile of v2, /device:TPU:0, one launch (start us, length us, event | category | flops | bytes accessed | tf_op | source)
XLA Modules:
  0.0 1897.7 jit_solution(16730986889580359879)
XLA Ops:
  9.7 33.1 %shard_map.118 = (bf16[4096,4096]{1,0:T(8,128)(2,1)}, f32[4096,1]{1,0:T(8,128)}, bf16[4096,256]{1,0:T(8,128)(2,1)}) custom-call(bf16[4096,4096]{1,0:T(8,128)(2,1)} %bitcast.54, f32[1,4096]{1,0:T(1,128)} %bitcast.43, bf16[4096,2304]{1,0:T(8,128)(2,1)} %refs_1_.1, f32[1,2304]{1,0:T(1,128)} %reshape.74.b_ref.refs_2_, ...), custom_call_target="tpu_custom_call" | custom-call | flops 27888001024 | bytes 28000000 | tf_op jit(solution)/shard_map/pallas_call | solution.py:38
  48.4 44.9 %collective-permute-done = bf16[8,512,256]{2,1,0:T(8,128)(2,1)S(1)} collective-permute-done((bf16[8,512,256]{2,1,0:T(8,128)(2,1)}, bf16[8,512,256]{2,1,0:T(8,128)(2,1)S(1)}, u32[]{:S(2)}, u32[]{:S(2)}) %collective-permute-start) | collective-permute-done | bytes 2097184 | tf_op jit(solution)/shard_map/ppermute | solution.py:585
  98.8 50.5 %shard_map.119 = (bf16[16,128,2048]{2,1,0:T(8,128)(2,1)}, bf16[2304,4096]{1,0:T(8,128)(2,1)}, bf16[2304,2048]{1,0:T(8,128)(2,1)}) custom-call(s32[1]{0:T(128)} %bitcast.s_ref.refs_0_, bf16[4096,4096]{1,0:T(8,128)(2,1)} %get-tuple-element.37.h_ref.refs_0_, bf16[4096,2304]{1,0:T(8,128)(2,1)} %refs_1_.1, f32[1,2304]{1,0:T(1,128)} %reshape.74.b_ref.refs_2_, ...), custom_call_target="tpu_custom_call" | custom-call | flops 41832001536 | bytes 42000000 | tf_op jit(solution)/shard_map/pallas_call | solution.py:38
  149.3 32.3 %shard_map.120 = (bf16[4096,1024]{1,0:T(8,128)(2,1)}, bf16[16,128,2048]{2,1,0:T(8,128)(2,1)}, f32[16,1,2048]{2,1,0:T(1,128)}) custom-call(s32[17]{0:T(128)} %pad_add_fusion.s_ref.refs_0_, s32[8,1,512]{2,1,0:T(1,128)} %broadcast_in_dim.22.start_ref.refs_1_, bf16[16,128,2048]{2,1,0:T(8,128)(2,1)} %get-tuple-element.38.qt_ref.qta_ref.refs_2_, ...), custom_call_target="tpu_custom_call" | custom-call | flops 64739999744 | bytes 65000000 | tf_op jit(solution)/shard_map/pallas_call | solution.py:38
  181.6 24.1 %fusion.22 = f32[512,4096]{1,0:T(8,128)} fusion(bf16[4096,4096]{1,0:T(8,128)(2,1)} %bitcast.46, bf16[4096,1024]{1,0:T(8,128)(2,1)} %get-tuple-element.40.refs_2_, s32[]{:T(128)S(6)} %select_n.55), kind=kOutput, calls=%fused_computation.21 | convolution fusion | flops 17179869184 | bytes 46137348 | tf_op jit(solution)/shard_map/dot_general | solution.py:631
  227.8 24.8 %shard_map.121.refs_5_ = bf16[16,128,2048]{2,1,0:T(8,128)(2,1)} custom-call(bf16[4096,4096]{1,0:T(8,128)(2,1)} %get-tuple-element.37.h_ref.refs_0_, bf16[4096,2304]{1,0:T(8,128)(2,1)} %refs_1_.1, f32[1,2304]{1,0:T(1,128)} %reshape.74.b_ref.refs_2_, f32[64,4096]{1,0:T(8,128)} %get-tuple-element.69.cos_ref.refs_3_.refs_10_, ...), custom_call_target="tpu_custom_call" | custom-call | flops 20916000768 | bytes 21000000 | tf_op jit(solution)/shard_map/pallas_call | solution.py:38
  252.6 24.6 %shard_map.122.qt_ref.qtb_ref.refs_3_ = bf16[16,128,2048]{2,1,0:T(8,128)(2,1)} custom-call(bf16[4096,4096]{1,0:T(8,128)(2,1)} %get-tuple-element.37.h_ref.refs_0_, bf16[4096,2304]{1,0:T(8,128)(2,1)} %refs_1_.1, f32[1,2304]{1,0:T(1,128)} %reshape.74.b_ref.refs_2_, ...), custom_call_target="tpu_custom_call", output_to_operand_aliasing={{}: (5, {})} | custom-call | flops 20916000768 | bytes 21000000 | tf_op jit(solution)/shard_map/pallas_call | solution.py:38
  277.2 28.5 %convolution_add_fusion.refs_0_ = f32[512,4096]{1,0:T(8,128)} fusion(f32[512,4096]{1,0:T(8,128)} %collective-permute-done.12, bf16[4096,4096]{1,0:T(8,128)(2,1)} %bitcast.47, bf16[4096,1024]{1,0:T(8,128)(2,1)} %get-tuple-element.40.refs_2_, s32[]{:T(128)S(6)} %select_n.54), kind=kOutput, calls=%fused_computation.18 | convolution fusion | flops 17181966336 | bytes 54525956 | tf_op jit(solution)/shard_map/dot_general | solution.py:631
  313.2 43.2 %fusion.16.dcta_ref.refs_4_ = bf16[1024,4096]{1,0:T(8,128)(2,1)} fusion(bf16[4096,4096]{1,0:T(8,128)(2,1)} %bitcast.48, bf16[2048,4096]{1,0:T(8,128)(2,1)} %refs_6_.1), kind=kOutput, calls=%fused_computation.16 | convolution fusion | flops 34363932672 | bytes 50331648 | tf_op jit(solution)/shard_map/dot_general | solution.py:645
  356.4 42.7 %fusion.19.dctb_ref.refs_5_ = bf16[1024,4096]{1,0:T(8,128)(2,1)} fusion(bf16[4096,4096]{1,0:T(8,128)(2,1)} %bitcast.49, bf16[2048,4096]{1,0:T(8,128)(2,1)} %refs_6_.1), kind=kOutput, calls=%fused_computation.17 | convolution fusion | flops 34363932672 | bytes 50331648 | tf_op jit(solution)/shard_map/dot_general | solution.py:645
  399.1 95.2 %collective-permute-done.13.refs_1_ = f32[512,4096]{1,0:T(8,128)} collective-permute-done((f32[512,4096]{1,0:T(8,128)}, f32[512,4096]{1,0:T(8,128)}, u32[]{:S(2)}, u32[]{:S(2)}) %collective-permute-start.13) | collective-permute-done | bytes 8388640 | tf_op jit(solution)/shard_map/ppermute | solution.py:585
  494.3 32.2 %shard_map.123 = (bf16[4096,1024]{1,0:T(8,128)(2,1)}, bf16[16,128,2048]{2,1,0:T(8,128)(2,1)}, f32[16,1,2048]{2,1,0:T(1,128)}) custom-call(s32[17]{0:T(128)} %pad_add_fusion.s_ref.refs_0_, s32[8,1,512]{2,1,0:T(1,128)} %broadcast_in_dim.22.start_ref.refs_1_, bf16[16,128,2048]{2,1,0:T(8,128)(2,1)} %shard_map.122.qt_ref.qtb_ref.refs_3_, ...), custom_call_target="tpu_custom_call" | custom-call | flops 64739999744 | bytes 65000000 | tf_op jit(solution)/shard_map/pallas_call | solution.py:38
  526.5 24.3 %fusion.25 = f32[512,4096]{1,0:T(8,128)} fusion(bf16[4096,4096]{1,0:T(8,128)(2,1)} %bitcast.50, bf16[4096,1024]{1,0:T(8,128)(2,1)} %get-tuple-element.41.refs_3_, s32[]{:T(128)S(6)} %select_n.55), kind=kOutput, calls=%fused_computation.24 | convolution fusion | flops 17179869184 | bytes 46137348 | tf_op jit(solution)/shard_map/dot_general | solution.py:631
  566.3 57.1 %shard_map.124 = (bf16[4096,2048]{1,0:T(8,128)(2,1)}, bf16[2048,2048]{1,0:T(8,128)(2,1)}, f32[4,512,256]{2,1,0:T(8,128)}, f32[4,512,256]{2,1,0:T(8,128)}, f32[2,...) custom-call(s32[17]{0:T(128)} %pad_add_fusion.s_ref.refs_0_, s32[8,1,512]{2,1,0:T(1,128)} %broadcast_in_dim.22.start_ref.refs_1_, ...), custom_call_target="tpu_custom_call" | custom-call | flops 79679995904 | bytes 80000000 | tf_op jit(solution)/shard_map/pallas_call | solution.py:38
  637.5 43.6 %shard_map.126 = (bf16[4096,2048]{1,0:T(8,128)(2,1)}, bf16[2048,2048]{1,0:T(8,128)(2,1)}, f32[4,512,256]{2,1,0:T(8,128)}, f32[4,512,256]{2,1,0:T(8,128)}, f32[2,4,512,256]{3,2,1,0:T(8,128)}) custom-call(s32[17]{0:T(128)} %pad_add_fusion.s_ref.refs_0_, s32[8,1,512]{2,1,0:T(1,128)} %broadcast_in_dim.22.start_ref.refs_1_, ...), custom_call_target="tpu_custom_call", output_to_operand_aliasing={{0}: (14, {})} | custom-call | flops 79679995904 | bytes 80000000 | tf_op jit(solution)/shard_map/pallas_call | solution.py:38
  681.2 19.8 %collective-permute-start.16 = (f32[2,4,512,256]{3,2,1,0:T(8,128)}, f32[2,4,512,256]{3,2,1,0:T(8,128)}, u32[]{:S(2)}, u32[]{:S(2)}) collective-permute-start(f32[2,4,512,256]{3,2,1,0:T(8,128)} %get-tuple-element.52), channel_id=1, source_target_pairs={{0,1},{1,0},{2,3},{3,2},{4,5},{5,4},{6,7},{7,6}} | collective-permute-start | bytes 12582920 | tf_op jit(solution)/shard_map/ppermute | solution.py:588
  701.0 27.4 %collective-permute-start.5 = (bf16[2048,1024]{1,0:T(8,128)(2,1)}, bf16[2048,1024]{1,0:T(8,128)(2,1)}, u32[]{:S(2)}, u32[]{:S(2)}) collective-permute-start(bf16[2048,1024]{1,0:T(8,128)(2,1)} %collective-permute-done.4.refs_7_), channel_id=1, source_target_pairs={{0,2},{1,3},{2,0},{3,1},{4,6},{5,7},{6,4},{7,5}} | collective-permute-start | bytes 12582920 | tf_op jit(solution)/shard_map/ppermute | solution.py:585
  735.2 28.5 %convolution_add_fusion.1.refs_11_ = f32[512,4096]{1,0:T(8,128)} fusion(f32[512,4096]{1,0:T(8,128)} %collective-permute-done.8, bf16[4096,4096]{1,0:T(8,128)(2,1)} %bitcast.51, bf16[4096,1024]{1,0:T(8,128)(2,1)} %get-tuple-element.41.refs_3_, s32[]{:T(128)S(6)} %select_n.54), kind=kOutput, calls=%fused_computation.19 | convolution fusion | flops 17181966336 | bytes 54525956 | tf_op jit(solution)/shard_map/dot_general | solution.py:631
  767.0 97.5 %collective-permute-done.23.c_ref = f32[4,512,256]{2,1,0:T(8,128)} collective-permute-done((f32[4,512,256]{2,1,0:T(8,128)}, f32[4,512,256]{2,1,0:T(8,128)}, u32[]{:S(2)}, u32[]{:S(2)}) %collective-permute-start.23) | collective-permute-done | bytes 2097184 | tf_op jit(solution)/shard_map/ppermute | solution.py:585
  865.7 24.3 %fusion.4 = f32[1024,2048]{1,0:T(8,128)} fusion(bf16[4096,2048]{1,0:T(8,128)(2,1)} %get-tuple-element.50.qa_ref.refs_5_, bf16[4096,4096]{1,0:T(8,128)(2,1)} %get-tuple-element.37.h_ref.refs_0_, s32[]{:T(128)S(6)} %select_n.57), kind=kOutput, calls=%fused_computation.4 | convolution fusion | flops 17179869184 | bytes 33554436 | tf_op jit(solution)/shard_map/dot_general | solution.py:631
  895.4 18.2 collective-permute-done.17.c_ref
  915.2 24.2 %fusion.8 = f32[1024,2048]{1,0:T(8,128)} fusion(bf16[4096,2048]{1,0:T(8,128)(2,1)} %get-tuple-element.50.qa_ref.refs_5_, bf16[4096,4096]{1,0:T(8,128)(2,1)} %get-tuple-element.37.h_ref.refs_0_, s32[]{:T(128)S(6)} %select_n.59), kind=kOutput, calls=%fused_computation.8 | convolution fusion | flops 17179869184 | bytes 33554436 | tf_op jit(solution)/shard_map/dot_general | solution.py:631
  947.3 113.6 %shard_map.129 = (bf16[4096,4096]{1,0:T(8,128)(2,1)}, f32[1,4096]{1,0:T(1,128)}, f32[1,2304]{1,0:T(1,128)}) custom-call(s32[1]{0:T(128)} %bitcast.s_ref.refs_0_, bf16[4096,4096]{1,0:T(8,128)(2,1)} %bitcast.55, bf16[4096,4096]{1,0:T(8,128)(2,1)} %bitcast.52, f32[4096,1]{1,0:T(8,128)} %get-tuple-element.48.r_ref.refs_3_, f32[1,4096]{1,0:T(1,128)} %bitcast.44, ...), custom_call_target="tpu_custom_call" | custom-call | flops 99599998976 | bytes 100000000 | tf_op jit(solution)/shard_map/pallas_call | solution.py:38
  1060.9 25.4 %fusion.31.a_ref = f32[1024,2048]{1,0:T(8,128)} fusion(f32[1024,2048]{1,0:T(8,128)} %collective-permute-done.36, bf16[4096,2048]{1,0:T(8,128)(2,1)} %get-tuple-element.50.qa_ref.refs_5_, bf16[4096,4096]{1,0:T(8,128)(2,1)} %get-tuple-element.37.h_ref.refs_0_, s32[]{:T(128)S(6)} %select_n.56), kind=kOutput, calls=%fused_computation.28 | convolution fusion | flops 17181966336 | bytes 41943044 | tf_op jit(solution)/shard_map/dot_general | solution.py:631
  1086.8 24.8 %fusion.28.refs_1_ = f32[1024,2048]{1,0:T(8,128)} fusion(f32[1024,2048]{1,0:T(8,128)} %collective-permute-done.32, bf16[4096,2048]{1,0:T(8,128)(2,1)} %get-tuple-element.50.qa_ref.refs_5_, bf16[4096,4096]{1,0:T(8,128)(2,1)} %get-tuple-element.37.h_ref.refs_0_, s32[]{:T(128)S(6)} %select_n.58), kind=kOutput, calls=%fused_computation.27 | convolution fusion | flops 17181966336 | bytes 41943044 | tf_op jit(solution)/shard_map/dot_general | solution.py:631
  1128.9 201.6 %collective-permute-done.19.refs_8_ = bf16[2048,256]{1,0:T(8,128)(2,1)S(1)} collective-permute-done((bf16[2048,256]{1,0:T(8,128)(2,1)S(1)}, bf16[2048,256]{1,0:T(8,128)(2,1)S(1)}, u32[]{:S(2)}, u32[]{:S(2)}) %collective-permute-start.19) | collective-permute-done | bytes 1048608 | tf_op jit(solution)/shard_map/ppermute | solution.py:582
  1333.6 113.6 %shard_map.130 = (bf16[4096,4096]{1,0:T(8,128)(2,1)}, f32[1,4096]{1,0:T(1,128)}, f32[1,2304]{1,0:T(1,128)}) custom-call(s32[1]{0:T(128)} %bitcast.s_ref.refs_0_, bf16[4096,4096]{1,0:T(8,128)(2,1)} %bitcast.56, bf16[4096,4096]{1,0:T(8,128)(2,1)} %bitcast.53, f32[4096,1]{1,0:T(8,128)} %get-tuple-element.48.r_ref.refs_3_, ...), custom_call_target="tpu_custom_call", output_to_operand_aliasing={{0}: (12, {})} | custom-call | flops 99599998976 | bytes 100000000 | tf_op jit(solution)/shard_map/pallas_call | solution.py:38
  1448.7 59.0 %collective-permute-done.2.refs_4_ = bf16[4096,1024]{1,0:T(8,128)(2,1)} collective-permute-done((bf16[4096,1024]{1,0:T(8,128)(2,1)}, bf16[4096,1024]{1,0:T(8,128)(2,1)}, u32[]{:S(2)}, u32[]{:S(2)}) %collective-permute-start.2) | collective-permute-done | bytes 8388640 | tf_op jit(solution)/shard_map/ppermute | solution.py:582
  1532.6 159.9 %collective-permute-done.27 = f32[50,128]{1,0:T(8,128)} collective-permute-done((f32[50,128]{1,0:T(8,128)S(1)}, f32[50,128]{1,0:T(8,128)}, u32[]{:S(2)}, u32[]{:S(2)}) %collective-permute-start.27) | collective-permute-done | bytes 25632 | tf_op jit(solution)/shard_map/ppermute | solution.py:585
  1693.1 157.2 %shard_map.125 = (f32[2048,4096]{1,0:T(8,128)}, bf16[4096,4096]{1,0:T(8,128)(2,1)}) custom-call(s32[1]{0:T(128)} %bitcast.s_ref.refs_0_, bf16[4096,4096]{1,0:T(8,128)(2,1)} %bitcast.57, bf16[4096,1024]{1,0:T(8,128)(2,1)} %get-tuple-element.40.refs_2_, bf16[4096,1024]{1,0:T(8,128)(2,1)} %get-tuple-element.41.refs_3_, ...), custom_call_target="tpu_custom_call", output_to_operand_aliasing={{0}: (15, {})} | custom-call | flops 149399994368 | bytes 150000000 | tf_op jit(solution)/shard_map/pallas_call | solution.py:38
  1852.8 18.2 shard_map.131.refs_5_
  1871.1 18.3 shard_map.132.refs_5_
  (117 shorter events, 164.1 us)
Async XLA Ops:
  97.3 52.0 %collective-permute-start.1 = (bf16[2,8,512,256]{3,2,1,0:T(8,128)(2,1)}, bf16[2,8,512,256]{3,2,1,0:T(8,128)(2,1)}, u32[]{:S(2)}, u32[]{:S(2)}) collective-permute-start(bf16[2,8,512,256]{3,2,1,0:T(8,128)(2,1)} %pad_maximum_fusion.kva_ref.refs_12_), channel_id=1, source_target_pairs={{0,1},{1,0},{2,3},{3,2},{4,5},{5,4},{6,7},{7,6}} | collective-permute-start | bytes 12582920 | tf_op jit(solution)/shard_map/ppermute | solution.py:588
  205.7 71.5 %collective-permute-start.12 = (f32[512,4096]{1,0:T(8,128)}, f32[512,4096]{1,0:T(8,128)}, u32[]{:S(2)}, u32[]{:S(2)}) collective-permute-start(f32[512,4096]{1,0:T(8,128)} %fusion.22), channel_id=1, source_target_pairs={{0,1},{1,0},{2,3},{3,2},{4,5},{5,4},{6,7},{7,6}} | collective-permute-start | bytes 25165832 | tf_op jit(solution)/shard_map/ppermute | solution.py:588
  221.1 479.9 %collective-permute-start.20 = (bf16[2304,2048]{1,0:T(8,128)(2,1)}, bf16[2304,2048]{1,0:T(8,128)(2,1)}, u32[]{:S(2)}, u32[]{:S(2)}) collective-permute-start(bf16[2304,2048]{1,0:T(8,128)(2,1)} %get-tuple-element.56), channel_id=1, source_target_pairs={{0,4},{4,0},{1,5},{5,1},{2,6},{6,2},{3,7},{7,3}} | collective-permute-start | bytes 28311560 | tf_op jit(solution)/shard_map/ppermute | solution.py:582
  227.3 473.7 %collective-permute-start.4 = (bf16[2048,1024]{1,0:T(8,128)(2,1)}, bf16[2048,1024]{1,0:T(8,128)(2,1)}, u32[]{:S(2)}, u32[]{:S(2)}) collective-permute-start(bf16[2048,1024]{1,0:T(8,128)(2,1)} %constant_dynamic-slice_fusion), channel_id=1, source_target_pairs={{0,4},{4,0},{1,5},{5,1},{2,6},{6,2},{3,7},{7,3}} | collective-permute-start | bytes 12582920 | tf_op jit(solution)/shard_map/ppermute | solution.py:582
  305.7 188.6 %collective-permute-start.13 = (f32[512,4096]{1,0:T(8,128)}, f32[512,4096]{1,0:T(8,128)}, u32[]{:S(2)}, u32[]{:S(2)}) collective-permute-start(f32[512,4096]{1,0:T(8,128)} %convolution_add_fusion.refs_0_), channel_id=1, source_target_pairs={{0,2},{1,3},{2,0},{3,1},{4,6},{5,7},{6,4},{7,5}} | collective-permute-start | bytes 25165832 | tf_op jit(solution)/shard_map/ppermute | solution.py:585
  399.1 167.2 %collective-permute-start.14 = (f32[512,4096]{1,0:T(8,128)}, f32[512,4096]{1,0:T(8,128)}, u32[]{:S(2)}, u32[]{:S(2)}) collective-permute-start(f32[512,4096]{1,0:T(8,128)} %convolution_add_fusion.refs_0_), channel_id=1, source_target_pairs={{0,1},{1,0},{2,3},{3,2},{4,5},{5,4},{6,7},{7,6}} | collective-permute-start | bytes 25165832 | tf_op jit(solution)/shard_map/ppermute | solution.py:588
  494.3 72.0 %collective-permute-start.15 = (f32[512,4096]{1,0:T(8,128)}, f32[512,4096]{1,0:T(8,128)}, u32[]{:S(2)}, u32[]{:S(2)}) collective-permute-start(f32[512,4096]{1,0:T(8,128)} %collective-permute-done.13.refs_1_), channel_id=1, source_target_pairs={{0,1},{1,0},{2,3},{3,2},{4,5},{5,4},{6,7},{7,6}} | collective-permute-start | bytes 25165832 | tf_op jit(solution)/shard_map/ppermute | solution.py:588
  550.8 183.0 %collective-permute-start.8 = (f32[512,4096]{1,0:T(8,128)}, f32[512,4096]{1,0:T(8,128)}, u32[]{:S(2)}, u32[]{:S(2)}) collective-permute-start(f32[512,4096]{1,0:T(8,128)} %fusion.25), channel_id=1, source_target_pairs={{0,1},{1,0},{2,3},{3,2},{4,5},{5,4},{6,7},{7,6}} | collective-permute-start | bytes 25165832 | tf_op jit(solution)/shard_map/ppermute | solution.py:588
  623.4 105.0 %collective-permute-start.22 = (f32[2,4,512,256]{3,2,1,0:T(8,128)}, f32[2,4,512,256]{3,2,1,0:T(8,128)}, u32[]{:S(2)}, u32[]{:S(2)}) collective-permute-start(f32[2,4,512,256]{3,2,1,0:T(8,128)} %get-tuple-element.58), channel_id=1, source_target_pairs={{0,1},{1,0},{2,3},{3,2},{4,5},{5,4},{6,7},{7,6}} | collective-permute-start | bytes 12582920 | tf_op jit(solution)/shard_map/ppermute | solution.py:588
  681.2 82.6 %collective-permute-start.16 = (f32[2,4,512,256]{3,2,1,0:T(8,128)}, f32[2,4,512,256]{3,2,1,0:T(8,128)}, u32[]{:S(2)}, u32[]{:S(2)}) collective-permute-start(f32[2,4,512,256]{3,2,1,0:T(8,128)} %get-tuple-element.52), channel_id=1, source_target_pairs={{0,1},{1,0},{2,3},{3,2},{4,5},{5,4},{6,7},{7,6}} | collective-permute-start | bytes 12582920 | tf_op jit(solution)/shard_map/ppermute | solution.py:588
  701.0 244.2 %collective-permute-start.21 = (bf16[2304,2048]{1,0:T(8,128)(2,1)}, bf16[2304,2048]{1,0:T(8,128)(2,1)}, u32[]{:S(2)}, u32[]{:S(2)}) collective-permute-start(bf16[2304,2048]{1,0:T(8,128)(2,1)} %collective-permute-done.20.p0_ref.refs_10_), channel_id=1, source_target_pairs={{0,1},{1,0},{2,3},{3,2},{4,5},{5,4},{6,7},{7,6}} | collective-permute-start | bytes 28311560 | tf_op jit(solution)/shard_map/ppermute | solution.py:588
  701.0 243.7 %collective-permute-start.5 = (bf16[2048,1024]{1,0:T(8,128)(2,1)}, bf16[2048,1024]{1,0:T(8,128)(2,1)}, u32[]{:S(2)}, u32[]{:S(2)}) collective-permute-start(bf16[2048,1024]{1,0:T(8,128)(2,1)} %collective-permute-done.4.refs_7_), channel_id=1, source_target_pairs={{0,2},{1,3},{2,0},{3,1},{4,6},{5,7},{6,4},{7,5}} | collective-permute-start | bytes 12582920 | tf_op jit(solution)/shard_map/ppermute | solution.py:585
  728.4 217.3 %collective-permute-start.24 = (bf16[2048,2048]{1,0:T(8,128)(2,1)}, bf16[2048,2048]{1,0:T(8,128)(2,1)}, u32[]{:S(2)}, u32[]{:S(2)}) collective-permute-start(bf16[2048,2048]{1,0:T(8,128)(2,1)} %get-tuple-element.60), channel_id=1, source_target_pairs={{0,4},{4,0},{1,5},{5,1},{2,6},{6,2},{3,7},{7,3}} | collective-permute-start | bytes 25165832 | tf_op jit(solution)/shard_map/ppermute | solution.py:582
  733.8 130.6 %collective-permute-start.23 = (f32[4,512,256]{2,1,0:T(8,128)}, f32[4,512,256]{2,1,0:T(8,128)}, u32[]{:S(2)}, u32[]{:S(2)}) collective-permute-start(f32[4,512,256]{2,1,0:T(8,128)} %fusion.37), channel_id=1, source_target_pairs={{2,0},{3,1},{6,4},{7,5}} | collective-permute-start | bytes 6291464 | tf_op jit(solution)/shard_map/ppermute | solution.py:585
  763.8 181.4 %collective-permute-start.6 = (bf16[2048,1024]{1,0:T(8,128)(2,1)}, bf16[2048,1024]{1,0:T(8,128)(2,1)}, u32[]{:S(2)}, u32[]{:S(2)}) collective-permute-start(bf16[2048,1024]{1,0:T(8,128)(2,1)} %collective-permute-done.4.refs_7_), channel_id=1, source_target_pairs={{0,1},{1,0},{2,3},{3,2},{4,5},{5,4},{6,7},{7,6}} | collective-permute-start | bytes 12582920 | tf_op jit(solution)/shard_map/ppermute | solution.py:588
  944.7 183.6 %collective-permute-start.3 = (bf16[4096,1024]{1,0:T(8,128)(2,1)}, bf16[4096,1024]{1,0:T(8,128)(2,1)}, u32[]{:S(2)}, u32[]{:S(2)}) collective-permute-start(bf16[4096,1024]{1,0:T(8,128)(2,1)} %get-tuple-element.41.refs_3_), channel_id=1, source_target_pairs={{0,4},{4,0},{1,5},{5,1},{2,6},{6,2},{3,7},{7,3}} | collective-permute-start | bytes 25165832 | tf_op jit(solution)/shard_map/ppermute | solution.py:582
  945.2 183.2 %collective-permute-start.9 = (f32[512,4096]{1,0:T(8,128)}, f32[512,4096]{1,0:T(8,128)}, u32[]{:S(2)}, u32[]{:S(2)}) collective-permute-start(f32[512,4096]{1,0:T(8,128)} %convolution_add_fusion.1.refs_11_), channel_id=1, source_target_pairs={{0,2},{1,3},{2,0},{3,1},{4,6},{5,7},{6,4},{7,5}} | collective-permute-start | bytes 25165832 | tf_op jit(solution)/shard_map/ppermute | solution.py:585
  945.2 115.7 %collective-permute-start.36 = (f32[1024,2048]{1,0:T(8,128)}, f32[1024,2048]{1,0:T(8,128)}, u32[]{:S(2)}, u32[]{:S(2)}) collective-permute-start(f32[1024,2048]{1,0:T(8,128)} %fusion.4), channel_id=1, source_target_pairs={{0,1},{1,0},{2,3},{3,2},{4,5},{5,4},{6,7},{7,6}} | collective-permute-start | bytes 25165832 | tf_op jit(solution)/shard_map/ppermute | solution.py:588
  945.2 141.1 %collective-permute-start.32 = (f32[1024,2048]{1,0:T(8,128)}, f32[1024,2048]{1,0:T(8,128)}, u32[]{:S(2)}, u32[]{:S(2)}) collective-permute-start(f32[1024,2048]{1,0:T(8,128)} %fusion.8), channel_id=1, source_target_pairs={{0,1},{1,0},{2,3},{3,2},{4,5},{5,4},{6,7},{7,6}} | collective-permute-start | bytes 25165832 | tf_op jit(solution)/shard_map/ppermute | solution.py:588
  945.7 385.8 %collective-permute-start.18 = (bf16[2048,2048]{1,0:T(8,128)(2,1)}, bf16[2048,2048]{1,0:T(8,128)(2,1)}, u32[]{:S(2)}, u32[]{:S(2)}) collective-permute-start(bf16[2048,2048]{1,0:T(8,128)(2,1)} %get-tuple-element.54), channel_id=1, source_target_pairs={{0,4},{4,0},{1,5},{5,1},{2,6},{6,2},{3,7},{7,3}} | collective-permute-start | bytes 25165832 | tf_op jit(solution)/shard_map/ppermute | solution.py:582
  1086.3 244.2 %collective-permute-start.19 = (bf16[2048,256]{1,0:T(8,128)(2,1)S(1)}, bf16[2048,256]{1,0:T(8,128)(2,1)S(1)}, u32[]{:S(2)}, u32[]{:S(2)}) collective-permute-start(bf16[2048,256]{1,0:T(8,128)(2,1)S(1)} %copy-done.5), channel_id=1, source_target_pairs={{0,4},{4,0},{1,5},{5,1},{2,6},{6,2},{3,7},{7,3}} | collective-permute-start | bytes 3145736 | tf_op jit(solution)/shard_map/ppermute | solution.py:582
  1111.6 396.2 %collective-permute-start.2 = (bf16[4096,1024]{1,0:T(8,128)(2,1)}, bf16[4096,1024]{1,0:T(8,128)(2,1)}, u32[]{:S(2)}, u32[]{:S(2)}) collective-permute-start(bf16[4096,1024]{1,0:T(8,128)(2,1)} %get-tuple-element.40.refs_2_), channel_id=1, source_target_pairs={{0,4},{4,0},{1,5},{5,1},{2,6},{6,2},{3,7},{7,3}} | collective-permute-start | bytes 25165832 | tf_op jit(solution)/shard_map/ppermute | solution.py:582
  1128.4 403.7 %collective-permute-start.10 = (f32[512,4096]{1,0:T(8,128)}, f32[512,4096]{1,0:T(8,128)}, u32[]{:S(2)}, u32[]{:S(2)}) collective-permute-start(f32[512,4096]{1,0:T(8,128)} %convolution_add_fusion.1.refs_11_), channel_id=1, source_target_pairs={{0,1},{1,0},{2,3},{3,2},{4,5},{5,4},{6,7},{7,6}} | collective-permute-start | bytes 25165832 | tf_op jit(solution)/shard_map/ppermute | solution.py:588
  1128.4 404.1 %collective-permute-start.11 = (f32[512,4096]{1,0:T(8,128)}, f32[512,4096]{1,0:T(8,128)}, u32[]{:S(2)}, u32[]{:S(2)}) collective-permute-start(f32[512,4096]{1,0:T(8,128)} %collective-permute-done.9.refs_12_), channel_id=1, source_target_pairs={{0,1},{1,0},{2,3},{3,2},{4,5},{5,4},{6,7},{7,6}} | collective-permute-start | bytes 25165832 | tf_op jit(solution)/shard_map/ppermute | solution.py:588
  1331.5 361.0 %collective-permute-start.37 = (f32[1024,2048]{1,0:T(8,128)}, f32[1024,2048]{1,0:T(8,128)}, u32[]{:S(2)}, u32[]{:S(2)}) collective-permute-start(f32[1024,2048]{1,0:T(8,128)} %fusion.31.a_ref), channel_id=1, source_target_pairs={{0,2},{1,3},{2,0},{3,1},{4,6},{5,7},{6,4},{7,5}} | collective-permute-start | bytes 25165832 | tf_op jit(solution)/shard_map/ppermute | solution.py:585
  1331.5 361.0 %collective-permute-start.33 = (f32[1024,2048]{1,0:T(8,128)}, f32[1024,2048]{1,0:T(8,128)}, u32[]{:S(2)}, u32[]{:S(2)}) collective-permute-start(f32[1024,2048]{1,0:T(8,128)} %fusion.28.refs_1_), channel_id=1, source_target_pairs={{0,2},{1,3},{2,0},{3,1},{4,6},{5,7},{6,4},{7,5}} | collective-permute-start | bytes 25165832 | tf_op jit(solution)/shard_map/ppermute | solution.py:585
  1521.1 171.4 %collective-permute-start.27 = (f32[50,128]{1,0:T(8,128)S(1)}, f32[50,128]{1,0:T(8,128)}, u32[]{:S(2)}, u32[]{:S(2)}) collective-permute-start(f32[50,128]{1,0:T(8,128)S(1)} %bitcast_add_fusion), channel_id=1, source_target_pairs={{0,2},{1,3},{2,0},{3,1},{4,6},{5,7},{6,4},{7,5}} | collective-permute-start | bytes 76808 | tf_op jit(solution)/shard_map/ppermute | solution.py:585
  1532.1 320.3 %collective-permute-start.38 = (f32[1024,2048]{1,0:T(8,128)}, f32[1024,2048]{1,0:T(8,128)}, u32[]{:S(2)}, u32[]{:S(2)}) collective-permute-start(f32[1024,2048]{1,0:T(8,128)} %fusion.31.a_ref), channel_id=1, source_target_pairs={{0,1},{1,0},{2,3},{3,2},{4,5},{5,4},{6,7},{7,6}} | collective-permute-start | bytes 25165832 | tf_op jit(solution)/shard_map/ppermute | solution.py:588
  1532.5 338.6 %collective-permute-start.34 = (f32[1024,2048]{1,0:T(8,128)}, f32[1024,2048]{1,0:T(8,128)}, u32[]{:S(2)}, u32[]{:S(2)}) collective-permute-start(f32[1024,2048]{1,0:T(8,128)} %fusion.28.refs_1_), channel_id=1, source_target_pairs={{0,1},{1,0},{2,3},{3,2},{4,5},{5,4},{6,7},{7,6}} | collective-permute-start | bytes 25165832 | tf_op jit(solution)/shard_map/ppermute | solution.py:588
  1692.5 159.8 %collective-permute-start.29 = (f32[2048,256]{1,0:T(8,128)}, f32[2048,256]{1,0:T(8,128)}, u32[]{:S(2)}, u32[]{:S(2)}) collective-permute-start(f32[2048,256]{1,0:T(8,128)} %fusion.34.refs_1_), channel_id=1, source_target_pairs={{0,2},{1,3},{2,0},{3,1},{4,6},{5,7},{6,4},{7,5}} | collective-permute-start | bytes 6291464 | tf_op jit(solution)/shard_map/ppermute | solution.py:585
  1692.5 160.3 %collective-permute-start.39 = (f32[1024,2048]{1,0:T(8,128)}, f32[1024,2048]{1,0:T(8,128)}, u32[]{:S(2)}, u32[]{:S(2)}) collective-permute-start(f32[1024,2048]{1,0:T(8,128)} %collective-permute-done.37.b_ref), channel_id=1, source_target_pairs={{0,1},{1,0},{2,3},{3,2},{4,5},{5,4},{6,7},{7,6}} | collective-permute-start | bytes 25165832 | tf_op jit(solution)/shard_map/ppermute | solution.py:588
  1692.6 178.5 %collective-permute-start.35 = (f32[1024,2048]{1,0:T(8,128)}, f32[1024,2048]{1,0:T(8,128)}, u32[]{:S(2)}, u32[]{:S(2)}) collective-permute-start(f32[1024,2048]{1,0:T(8,128)} %collective-permute-done.33.refs_2_), channel_id=1, source_target_pairs={{0,1},{1,0},{2,3},{3,2},{4,5},{5,4},{6,7},{7,6}} | collective-permute-start | bytes 25165832 | tf_op jit(solution)/shard_map/ppermute | solution.py:588
  (16 other events, 476.5 us)

commit v3 on v2

--- a/solution.py
+++ b/solution.py
@@ -211,12 +211,15 @@
     return jnp.where((j >= start_ref[0]) & (j <= i), 0.0, NEG).astype(F32)
 
 
-def kv_slots(a_ref, b_ref):
-    return ((a_ref, 0, 0), (a_ref, 1, 2), (b_ref, 0, 1), (b_ref, 1, 3))
-
-
-def kv_spec(chunk, b0=0):
-    return pl.BlockSpec((2, 1, chunk, 2 * HEAD), lambda b, *_: (0, b + b0, 0, 0))
+FLIPS = (0, 2, 1, 3)
+
+
+def chunk_rows(s_ref, flip, chunk):
+    return pl.ds(pl.multiple_of((s_ref[0] ^ flip) * chunk, chunk), chunk)
+
+
+def of_batch(dims, b0=0):
+    return pl.BlockSpec(dims, lambda b, *_: (b + b0, 0, 0))
 
 
 def start_spec(b0=0):
@@ -228,17 +231,16 @@
     return q0, s_ref[1 + b * nq + t] // TK, (q0 + TQ - 1) // TK + 1
 
 
-def fwd_kernel(s_ref, start_ref, qt_ref, kva_ref, kvb_ref, o_ref, ct_ref, lse_ref, k_s, vt_s, t_s, acc_s, m_s, m8_s, l8_s, e_s):
+def fwd_kernel(s_ref, start_ref, qt_ref, kv0_ref, kv1_ref, kv2_ref, kv3_ref, o_ref, ct_ref, lse_ref, k_s, vt_s, t_s, acc_s, m_s, m8_s, l8_s, e_s):
     b, t, nq = pl.program_id(0), pl.program_id(1), pl.num_programs(1)
     heads = qt_ref.shape[2] // TQ
-    chunk = kva_ref.shape[2]
 
     @pl.when(t == 0)
     def _():
-        for ref, i, flip in kv_slots(kva_ref, kvb_ref):
-            rows = pl.ds(pl.multiple_of((s_ref[0] ^ flip) * chunk, chunk), chunk)
-            k_s[rows, :] = ref[i, 0, :, :HEAD]
-            vt_s[:, rows] = ref[i, 0, :, HEAD:].T
+        for ref, flip in zip((kv0_ref, kv1_ref, kv2_ref, kv3_ref), FLIPS):
+            rows = chunk_rows(s_ref, flip, ref.shape[1])
+            k_s[rows, :] = ref[0, :, :HEAD]
+            vt_s[:, rows] = ref[0, :, HEAD:].T
 
     m8_s[...] = jnp.full_like(m8_s, NEG)
     l8_s[...] = jnp.zeros_like(l8_s)
@@ -278,40 +280,40 @@
         o_ref[:, head_slice(h)] = ct.T
 
 
-def attn_fwd(table, start, qt, kva, kvb):
+def attn_fwd(table, start, qt, kvs):
     batch, _, chunk = start.shape
     nq = chunk // TQ
     n, _, cols = qt.shape
     width = cols // TQ * HEAD
     keys = 4 * chunk
-    kv, tile = kv_spec(chunk), tiles_of((1, HEAD, cols), nq)
+    kv, tile = of_batch((1, chunk, 2 * HEAD)), tiles_of((1, HEAD, cols), nq)
     return kernel_call(
         fwd_kernel, 65, (batch, nq),
-        [start_spec(), tile, kv, kv],
+        [start_spec(), tile, kv, kv, kv, kv],
         [tiles_of((TQ, width), nq), tile, tiles_of((1, 1, cols), nq)],
-        [shape((n * TQ, width), BF), shape((n, HEAD, cols), BF), shape((n, 1, cols), F32)], (table, start, qt, kva, kvb),
+        [shape((n * TQ, width), BF), shape((n, HEAD, cols), BF), shape((n, 1, cols), F32)], (table, start, qt, *kvs),
         [pltpu.VMEM((keys, HEAD), BF), pltpu.VMEM((HEAD, keys), BF), pltpu.VMEM((keys, cols), F32), pltpu.VMEM((HEAD, cols), F32),
          pltpu.VMEM((1, cols), F32), pltpu.VMEM((8, cols), F32), pltpu.VMEM((8, cols), F32), pltpu.VMEM((2 * TK, cols), BF)],
         prefetch=1)
 
 
 def bwd_kernel(b0, riding, s_ref, start_ref, qta_ref, qtb_ref, dcta_ref, dctb_ref, cta_ref, ctb_ref, la_ref, lb_ref,
-               cos_ref, sin_ref, kva_ref, kvb_ref, *refs):
+               cos_ref, sin_ref, kv0_ref, kv1_ref, kv2_ref, kv3_ref, *refs):
     nb, nq = pl.num_programs(0), pl.num_programs(1)
     if riding:
-        put_sums(pl.program_id(0) * nq + pl.program_id(1), nb * nq, refs[:riding], refs[riding + 5])
-    dq_ref, half_ref, dkv0_ref, dkv1_ref, dkvb_ref = refs[riding:riding + 5]
+        put_sums(pl.program_id(0) * nq + pl.program_id(1), nb * nq, refs[:riding], refs[riding + 6])
+    dq_ref, half_ref, *dkv_refs = refs[riding:riding + 6]
     kv_s, kt_s, dct_s, dqt_s, delta_s, ds_s, dsn_s, pn_s, dkvt_s = refs[-9:]
     b, t = pl.program_id(0) + b0, pl.program_id(1)
     heads = dq_ref.shape[1] // HEAD
-    chunk = kva_ref.shape[2]
+    chunk = kv0_ref.shape[1]
 
     @pl.when(t == 0)
     def _():
-        for ref, i, flip in kv_slots(kva_ref, kvb_ref):
-            rows = pl.ds(pl.multiple_of((s_ref[0] ^ flip) * chunk, chunk), chunk)
-            kv_s[rows, :] = ref[i, 0]
-            kt_s[:, rows] = ref[i, 0, :, :HEAD].T
+        for ref, flip in zip((kv0_ref, kv1_ref, kv2_ref, kv3_ref), FLIPS):
+            rows = chunk_rows(s_ref, flip, chunk)
+            kv_s[rows, :] = ref[0]
+            kt_s[:, rows] = ref[0, :, :HEAD].T
         dkvt_s[...] = jnp.zeros_like(dkvt_s)
 
     def of_head(h, a_ref, b_ref):
@@ -360,13 +362,13 @@
 
     @pl.when(t == nq - 1)
     def _():
-        for ref, flip in ((dkv0_ref.at[0], 0), (dkv1_ref.at[0], 2), (dkvb_ref.at[0, 0], 1), (dkvb_ref.at[1, 0], 3)):
-            rows = pl.ds(pl.multiple_of((s_ref[0] ^ flip) * chunk, chunk), chunk)
-            ref[:, :HEAD] = (dkvt_s[:HEAD, rows] * SCALE).T
-            ref[:, HEAD:] = dkvt_s[HEAD:, rows].T
-
-
-def attn_bwd(half, whole, sums, table, start, qts, dcts, cts, lses, cos_t, sin_t, kva, kvb):
+        for ref, flip in zip(dkv_refs, FLIPS):
+            rows = chunk_rows(s_ref, flip, chunk)
+            ref[0, :HEAD, :] = dkvt_s[:HEAD, rows] * SCALE
+            ref[0, HEAD:, :] = dkvt_s[HEAD:, rows]
+
+
+def attn_bwd(half, whole, sums, table, start, qts, dcts, cts, lses, cos_t, sin_t, kvs):
     batch, _, chunk = start.shape
     nq = chunk // TQ
     n, _, cols = qts[0].shape
@@ -374,14 +376,13 @@
     keys = 4 * chunk
     nb = batch // 2
     b0 = half * nb
-    kv, tile, line = kv_spec(chunk, b0), tiles_of((1, HEAD, cols), nq, b0), tiles_of((1, 1, cols), nq, b0)
+    kv, tile, line = of_batch((1, chunk, 2 * HEAD), b0), tiles_of((1, HEAD, cols), nq, b0), tiles_of((1, 1, cols), nq, b0)
     dct, tab = tile_cols(width // 2, nq, b0), tile_cols(ROT, nq, b0)
-    one = shape((nb, chunk, 2 * HEAD), F32)
-    one_spec = pl.BlockSpec((1, chunk, 2 * HEAD), lambda b, *_: (b, 0, 0))
-    in_specs = [start_spec(b0), tile, tile, dct, dct, tile, tile, line, line, tab, tab, kv, kv]
-    args = [table, start, *qts, *dcts, *cts, *lses, cos_t, sin_t, kva, kvb]
-    out_specs = [tiles_of((TQ, width), nq, b0), tiles_of((TQ, width), nq), one_spec, one_spec, kv_spec(chunk)]
-    out_shape = [shape((n * TQ, width), BF), shape((n * TQ // 2, width), BF), one, one, shape((2, nb, chunk, 2 * HEAD), F32)]
+    one, one_spec = shape((nb, 2 * HEAD, chunk), F32), of_batch((1, 2 * HEAD, chunk))
+    in_specs = [start_spec(b0), tile, tile, dct, dct, tile, tile, line, line, tab, tab] + [kv] * 4
+    args = [table, start, *qts, *dcts, *cts, *lses, cos_t, sin_t, *kvs]
+    out_specs = [tiles_of((TQ, width), nq, b0), tiles_of((TQ, width), nq)] + [one_spec] * 4
+    out_shape = [shape((n * TQ, width), BF), shape((n * TQ // 2, width), BF)] + [one] * 4
     if sums:
         specs, block, put = ride(nb * nq, lambda b, i, s: b * nq + i, lambda core: core, sums)
         in_specs += specs
@@ -474,20 +475,17 @@
 
 
 def finish_kernel(a_ref, b_ref, c_ref, cos_ref, sin_ref, o_ref):
-    dkv = a_ref[0] + b_ref[0, 0] + c_ref[0]
-    k = dkv[:, :HEAD].T
-    top = k[:ROT]
+    dkv = a_ref[0] + b_ref[0] + c_ref[0]
+    top = dkv[:ROT]
     turned = top * cos_ref[...] - swap_pairs(top) * sin_ref[...]
-    o_ref[:, :HEAD] = jnp.concatenate([turned, k[ROT:]], axis=0).T.astype(BF)
-    o_ref[:, HEAD:] = dkv[:, HEAD:].astype(BF)
+    o_ref[...] = jnp.concatenate([turned, dkv[ROT:]], axis=0).astype(BF).T
 
 
 def finish_dkv(half, own, core, away, cos_t, sin_t):
-    nb, chunk, width = own.shape
-    one = pl.BlockSpec((1, chunk, width), lambda b: (b, 0, 0))
-    tab = cols_of(ROT, chunk, half * nb)
+    nb, width, chunk = own.shape
+    one, tab = of_batch((1, width, chunk)), cols_of(ROT, chunk, half * nb)
     return kernel_call(
-        finish_kernel, 4, (nb,), [one, kv_spec(chunk), one, tab, tab], rows_of(chunk, width),
+        finish_kernel, 4, (nb,), [one, one, one, tab, tab], rows_of(chunk, width),
         shape((nb * chunk, width), BF), (own, core, away, cos_t, sin_t))
 
 
@@ -533,7 +531,7 @@
             gb8_s[:, cs] += jnp.sum(a_s[rs, cs].astype(F32).reshape(n // 8, 8, HEAD), axis=0)
         return 0
 
-    lax.fori_loop(0, tm // 128, norm, 0)
+    lax.fori_loop(0, tm // 128, norm, 0, unroll=True)
 
     @pl.when(i == pl.num_programs(0) - 1)
     def _():
@@ -565,7 +563,7 @@
 
 
 def place(table, sums, quarter, column, whole, dims):
-    steps = 8
+    steps = max(4, sums[0].shape[1] // 256)
     in_specs, block, put = ride(steps, lambda i, s: i, quarter, sums)
     args = [table, *sums]
     body, alias = with_whole(place_kernel, len(args), args, in_specs, whole)
@@ -612,8 +610,8 @@
         wo0 = send_tp(lax.dynamic_slice_in_dim(w_out, cp * (d // 4), d // 4, 1))
         h, inv_rms, kv = prep(x, gain, w_qkv, bias, cos_t, sin_t, qw)
         kv_own = kv.reshape(batch, chunk, 2 * HEAD)
-        kva = jnp.stack([kv_own, send_x(kv_own, over_x[:2])])
-        kvb = send_core(kva)
+        kv_x = send_x(kv_own, over_x[:2])
+        kvs = (kv_own, kv_x, send_core(kv_own), send_core(kv_x))
         q_args = (h, w_qkv, bias, cos_t, sin_t, qw)
         qta, wq_t, wq_half = q_project(0, 0, 1, None, *q_args, table=me)
         wq0 = send_tp(wq_half)
@@ -621,9 +619,9 @@
         wo_pieces = (wo0, wo1, send_core(wo0), send_core(wo1))
         wq_pieces = (wq0, send_core(wq0))
 
-        ctx_a, ct_a, lse_a = attn_fwd(table, start, qta, kva, kvb)
+        ctx_a, ct_a, lse_a = attn_fwd(table, start, qta, kvs)
         qtb, = q_project(1, 1, 2, q_project(1, 0, 2, None, *q_args), *q_args)
-        ctx_b, ct_b, lse_b = attn_fwd(table, start, qtb, kva, kvb)
+        ctx_b, ct_b, lse_b = attn_fwd(table, start, qtb, kvs)
         peer_ctx = (send_tp(ctx_a), send_tp(ctx_b))
 
         def part(lhs, rhs, first, k):
@@ -646,11 +644,12 @@
 
         dctx_t = (grad_ctx(w_out[:qw // 2]), grad_ctx(w_out[qw // 2:]))
 
-        attn_args = (table, start, (qta, qtb), dctx_t, (ct_a, ct_b), (lse_a, lse_b), cos_t, sin_t, kva, kvb)
-
-        def own_dkv(half, own, away, others):
-            got = send_core(others)
-            return finish_dkv(half, own, got, send_x(away + got[1], over_x[2:]), cos_t, sin_t)
+        attn_args = (table, start, (qta, qtb), dctx_t, (ct_a, ct_b), (lse_a, lse_b), cos_t, sin_t, kvs)
+
+        def own_dkv(half, own, away, core, both):
+            away = away + send_core(both)
+            core = send_core(core)
+            return finish_dkv(half, own, core, send_x(away, over_x[2:]), cos_t, sin_t)
 
         dq, dq_a, *dkv_parts, gw_out = attn_bwd(0, None, go[0], *attn_args)
         dqp_a = send_tp(dq_a)

time: 1900 us -> 2100 us (1.11)
  waiting for transfers between devices: 695 us -> 915 us
    ppermute x8, waiting for transfers between devices: 276 us -> 421 us  [send_tp(): return lax.ppermute(v, 'tp', over_tp)]
    ppermute x10, waiting for transfers between devices: 416 us -> 475 us  [send_x(): return lax.ppermute(v, 'cp', pairs)]
    ppermute x22 -> x25, starting transfers between devices: 67.9 us -> 67.5 us  [send_core(): return lax.ppermute(v, 'cp', over_core)]
  transfers between devices with their start and end apart: 40 -> 43, of which waited for: 9 -> 11; matrix products, arithmetic and copies ran while one was open for 16% -> 15% of each run, Pallas kernels for 35% -> 31%
where the time goes in v3:
time: 2100 us; the launch traced here: 2090 us
  waiting for transfers between devices  915 us (44%)
  Pallas kernels  729 us (35%)
  matrix products  312 us (15%)
  starting transfers between devices  108 us (5%)
    pallas_call x16, Pallas kernels, kernel_call(): pl.pallas_call(body, grid_spec=pltpu.PrefetchScalarGridSpec(num_scalar_pr...  729 us
    ppermute x10, waiting for transfers between devices, send_x(): return lax.ppermute(v, 'cp', pairs)  475 us
    ppermute x8, waiting for transfers between devices, send_tp(): return lax.ppermute(v, 'tp', over_tp)  421 us
    dot_general x10, matrix products, part(): lax.dot_general(cols, rhs, (((0,), (0,)), ((), ())), preferred_element_ty...  226 us
    dot_general x2, matrix products, grad_ctx(): lax.dot_general(w, g, (((1,), (1,)), ((), ())), preferred_element_type=F32)  85.9 us
    ppermute x25, starting transfers between devices, send_core(): return lax.ppermute(v, 'cp', over_core)  67.5 us
  transfers between devices with their start and end apart: 43, of which 11 were waited for; matrix products, arithmetic and copies ran while one was open for 15% of the time, Pallas kernels for 31%

profile of v3, /device:TPU:0, one launch (start us, length us, event | category | flops | bytes accessed | tf_op | source)
XLA Modules:
  0.0 2092.3 jit_solution(3000361022264437809)
XLA Ops:
  9.7 33.1 %shard_map.118 = (bf16[4096,4096]{1,0:T(8,128)(2,1)}, f32[4096,1]{1,0:T(8,128)}, bf16[4096,256]{1,0:T(8,128)(2,1)}) custom-call(bf16[4096,4096]{1,0:T(8,128)(2,1)} %bitcast.41, f32[1,4096]{1,0:T(1,128)} %bitcast.30, bf16[4096,2304]{1,0:T(8,128)(2,1)} %refs_1_.1, f32[1,2304]{1,0:T(1,128)} %reshape.74.b_ref.refs_2_, ...), custom_call_target="tpu_custom_call" | custom-call | flops 27888001024 | bytes 28000000 | tf_op jit(solution)/shard_map/pallas_call | solution.py:38
  52.3 40.9 %collective-permute-done.kv1_ref.refs_13_ = bf16[8,512,256]{2,1,0:T(8,128)(2,1)} collective-permute-done((bf16[8,512,256]{2,1,0:T(8,128)(2,1)}, bf16[8,512,256]{2,1,0:T(8,128)(2,1)}, u32[]{:S(2)}, u32[]{:S(2)}) %collective-permute-start) | collective-permute-done | bytes 2097184 | tf_op jit(solution)/shard_map/ppermute | solution.py:583
  93.2 50.6 %shard_map.119 = (bf16[16,128,2048]{2,1,0:T(8,128)(2,1)}, bf16[2304,4096]{1,0:T(8,128)(2,1)}, bf16[2304,2048]{1,0:T(8,128)(2,1)}) custom-call(s32[1]{0:T(128)} %bitcast.s_ref.refs_0_, bf16[4096,4096]{1,0:T(8,128)(2,1)} %get-tuple-element.39.h_ref.refs_0_, bf16[4096,2304]{1,0:T(8,128)(2,1)} %refs_1_.1, f32[1,2304]{1,0:T(1,128)} %reshape.74.b_ref.refs_2_, ...), custom_call_target="tpu_custom_call" | custom-call | flops 41832001536 | bytes 42000000 | tf_op jit(solution)/shard_map/pallas_call | solution.py:38
  143.8 32.2 %shard_map.120 = (bf16[4096,1024]{1,0:T(8,128)(2,1)}, bf16[16,128,2048]{2,1,0:T(8,128)(2,1)}, f32[16,1,2048]{2,1,0:T(1,128)}) custom-call(s32[17]{0:T(128)} %pad_add_fusion.s_ref.refs_0_, s32[8,1,512]{2,1,0:T(1,128)} %broadcast_in_dim.22.start_ref.refs_1_, bf16[16,128,2048]{2,1,0:T(8,128)(2,1)} %get-tuple-element.40.qt_ref.qta_ref.refs_2_, ...), custom_call_target="tpu_custom_call" | custom-call | flops 64739999744 | bytes 65000000 | tf_op jit(solution)/shard_map/pallas_call | solution.py:38
  175.9 24.1 %fusion.22 = f32[512,4096]{1,0:T(8,128)} fusion(bf16[4096,4096]{1,0:T(8,128)(2,1)} %bitcast.33, bf16[4096,1024]{1,0:T(8,128)(2,1)} %get-tuple-element.42.refs_2_, s32[]{:T(128)S(6)} %select_n.55), kind=kOutput, calls=%fused_computation.20 | convolution fusion | flops 17179869184 | bytes 46137348 | tf_op jit(solution)/shard_map/dot_general | solution.py:629
  222.1 24.8 %shard_map.121.refs_5_ = bf16[16,128,2048]{2,1,0:T(8,128)(2,1)} custom-call(bf16[4096,4096]{1,0:T(8,128)(2,1)} %get-tuple-element.39.h_ref.refs_0_, bf16[4096,2304]{1,0:T(8,128)(2,1)} %refs_1_.1, f32[1,2304]{1,0:T(1,128)} %reshape.74.b_ref.refs_2_, f32[64,4096]{1,0:T(8,128)} %get-tuple-element.73.cos_ref.refs_3_.refs_10_, ...), custom_call_target="tpu_custom_call" | custom-call | flops 20916000768 | bytes 21000000 | tf_op jit(solution)/shard_map/pallas_call | solution.py:38
  246.9 24.6 %shard_map.122.qt_ref.qtb_ref.refs_3_ = bf16[16,128,2048]{2,1,0:T(8,128)(2,1)} custom-call(bf16[4096,4096]{1,0:T(8,128)(2,1)} %get-tuple-element.39.h_ref.refs_0_, bf16[4096,2304]{1,0:T(8,128)(2,1)} %refs_1_.1, f32[1,2304]{1,0:T(1,128)} %reshape.74.b_ref.refs_2_, ...), custom_call_target="tpu_custom_call", output_to_operand_aliasing={{}: (5, {})} | custom-call | flops 20916000768 | bytes 21000000 | tf_op jit(solution)/shard_map/pallas_call | solution.py:38
  271.5 28.4 %convolution_add_fusion.refs_0_ = f32[512,4096]{1,0:T(8,128)} fusion(f32[512,4096]{1,0:T(8,128)} %collective-permute-done.13, bf16[4096,4096]{1,0:T(8,128)(2,1)} %bitcast.34, bf16[4096,1024]{1,0:T(8,128)(2,1)} %get-tuple-element.42.refs_2_, s32[]{:T(128)S(6)} %select_n.54), kind=kOutput, calls=%fused_computation.18 | convolution fusion | flops 17181966336 | bytes 54525956 | tf_op jit(solution)/shard_map/dot_general | solution.py:629
  307.6 43.2 %fusion.16.dcta_ref.refs_4_ = bf16[1024,4096]{1,0:T(8,128)(2,1)} fusion(bf16[4096,4096]{1,0:T(8,128)(2,1)} %bitcast.35, bf16[2048,4096]{1,0:T(8,128)(2,1)} %refs_6_.1), kind=kOutput, calls=%fused_computation.16 | convolution fusion | flops 34363932672 | bytes 50331648 | tf_op jit(solution)/shard_map/dot_general | solution.py:643
  350.8 42.7 %fusion.19.dctb_ref.refs_5_ = bf16[1024,4096]{1,0:T(8,128)(2,1)} fusion(bf16[4096,4096]{1,0:T(8,128)(2,1)} %bitcast.36, bf16[2048,4096]{1,0:T(8,128)(2,1)} %refs_6_.1), kind=kOutput, calls=%fused_computation.17 | convolution fusion | flops 34363932672 | bytes 50331648 | tf_op jit(solution)/shard_map/dot_general | solution.py:643
  393.5 95.2 %collective-permute-done.14.refs_1_ = f32[512,4096]{1,0:T(8,128)} collective-permute-done((f32[512,4096]{1,0:T(8,128)}, f32[512,4096]{1,0:T(8,128)}, u32[]{:S(2)}, u32[]{:S(2)}) %collective-permute-start.14) | collective-permute-done | bytes 8388640 | tf_op jit(solution)/shard_map/ppermute | solution.py:583
  488.7 32.2 %shard_map.123 = (bf16[4096,1024]{1,0:T(8,128)(2,1)}, bf16[16,128,2048]{2,1,0:T(8,128)(2,1)}, f32[16,1,2048]{2,1,0:T(1,128)}) custom-call(s32[17]{0:T(128)} %pad_add_fusion.s_ref.refs_0_, s32[8,1,512]{2,1,0:T(1,128)} %broadcast_in_dim.22.start_ref.refs_1_, bf16[16,128,2048]{2,1,0:T(8,128)(2,1)} %shard_map.122.qt_ref.qtb_ref.refs_3_, ...), custom_call_target="tpu_custom_call" | custom-call | flops 64739999744 | bytes 65000000 | tf_op jit(solution)/shard_map/pallas_call | solution.py:38
  520.8 24.4 %fusion.25 = f32[512,4096]{1,0:T(8,128)} fusion(bf16[4096,4096]{1,0:T(8,128)(2,1)} %bitcast.37, bf16[4096,1024]{1,0:T(8,128)(2,1)} %get-tuple-element.43.refs_3_, s32[]{:T(128)S(6)} %select_n.55), kind=kOutput, calls=%fused_computation.23 | convolution fusion | flops 17179869184 | bytes 46137348 | tf_op jit(solution)/shard_map/dot_general | solution.py:629
  560.6 55.2 %shard_map.124 = (bf16[4096,2048]{1,0:T(8,128)(2,1)}, bf16[2048,2048]{1,0:T(8,128)(2,1)}, f32[4,256,512]{2,1,0:T(8,128)}, f32[4,256,512]{2,1,0:T(8,128)}, f32[4,...) custom-call(s32[17]{0:T(128)} %pad_add_fusion.s_ref.refs_0_, ...), custom_call_target="tpu_custom_call" | custom-call | flops 79679995904 | bytes 80000000 | tf_op jit(solution)/shard_map/pallas_call | solution.py:38
  630.2 41.9 %shard_map.126 = (bf16[4096,2048]{1,0:T(8,128)(2,1)}, bf16[2048,2048]{1,0:T(8,128)(2,1)}, f32[4,256,512]{2,1,0:T(8,128)}, f32[4,256,512]{2,1,0:T(8,128)}, f32[4,...) custom-call(s32[17]{0:T(128)} %pad_add_fusion.s_ref.refs_0_, ...), custom_call_target="tpu_custom_call", output_to_operand_aliasing={{0}: (16, {})} | custom-call | flops 79679995904 | bytes 80000000 | tf_op jit(solution)/shard_map/pallas_call | solution.py:38
  672.1 24.4 %fusion.4 = f32[1024,2048]{1,0:T(8,128)} fusion(bf16[4096,2048]{1,0:T(8,128)(2,1)} %get-tuple-element.52.qa_ref.refs_5_, bf16[4096,4096]{1,0:T(8,128)(2,1)} %get-tuple-element.39.h_ref.refs_0_, s32[]{:T(128)S(6)} %select_n.57), kind=kOutput, calls=%fused_computation.4 | convolution fusion | flops 17179869184 | bytes 33554436 | tf_op jit(solution)/shard_map/dot_general | solution.py:629
  696.5 19.8 collective-permute-start.39
  742.6 28.3 %convolution_add_fusion.1.refs_11_ = f32[512,4096]{1,0:T(8,128)} fusion(f32[512,4096]{1,0:T(8,128)} %collective-permute-done.9, bf16[4096,4096]{1,0:T(8,128)(2,1)} %bitcast.38, bf16[4096,1024]{1,0:T(8,128)(2,1)} %get-tuple-element.43.refs_3_, s32[]{:T(128)S(6)} %select_n.54), kind=kOutput, calls=%fused_computation.19 | convolution fusion | flops 17181966336 | bytes 54525956 | tf_op jit(solution)/shard_map/dot_general | solution.py:629
  770.9 44.5 %collective-permute-done.26.c_ref = f32[4,256,512]{2,1,0:T(8,128)} collective-permute-done((f32[4,256,512]{2,1,0:T(8,128)}, f32[4,256,512]{2,1,0:T(8,128)}, u32[]{:S(2)}, u32[]{:S(2)}) %collective-permute-start.26) | collective-permute-done | bytes 2097184 | tf_op jit(solution)/shard_map/ppermute | solution.py:583
  815.5 44.9 %collective-permute-done.19.c_ref = f32[4,256,512]{2,1,0:T(8,128)} collective-permute-done((f32[4,256,512]{2,1,0:T(8,128)S(1)}, f32[4,256,512]{2,1,0:T(8,128)}, u32[]{:S(2)}, u32[]{:S(2)}) %collective-permute-start.19) | collective-permute-done | bytes 2097184 | tf_op jit(solution)/shard_map/ppermute | solution.py:583
  860.4 24.2 %fusion.8 = f32[1024,2048]{1,0:T(8,128)} fusion(bf16[4096,2048]{1,0:T(8,128)(2,1)} %get-tuple-element.52.qa_ref.refs_5_, bf16[4096,4096]{1,0:T(8,128)(2,1)} %get-tuple-element.39.h_ref.refs_0_, s32[]{:T(128)S(6)} %select_n.59), kind=kOutput, calls=%fused_computation.8 | convolution fusion | flops 17179869184 | bytes 33554436 | tf_op jit(solution)/shard_map/dot_general | solution.py:629
  894.5 25.2 %fusion.31.a_ref = f32[1024,2048]{1,0:T(8,128)} fusion(f32[1024,2048]{1,0:T(8,128)} %collective-permute-done.39, bf16[4096,2048]{1,0:T(8,128)(2,1)} %get-tuple-element.52.qa_ref.refs_5_, bf16[4096,4096]{1,0:T(8,128)(2,1)} %get-tuple-element.39.h_ref.refs_0_, s32[]{:T(128)S(6)} %select_n.56), kind=kOutput, calls=%fused_computation.27 | convolution fusion | flops 17181966336 | bytes 41943044 | tf_op jit(solution)/shard_map/dot_general | solution.py:629
  919.7 29.8 %collective-permute-done.6.refs_8_ = bf16[2048,1024]{1,0:T(8,128)(2,1)} collective-permute-done((bf16[2048,1024]{1,0:T(8,128)(2,1)}, bf16[2048,1024]{1,0:T(8,128)(2,1)}, u32[]{:S(2)}, u32[]{:S(2)}) %collective-permute-start.6) | collective-permute-done | bytes 4194336 | tf_op jit(solution)/shard_map/ppermute | solution.py:583
  952.0 113.2 %shard_map.129 = (bf16[4096,4096]{1,0:T(8,128)(2,1)}, f32[1,4096]{1,0:T(1,128)}, f32[1,2304]{1,0:T(1,128)}) custom-call(s32[1]{0:T(128)} %bitcast.s_ref.refs_0_, bf16[4096,4096]{1,0:T(8,128)(2,1)} %bitcast.42, bf16[4096,4096]{1,0:T(8,128)(2,1)} %bitcast.39, f32[4096,1]{1,0:T(8,128)} %get-tuple-element.50.r_ref.refs_3_, f32[1,4096]{1,0:T(1,128)} %bitcast.31, ...), custom_call_target="tpu_custom_call" | custom-call | flops 99599998976 | bytes 100000000 | tf_op jit(solution)/shard_map/pallas_call | solution.py:38
  1066.9 25.0 %fusion.28.refs_1_ = f32[1024,2048]{1,0:T(8,128)} fusion(f32[1024,2048]{1,0:T(8,128)} %collective-permute-done.35, bf16[4096,2048]{1,0:T(8,128)(2,1)} %get-tuple-element.52.qa_ref.refs_5_, bf16[4096,4096]{1,0:T(8,128)(2,1)} %get-tuple-element.39.h_ref.refs_0_, s32[]{:T(128)S(6)} %select_n.58), kind=kOutput, calls=%fused_computation.26 | convolution fusion | flops 17181966336 | bytes 41943044 | tf_op jit(solution)/shard_map/dot_general | solution.py:629
  1091.9 41.2 %collective-permute-done.4.refs_5_ = bf16[4096,1024]{1,0:T(8,128)(2,1)} collective-permute-done((bf16[4096,1024]{1,0:T(8,128)(2,1)}, bf16[4096,1024]{1,0:T(8,128)(2,1)}, u32[]{:S(2)}, u32[]{:S(2)}) %collective-permute-start.4) | collective-permute-done | bytes 8388640 | tf_op jit(solution)/shard_map/ppermute | solution.py:580
  1133.1 179.8 %collective-permute-done.3.refs_4_ = bf16[4096,1024]{1,0:T(8,128)(2,1)} collective-permute-done((bf16[4096,1024]{1,0:T(8,128)(2,1)}, bf16[4096,1024]{1,0:T(8,128)(2,1)}, u32[]{:S(2)}, u32[]{:S(2)}) %collective-permute-start.3) | collective-permute-done | bytes 8388640 | tf_op jit(solution)/shard_map/ppermute | solution.py:580
  1313.4 200.0 %collective-permute-done.21.refs_8_ = bf16[2048,256]{1,0:T(8,128)(2,1)} collective-permute-done((bf16[2048,256]{1,0:T(8,128)(2,1)}, bf16[2048,256]{1,0:T(8,128)(2,1)}, u32[]{:S(2)}, u32[]{:S(2)}) %collective-permute-start.21) | collective-permute-done | bytes 1048608 | tf_op jit(solution)/shard_map/ppermute | solution.py:580
  1526.8 111.9 %shard_map.130 = (bf16[4096,4096]{1,0:T(8,128)(2,1)}, f32[1,4096]{1,0:T(1,128)}, f32[1,2304]{1,0:T(1,128)}) custom-call(s32[1]{0:T(128)} %bitcast.s_ref.refs_0_, bf16[4096,4096]{1,0:T(8,128)(2,1)} %bitcast.43, bf16[4096,4096]{1,0:T(8,128)(2,1)} %bitcast.40, f32[4096,1]{1,0:T(8,128)} %get-tuple-element.50.r_ref.refs_3_, ...), custom_call_target="tpu_custom_call", output_to_operand_aliasing={{0}: (12, {})} | custom-call | flops 99599998976 | bytes 100000000 | tf_op jit(solution)/shard_map/pallas_call | solution.py:38
  1668.7 220.1 %collective-permute-done.30 = f32[50,128]{1,0:T(8,128)} collective-permute-done((f32[50,128]{1,0:T(8,128)S(1)}, f32[50,128]{1,0:T(8,128)}, u32[]{:S(2)}, u32[]{:S(2)}) %collective-permute-start.30) | collective-permute-done | bytes 25632 | tf_op jit(solution)/shard_map/ppermute | solution.py:583
  1889.3 157.2 %shard_map.125 = (f32[2048,4096]{1,0:T(8,128)}, bf16[4096,4096]{1,0:T(8,128)(2,1)}) custom-call(s32[1]{0:T(128)} %bitcast.s_ref.refs_0_, bf16[4096,4096]{1,0:T(8,128)(2,1)} %bitcast.44, bf16[4096,1024]{1,0:T(8,128)(2,1)} %get-tuple-element.42.refs_2_, bf16[4096,1024]{1,0:T(8,128)(2,1)} %get-tuple-element.43.refs_3_, ...), custom_call_target="tpu_custom_call", output_to_operand_aliasing={{0}: (15, {})} | custom-call | flops 149399994368 | bytes 150000000 | tf_op jit(solution)/shard_map/pallas_call | solution.py:38
  2049.1 18.3 shard_map.131.refs_5_
  (118 shorter events, 189.9 us)
Async XLA Ops:
  49.4 94.3 %collective-permute-start.1 = (bf16[8,512,256]{2,1,0:T(8,128)(2,1)}, bf16[8,512,256]{2,1,0:T(8,128)(2,1)}, u32[]{:S(2)}, u32[]{:S(2)}) collective-permute-start(bf16[8,512,256]{2,1,0:T(8,128)(2,1)} %bitcast.46), channel_id=1, source_target_pairs={{0,1},{1,0},{2,3},{3,2},{4,5},{5,4},{6,7},{7,6}} | collective-permute-start | bytes 6291464 | tf_op jit(solution)/shard_map/ppermute | solution.py:586
  215.4 500.9 %collective-permute-start.22 = (bf16[2304,2048]{1,0:T(8,128)(2,1)}, bf16[2304,2048]{1,0:T(8,128)(2,1)}, u32[]{:S(2)}, u32[]{:S(2)}) collective-permute-start(bf16[2304,2048]{1,0:T(8,128)(2,1)} %get-tuple-element.59), channel_id=1, source_target_pairs={{0,4},{4,0},{1,5},{5,1},{2,6},{6,2},{3,7},{7,3}} | collective-permute-start | bytes 28311560 | tf_op jit(solution)/shard_map/ppermute | solution.py:580
  221.6 494.7 %collective-permute-start.5 = (bf16[2048,1024]{1,0:T(8,128)(2,1)}, bf16[2048,1024]{1,0:T(8,128)(2,1)}, u32[]{:S(2)}, u32[]{:S(2)}) collective-permute-start(bf16[2048,1024]{1,0:T(8,128)(2,1)} %constant_dynamic-slice_fusion), channel_id=1, source_target_pairs={{0,4},{4,0},{1,5},{5,1},{2,6},{6,2},{3,7},{7,3}} | collective-permute-start | bytes 12582920 | tf_op jit(solution)/shard_map/ppermute | solution.py:580
  299.9 188.8 %collective-permute-start.14 = (f32[512,4096]{1,0:T(8,128)}, f32[512,4096]{1,0:T(8,128)}, u32[]{:S(2)}, u32[]{:S(2)}) collective-permute-start(f32[512,4096]{1,0:T(8,128)} %convolution_add_fusion.refs_0_), channel_id=1, source_target_pairs={{0,2},{1,3},{2,0},{3,1},{4,6},{5,7},{6,4},{7,5}} | collective-permute-start | bytes 25165832 | tf_op jit(solution)/shard_map/ppermute | solution.py:583
  393.5 167.1 %collective-permute-start.15 = (f32[512,4096]{1,0:T(8,128)}, f32[512,4096]{1,0:T(8,128)}, u32[]{:S(2)}, u32[]{:S(2)}) collective-permute-start(f32[512,4096]{1,0:T(8,128)} %convolution_add_fusion.refs_0_), channel_id=1, source_target_pairs={{0,1},{1,0},{2,3},{3,2},{4,5},{5,4},{6,7},{7,6}} | collective-permute-start | bytes 25165832 | tf_op jit(solution)/shard_map/ppermute | solution.py:586
  488.7 71.9 %collective-permute-start.16 = (f32[512,4096]{1,0:T(8,128)}, f32[512,4096]{1,0:T(8,128)}, u32[]{:S(2)}, u32[]{:S(2)}) collective-permute-start(f32[512,4096]{1,0:T(8,128)} %collective-permute-done.14.refs_1_), channel_id=1, source_target_pairs={{0,1},{1,0},{2,3},{3,2},{4,5},{5,4},{6,7},{7,6}} | collective-permute-start | bytes 25165832 | tf_op jit(solution)/shard_map/ppermute | solution.py:586
  545.2 171.5 %collective-permute-start.9 = (f32[512,4096]{1,0:T(8,128)}, f32[512,4096]{1,0:T(8,128)}, u32[]{:S(2)}, u32[]{:S(2)}) collective-permute-start(f32[512,4096]{1,0:T(8,128)} %fusion.25), channel_id=1, source_target_pairs={{0,1},{1,0},{2,3},{3,2},{4,5},{5,4},{6,7},{7,6}} | collective-permute-start | bytes 25165832 | tf_op jit(solution)/shard_map/ppermute | solution.py:586
  615.9 100.9 %collective-permute-start.25 = (f32[4,256,512]{2,1,0:T(8,128)}, f32[4,256,512]{2,1,0:T(8,128)}, u32[]{:S(2)}, u32[]{:S(2)}) collective-permute-start(f32[4,256,512]{2,1,0:T(8,128)} %get-tuple-element.63), channel_id=1, source_target_pairs={{0,1},{1,0},{2,3},{3,2},{4,5},{5,4},{6,7},{7,6}} | collective-permute-start | bytes 6291464 | tf_op jit(solution)/shard_map/ppermute | solution.py:586
  696.5 197.6 %collective-permute-start.39 = (f32[1024,2048]{1,0:T(8,128)}, f32[1024,2048]{1,0:T(8,128)}, u32[]{:S(2)}, u32[]{:S(2)}) collective-permute-start(f32[1024,2048]{1,0:T(8,128)} %fusion.4), channel_id=1, source_target_pairs={{0,1},{1,0},{2,3},{3,2},{4,5},{5,4},{6,7},{7,6}} | collective-permute-start | bytes 25165832 | tf_op jit(solution)/shard_map/ppermute | solution.py:586
  716.8 234.7 %collective-permute-start.23 = (bf16[2304,2048]{1,0:T(8,128)(2,1)}, bf16[2304,2048]{1,0:T(8,128)(2,1)}, u32[]{:S(2)}, u32[]{:S(2)}) collective-permute-start(bf16[2304,2048]{1,0:T(8,128)(2,1)} %collective-permute-done.22.p0_ref.refs_10_), channel_id=1, source_target_pairs={{0,1},{1,0},{2,3},{3,2},{4,5},{5,4},{6,7},{7,6}} | collective-permute-start | bytes 28311560 | tf_op jit(solution)/shard_map/ppermute | solution.py:586
  732.3 219.2 %collective-permute-start.27 = (bf16[2048,2048]{1,0:T(8,128)(2,1)}, bf16[2048,2048]{1,0:T(8,128)(2,1)}, u32[]{:S(2)}, u32[]{:S(2)}) collective-permute-start(bf16[2048,2048]{1,0:T(8,128)(2,1)} %get-tuple-element.64), channel_id=1, source_target_pairs={{0,4},{4,0},{1,5},{5,1},{2,6},{6,2},{3,7},{7,3}} | collective-permute-start | bytes 25165832 | tf_op jit(solution)/shard_map/ppermute | solution.py:580
  740.0 75.5 %collective-permute-start.26 = (f32[4,256,512]{2,1,0:T(8,128)}, f32[4,256,512]{2,1,0:T(8,128)}, u32[]{:S(2)}, u32[]{:S(2)}) collective-permute-start(f32[4,256,512]{2,1,0:T(8,128)} %add.99), channel_id=1, source_target_pairs={{2,0},{3,1},{6,4},{7,5}} | collective-permute-start | bytes 6291464 | tf_op jit(solution)/shard_map/ppermute | solution.py:583
  741.3 119.1 %collective-permute-start.19 = (f32[4,256,512]{2,1,0:T(8,128)S(1)}, f32[4,256,512]{2,1,0:T(8,128)}, u32[]{:S(2)}, u32[]{:S(2)}) collective-permute-start(f32[4,256,512]{2,1,0:T(8,128)S(1)} %add.98), channel_id=1, source_target_pairs={{2,0},{3,1},{6,4},{7,5}} | collective-permute-start | bytes 6291464 | tf_op jit(solution)/shard_map/ppermute | solution.py:583
  815.5 134.0 %collective-permute-start.6 = (bf16[2048,1024]{1,0:T(8,128)(2,1)}, bf16[2048,1024]{1,0:T(8,128)(2,1)}, u32[]{:S(2)}, u32[]{:S(2)}) collective-permute-start(bf16[2048,1024]{1,0:T(8,128)(2,1)} %collective-permute-done.5.refs_7_), channel_id=1, source_target_pairs={{0,2},{1,3},{2,0},{3,1},{4,6},{5,7},{6,4},{7,5}} | collective-permute-start | bytes 12582920 | tf_op jit(solution)/shard_map/ppermute | solution.py:583
  860.4 89.5 %collective-permute-start.7 = (bf16[2048,1024]{1,0:T(8,128)(2,1)}, bf16[2048,1024]{1,0:T(8,128)(2,1)}, u32[]{:S(2)}, u32[]{:S(2)}) collective-permute-start(bf16[2048,1024]{1,0:T(8,128)(2,1)} %collective-permute-done.5.refs_7_), channel_id=1, source_target_pairs={{0,1},{1,0},{2,3},{3,2},{4,5},{5,4},{6,7},{7,6}} | collective-permute-start | bytes 12582920 | tf_op jit(solution)/shard_map/ppermute | solution.py:586
  949.5 183.6 %collective-permute-start.4 = (bf16[4096,1024]{1,0:T(8,128)(2,1)}, bf16[4096,1024]{1,0:T(8,128)(2,1)}, u32[]{:S(2)}, u32[]{:S(2)}) collective-permute-start(bf16[4096,1024]{1,0:T(8,128)(2,1)} %get-tuple-element.43.refs_3_), channel_id=1, source_target_pairs={{0,4},{4,0},{1,5},{5,1},{2,6},{6,2},{3,7},{7,3}} | collective-permute-start | bytes 25165832 | tf_op jit(solution)/shard_map/ppermute | solution.py:580
  949.9 362.9 %collective-permute-start.3 = (bf16[4096,1024]{1,0:T(8,128)(2,1)}, bf16[4096,1024]{1,0:T(8,128)(2,1)}, u32[]{:S(2)}, u32[]{:S(2)}) collective-permute-start(bf16[4096,1024]{1,0:T(8,128)(2,1)} %get-tuple-element.42.refs_2_), channel_id=1, source_target_pairs={{0,4},{4,0},{1,5},{5,1},{2,6},{6,2},{3,7},{7,3}} | collective-permute-start | bytes 25165832 | tf_op jit(solution)/shard_map/ppermute | solution.py:580
  951.5 361.4 %collective-permute-start.10 = (f32[512,4096]{1,0:T(8,128)}, f32[512,4096]{1,0:T(8,128)}, u32[]{:S(2)}, u32[]{:S(2)}) collective-permute-start(f32[512,4096]{1,0:T(8,128)} %convolution_add_fusion.1.refs_11_), channel_id=1, source_target_pairs={{0,2},{1,3},{2,0},{3,1},{4,6},{5,7},{6,4},{7,5}} | collective-permute-start | bytes 25165832 | tf_op jit(solution)/shard_map/ppermute | solution.py:583
  951.5 113.8 %collective-permute-start.35 = (f32[1024,2048]{1,0:T(8,128)}, f32[1024,2048]{1,0:T(8,128)}, u32[]{:S(2)}, u32[]{:S(2)}) collective-permute-start(f32[1024,2048]{1,0:T(8,128)} %fusion.8), channel_id=1, source_target_pairs={{0,1},{1,0},{2,3},{3,2},{4,5},{5,4},{6,7},{7,6}} | collective-permute-start | bytes 25165832 | tf_op jit(solution)/shard_map/ppermute | solution.py:586
  951.5 575.2 %collective-permute-start.20 = (bf16[2048,2048]{1,0:T(8,128)(2,1)}, bf16[2048,2048]{1,0:T(8,128)(2,1)}, u32[]{:S(2)}, u32[]{:S(2)}) collective-permute-start(bf16[2048,2048]{1,0:T(8,128)(2,1)} %get-tuple-element.57), channel_id=1, source_target_pairs={{0,4},{4,0},{1,5},{5,1},{2,6},{6,2},{3,7},{7,3}} | collective-permute-start | bytes 25165832 | tf_op jit(solution)/shard_map/ppermute | solution.py:580
  1065.3 448.1 %collective-permute-start.21 = (bf16[2048,256]{1,0:T(8,128)(2,1)}, bf16[2048,256]{1,0:T(8,128)(2,1)}, u32[]{:S(2)}, u32[]{:S(2)}) collective-permute-start(bf16[2048,256]{1,0:T(8,128)(2,1)} %shard_map.127.refs_6_), channel_id=1, source_target_pairs={{0,4},{4,0},{1,5},{5,1},{2,6},{6,2},{3,7},{7,3}} | collective-permute-start | bytes 3145736 | tf_op jit(solution)/shard_map/ppermute | solution.py:580
  1133.1 507.2 %collective-permute-start.8 = (bf16[2048,1024]{1,0:T(8,128)(2,1)}, bf16[2048,1024]{1,0:T(8,128)(2,1)}, u32[]{:S(2)}, u32[]{:S(2)}) collective-permute-start(bf16[2048,1024]{1,0:T(8,128)(2,1)} %collective-permute-done.6.refs_8_), channel_id=1, source_target_pairs={{0,1},{1,0},{2,3},{3,2},{4,5},{5,4},{6,7},{7,6}} | collective-permute-start | bytes 12582920 | tf_op jit(solution)/shard_map/ppermute | solution.py:586
  1312.9 355.8 %collective-permute-start.11 = (f32[512,4096]{1,0:T(8,128)}, f32[512,4096]{1,0:T(8,128)}, u32[]{:S(2)}, u32[]{:S(2)}) collective-permute-start(f32[512,4096]{1,0:T(8,128)} %convolution_add_fusion.1.refs_11_), channel_id=1, source_target_pairs={{0,1},{1,0},{2,3},{3,2},{4,5},{5,4},{6,7},{7,6}} | collective-permute-start | bytes 25165832 | tf_op jit(solution)/shard_map/ppermute | solution.py:586
  1312.9 355.8 %collective-permute-start.12 = (f32[512,4096]{1,0:T(8,128)}, f32[512,4096]{1,0:T(8,128)}, u32[]{:S(2)}, u32[]{:S(2)}) collective-permute-start(f32[512,4096]{1,0:T(8,128)} %collective-permute-done.10.refs_12_), channel_id=1, source_target_pairs={{0,1},{1,0},{2,3},{3,2},{4,5},{5,4},{6,7},{7,6}} | collective-permute-start | bytes 25165832 | tf_op jit(solution)/shard_map/ppermute | solution.py:586
  1513.4 375.4 %collective-permute-start.40 = (f32[1024,2048]{1,0:T(8,128)}, f32[1024,2048]{1,0:T(8,128)}, u32[]{:S(2)}, u32[]{:S(2)}) collective-permute-start(f32[1024,2048]{1,0:T(8,128)} %fusion.31.a_ref), channel_id=1, source_target_pairs={{0,2},{1,3},{2,0},{3,1},{4,6},{5,7},{6,4},{7,5}} | collective-permute-start | bytes 25165832 | tf_op jit(solution)/shard_map/ppermute | solution.py:583
  1526.8 362.5 %collective-permute-start.36 = (f32[1024,2048]{1,0:T(8,128)}, f32[1024,2048]{1,0:T(8,128)}, u32[]{:S(2)}, u32[]{:S(2)}) collective-permute-start(f32[1024,2048]{1,0:T(8,128)} %fusion.28.refs_1_), channel_id=1, source_target_pairs={{0,2},{1,3},{2,0},{3,1},{4,6},{5,7},{6,4},{7,5}} | collective-permute-start | bytes 25165832 | tf_op jit(solution)/shard_map/ppermute | solution.py:583
  1655.7 233.1 %collective-permute-start.30 = (f32[50,128]{1,0:T(8,128)S(1)}, f32[50,128]{1,0:T(8,128)}, u32[]{:S(2)}, u32[]{:S(2)}) collective-permute-start(f32[50,128]{1,0:T(8,128)S(1)} %bitcast_add_fusion), channel_id=1, source_target_pairs={{0,2},{1,3},{2,0},{3,1},{4,6},{5,7},{6,4},{7,5}} | collective-permute-start | bytes 76808 | tf_op jit(solution)/shard_map/ppermute | solution.py:583
  1668.7 379.9 %collective-permute-start.32 = (f32[2048,256]{1,0:T(8,128)}, f32[2048,256]{1,0:T(8,128)}, u32[]{:S(2)}, u32[]{:S(2)}) collective-permute-start(f32[2048,256]{1,0:T(8,128)} %fusion.34.refs_1_), channel_id=1, source_target_pairs={{0,2},{1,3},{2,0},{3,1},{4,6},{5,7},{6,4},{7,5}} | collective-permute-start | bytes 6291464 | tf_op jit(solution)/shard_map/ppermute | solution.py:583
  1668.7 380.4 %collective-permute-start.41 = (f32[1024,2048]{1,0:T(8,128)}, f32[1024,2048]{1,0:T(8,128)}, u32[]{:S(2)}, u32[]{:S(2)}) collective-permute-start(f32[1024,2048]{1,0:T(8,128)} %fusion.31.a_ref), channel_id=1, source_target_pairs={{0,1},{1,0},{2,3},{3,2},{4,5},{5,4},{6,7},{7,6}} | collective-permute-start | bytes 25165832 | tf_op jit(solution)/shard_map/ppermute | solution.py:586
  1888.8 178.6 %collective-permute-start.37 = (f32[1024,2048]{1,0:T(8,128)}, f32[1024,2048]{1,0:T(8,128)}, u32[]{:S(2)}, u32[]{:S(2)}) collective-permute-start(f32[1024,2048]{1,0:T(8,128)} %fusion.28.refs_1_), channel_id=1, source_target_pairs={{0,1},{1,0},{2,3},{3,2},{4,5},{5,4},{6,7},{7,6}} | collective-permute-start | bytes 25165832 | tf_op jit(solution)/shard_map/ppermute | solution.py:586
  1888.8 160.3 %collective-permute-start.42 = (f32[1024,2048]{1,0:T(8,128)}, f32[1024,2048]{1,0:T(8,128)}, u32[]{:S(2)}, u32[]{:S(2)}) collective-permute-start(f32[1024,2048]{1,0:T(8,128)} %collective-permute-done.40.b_ref), channel_id=1, source_target_pairs={{0,1},{1,0},{2,3},{3,2},{4,5},{5,4},{6,7},{7,6}} | collective-permute-start | bytes 25165832 | tf_op jit(solution)/shard_map/ppermute | solution.py:586
  1889.3 178.1 %collective-permute-start.38 = (f32[1024,2048]{1,0:T(8,128)}, f32[1024,2048]{1,0:T(8,128)}, u32[]{:S(2)}, u32[]{:S(2)}) collective-permute-start(f32[1024,2048]{1,0:T(8,128)} %collective-permute-done.36.refs_2_), channel_id=1, source_target_pairs={{0,1},{1,0},{2,3},{3,2},{4,5},{5,4},{6,7},{7,6}} | collective-permute-start | bytes 25165832 | tf_op jit(solution)/shard_map/ppermute | solution.py:586
  (17 other events, 536.1 us)
